TPU v7x, 32 devices: a whole 2x2x4 slice. The times are simulated.
32 devices in a mesh: ep: 4 (over y, x), tp: 4 (over z), dp: 2 (over core).
Axes of the slice: x: 2, y: 2, z: 4, core: 2. Of those that a mesh axis runs over, the one named last changes fastest.
Arguments:
- down_weight: bfloat16 [4, 16384, 3072], P('ep', 'tp', 'dp'), may hold values from -130 to 130
- owned_span: int32 [4, 4, 2], replicated, may hold values from 0 to 31, as said below
Outputs:
- saved_spans: bfloat16 [4, 4, 768, 16384], P('ep', 'tp', 'dp')
Inputs may be any that keep to these rules, and one draw needn't show every extreme that they name: `owned_span`: block g holds rows (g % 8) * 384 onward of expert g // 8; every block is stored by exactly one device; the block at [i, j, k] has (g % 8) // 4 == k; for each k the experts of the stored blocks form a Latin square over i and j: each expert once for each i and once for each j.
All inputs are finite; a program needn't handle non-finite values.
Results may differ from a plain program's by a relative error of at most 0.001.
Values may be sent and summed in bfloat16 or wider, within the bound.
No kernel may reach another device: no remote copies, remote signals or barrier semaphores. Data moves between devices by JAX's collectives and lax.ppermute only.
A program may use at most 128 MiB of HBM per device.

v0:
```python
import jax
import jax.numpy as jnp
from jax import lax
from jax.sharding import PartitionSpec as P


def local(down_weight, owned_span):
    local_rows = down_weight[0]
    tp_count = lax.axis_size("tp")
    dp_count = lax.axis_size("dp")
    per_expert = tp_count * dp_count
    hidden_rows = local_rows.shape[0]
    block_rows = local_rows.shape[1] // tp_count
    my_expert = lax.axis_index("ep")
    my_replica = lax.axis_index("dp")
    row_table = lax.dynamic_index_in_dim(owned_span, my_replica, 2, keepdims=False)
    experts_of = row_table // per_expert
    span_of = row_table % per_expert - my_replica * tp_count
    matches = experts_of == my_expert
    wanted = jnp.sum(jnp.where(matches, span_of, 0), axis=1)
    blocks = jnp.transpose(local_rows).reshape(tp_count, block_rows, hidden_rows)
    blocks_out = jnp.take(blocks, wanted, axis=0)
    arrived = lax.all_to_all(blocks_out, "ep", split_axis=0, concat_axis=0, tiled=True)
    expert_order = lax.dynamic_index_in_dim(experts_of, my_expert, 0, keepdims=False)
    regrouped = jnp.take(arrived, expert_order, axis=0)
    columns_in = lax.all_to_all(regrouped, "tp", split_axis=0, concat_axis=0, tiled=True)
    saved_block = jnp.transpose(columns_in, (1, 0, 2)).reshape(block_rows, tp_count * hidden_rows)
    return saved_block[None, None]


def solution(mesh):
    return jax.shard_map(
        local,
        mesh=mesh,
        in_specs=(P("ep", "tp", "dp"), P()),
        out_specs=P("ep", "tp", "dp", None),
        check_vma=False,
    )
```

profile of v0, /device:TPU:0, one launch (start us, length us, event | category | flops | bytes accessed | tf_op | source)
XLA Modules:
  0.0 538.8 jit_solution(8205511093044458266)
XLA Ops:
  0.0 0.0 copy-start
  0.0 0.7 copy-done
  0.7 0.1 fusion.2
  0.9 16.6 %copy.4 = bf16[1536,4096]{1,0:T(8,128)(2,1)} copy(bf16[1536,4096]{0,1:T(8,128)(2,1)} %bitcast.13) | data formatting | bytes 25165824 | tf_op jit(solution)/shard_map/transpose | solution.py:21
  17.5 10.7 %fusion.5 = (bf16[4,384,2048]{2,1,0:T(8,128)(2,1)}, bf16[4,384,2048]{2,1,0:T(8,128)(2,1)}) fusion(bf16[4,384,4096]{2,1,0:T(8,128)(2,1)} %bitcast.10), kind=kLoop, calls=%fused_computation.25 | loop fusion | bytes 25165824 | tf_op jit(solution)/shard_map/jit(_take)/gather | solution.py:22
  28.1 6.4 %gather_fusion = bf16[4,384,2048]{2,1,0:T(8,128)(2,1)} fusion(bf16[4,384,2048]{2,1,0:T(8,128)(2,1)} %get-tuple-element.12, s32[1024]{0:T(1024)S(1)} %pad_clamp_fusion.1), kind=kCustom, calls=%fused_computation.clone | custom fusion | bytes 12582928 | tf_op jit(solution)/shard_map/jit(_take)/gather | solution.py:22
  34.5 6.3 %gather_fusion.1 = bf16[4,384,2048]{2,1,0:T(8,128)(2,1)} fusion(bf16[4,384,2048]{2,1,0:T(8,128)(2,1)} %get-tuple-element.13, s32[1024]{0:T(1024)S(1)} %pad_clamp_fusion.1), kind=kCustom, calls=%fused_computation.1.clone | custom fusion | bytes 12582928 | tf_op jit(solution)/shard_map/jit(_take)/gather | solution.py:22
  40.8 11.2 %maximum_select_fusion = bf16[4,384,4096]{2,1,0:T(8,128)(2,1)} fusion(bf16[4,384,2048]{2,1,0:T(8,128)(2,1)} %gather_fusion.1, bf16[4,384,2048]{2,1,0:T(8,128)(2,1)} %gather_fusion, pred[4]{0:T(512)(128)(4,1)S(1)} %compare_and_fusion.1), kind=kLoop, calls=%fused_computation.4 | loop fusion | flops 31457280 | bytes 25165828 | tf_op jit(solution)/shard_map/jit(_take)/select_n | solution.py:22
  52.1 6.3 %all-to-all-start = ((bf16[4,384,4096]{2,1,0:T(8,128)(2,1)}), bf16[4,384,4096]{2,1,0:T(8,128)(2,1)}, u32[]{:S(2)}, u32[]{:S(2)}) async-start(bf16[4,384,4096]{2,1,0:T(8,128)(2,1)} %maximum_select_fusion), calls=%async_computation | async-start | bytes 25165824 | tf_op jit(solution)/shard_map/all_to_all | solution.py:23
  58.4 138.8 %all-to-all-done = bf16[4,384,4096]{2,1,0:T(8,128)(2,1)} async-done(((bf16[4,384,4096]{2,1,0:T(8,128)(2,1)}), bf16[4,384,4096]{2,1,0:T(8,128)(2,1)}, u32[]{:S(2)}, u32[]{:S(2)}) %all-to-all-start) | async-done | bytes 12582944 | tf_op jit(solution)/shard_map/all_to_all | solution.py:23
  197.2 10.7 %fusion.4 = (bf16[4,384,2048]{2,1,0:T(8,128)(2,1)}, bf16[4,384,2048]{2,1,0:T(8,128)(2,1)}) fusion(bf16[4,384,4096]{2,1,0:T(8,128)(2,1)} %all-to-all-done), kind=kLoop, calls=%fused_computation.24 | loop fusion | bytes 25165824 | tf_op jit(solution)/shard_map/jit(_take)/gather | solution.py:25
  207.9 6.4 %gather_fusion.2 = bf16[4,384,2048]{2,1,0:T(8,128)(2,1)} fusion(bf16[4,384,2048]{2,1,0:T(8,128)(2,1)} %get-tuple-element.10, s32[1024]{0:T(1024)S(1)} %pad_clamp_fusion), kind=kCustom, calls=%fused_computation.2.clone | custom fusion | bytes 12582928 | tf_op jit(solution)/shard_map/jit(_take)/gather | solution.py:25
  214.3 6.4 %gather_fusion.3 = bf16[4,384,2048]{2,1,0:T(8,128)(2,1)} fusion(bf16[4,384,2048]{2,1,0:T(8,128)(2,1)} %get-tuple-element.11, s32[1024]{0:T(1024)S(1)} %pad_clamp_fusion), kind=kCustom, calls=%fused_computation.3.clone | custom fusion | bytes 12582928 | tf_op jit(solution)/shard_map/jit(_take)/gather | solution.py:25
  220.7 7.3 %maximum_select_fusion.1 = bf16[4,384,4096]{2,1,0:T(8,128)(2,1)S(1)} fusion(bf16[4,384,2048]{2,1,0:T(8,128)(2,1)} %gather_fusion.3, bf16[4,384,2048]{2,1,0:T(8,128)(2,1)} %gather_fusion.2, pred[4]{0:T(512)(128)(4,1)S(1)} %get-tuple-element.6), kind=kLoop, calls=%fused_computation.5 | loop fusion | flops 31457280 | bytes 25165828 | tf_op jit(solution)/shard_map/jit(_take)/select_n | solution.py:25
  228.1 277.4 %all_to_all.10 = bf16[4,384,4096]{2,1,0:T(8,128)(2,1)} all-to-all(bf16[4,384,4096]{2,1,0:T(8,128)(2,1)S(1)} %maximum_select_fusion.1), channel_id=1, replica_groups=mesh['ep'=4,'tp'=4,'dp'=2] {'tp'}, dimensions={0} | all-to-all | bytes 25165824 | tf_op jit(solution)/shard_map/all_to_all | solution.py:26
  505.5 16.7 %copy.5 = bf16[384,4,4096]{0,2,1:T(8,128)(2,1)} copy(bf16[384,4,4096]{2,0,1:T(8,128)(2,1)} %bitcast.11) | data formatting | bytes 25165824 | tf_op jit(solution)/shard_map/transpose | solution.py:27
  522.2 0.0 copy-start.1
  522.2 16.6 %copy.6 = bf16[1,1,384,16384]{3,2,1,0:T(8,128)(2,1)} copy(bf16[1,1,384,16384]{2,3,1,0:T(8,128)(2,1)} %bitcast.12) | data formatting | bytes 25165824 | tf_op jit(solution)/shard_map/broadcast_in_dim;reshape | solution.py:28
  538.8 0.0 copy-done.1
  (6 shorter events, 0.0 us)
Async XLA Ops:
  0.0 0.7 copy-start
  52.1 145.2 %all-to-all-start = ((bf16[4,384,4096]{2,1,0:T(8,128)(2,1)}), bf16[4,384,4096]{2,1,0:T(8,128)(2,1)}, u32[]{:S(2)}, u32[]{:S(2)}) async-start(bf16[4,384,4096]{2,1,0:T(8,128)(2,1)} %maximum_select_fusion), calls=%async_computation | async-start | bytes 25165824 | tf_op jit(solution)/shard_map/all_to_all | solution.py:23
  522.2 16.6 %copy-start.1 = (s32[4,4,2]{1,2,0:T(2,128)S(1)}, s32[4,4,2]{1,2,0:T(2,128)}, u32[]{:S(2)}) copy-start(s32[4,4,2]{1,2,0:T(2,128)} %param.5) | copy-start | bytes 388
where the time goes:
time: 540 us; the launch traced here: 539 us
  blocking collectives  277 us (51%)
  waiting for transfers between devices  139 us (26%)
  local copies, waits for them, and re-layouts  97.4 us (18%)
  other arithmetic  18.7 us (3%)
  starting transfers between devices  6.32 us (1%)
    all_to_all x1, blocking collectives, local(): lax.all_to_all(regrouped, 'tp', split_axis=0, concat_axis=0, tiled=True)  277 us
    all_to_all x1, waiting for transfers between devices, local(): lax.all_to_all(blocks_out, 'ep', split_axis=0, concat_axis=0, tiled=True)  139 us
    gather x3, local copies, waits for them, and re-layouts, local(): regrouped = jnp.take(arrived, expert_order, axis=0)  23.5 us
    gather x3, local copies, waits for them, and re-layouts, local(): blocks_out = jnp.take(blocks, wanted, axis=0)  23.4 us
    transpose x1, local copies, waits for them, and re-layouts, local(): jnp.transpose(columns_in, (1, 0, 2))  16.7 us
    transpose x1, local copies, waits for them, and re-layouts, local(): jnp.transpose(local_rows).reshape(tp_count, block_rows, hidden_rows)  16.6 us
    another operation x1, local copies, waits for them, and re-layouts, local(): return saved_block[None, None]  16.6 us
    select_n x2, other arithmetic, local(): blocks_out = jnp.take(blocks, wanted, axis=0)  11.3 us
  transfers between devices with their start and end apart: 1, of which 1 were waited for; matrix products, arithmetic and copies ran while one was open for 0% of the time, Pallas kernels for 0%

commit v1 on v0

v1 whole, which is shorter than its diff:
```python
import jax
import jax.numpy as jnp
from jax import lax
from jax.experimental import pallas as pl
from jax.experimental.pallas import tpu as pltpu
from jax.sharding import PartitionSpec as P


TP_FIRST = 1
EP_FIRST = (1, 2, 4, 4, 3, 1)
ORDER = (
    "AX", "A0", "A1", "B0", "A2", "B1", "HX", "A3", "C0", "B2", "A4",
    "C1", "B3", "A5", "BX", "B4", "B5", "C2", "C3", "CX", "C4", "C5",
)
ANY = pl.BlockSpec(memory_space=pl.ANY)
SCALARS = pl.BlockSpec(memory_space=pltpu.SMEM)
PARAMS = pltpu.CompilerParams(vmem_limit_bytes=66_000_000)


def tile_of(width):
    return 256 if width % 256 == 0 else 128


def pick_rows(weight, spans, offset, width, block_rows):
    count = spans.shape[0]
    tile = tile_of(width)
    rows = weight.shape[1]

    def kernel(spans_ref, weight_ref, *refs):
        outs, turned = refs[-1 - count:-1], refs[-1]
        turned[...] = weight_ref[...].T
        for partner, out in enumerate(outs):
            start = pl.multiple_of(spans_ref[partner] * block_rows, 16)
            out[...] = turned[pl.ds(start, block_rows), :]

    return pl.pallas_call(
        kernel,
        grid_spec=pltpu.PrefetchScalarGridSpec(
            num_scalar_prefetch=1,
            grid=(width // tile,),
            in_specs=[pl.BlockSpec((tile, rows), lambda step, spans: (offset // tile + step, 0))],
            out_specs=[pl.BlockSpec((block_rows, tile), lambda step, spans: (0, step))] * count,
            scratch_shapes=[pltpu.VMEM((rows, tile), weight.dtype)],
        ),
        out_shape=[jax.ShapeDtypeStruct((block_rows, width), weight.dtype)] * count,
        compiler_params=PARAMS,
        name="pick_rows",
    )(spans, weight)


def choose(pieces, picks):
    count = len(pieces)

    def kernel(picks_ref, *refs):
        ins, outs, (held, arrive, leave) = refs[:count], refs[count:-3], refs[-3:]
        for slot in range(count):
            for source in range(count):
                @pl.when(picks_ref[slot] == source)
                def _():
                    pltpu.make_async_copy(ins[source], held.at[slot], arrive.at[slot]).start()
        for slot in range(count):
            pltpu.make_async_copy(ins[slot], held.at[slot], arrive.at[slot]).wait()
            pltpu.make_async_copy(held.at[slot], outs[slot], leave.at[slot]).start()
        for slot in range(count):
            pltpu.make_async_copy(held.at[slot], outs[slot], leave.at[slot]).wait()

    return pl.pallas_call(
        kernel,
        in_specs=[SCALARS] + [ANY] * count,
        out_specs=[ANY] * count,
        out_shape=[jax.ShapeDtypeStruct(piece.shape, piece.dtype) for piece in pieces],
        scratch_shapes=[
            pltpu.VMEM((count, *pieces[0].shape), pieces[0].dtype),
            pltpu.SemaphoreType.DMA((count,)),
            pltpu.SemaphoreType.DMA((count,)),
        ],
        compiler_params=PARAMS,
        name="choose",
    )(picks, *pieces)


def place(saved, pieces, starts, shape):
    count = len(pieces)
    width = pieces[0].shape[1]

    def kernel(starts_ref, *refs):
        ins, out, held, arrive, leave = refs[:count], *refs[-4:]
        reads, writes = [], []
        for slot in range(count):
            start = pl.multiple_of(starts_ref[slot], 128)
            reads.append(pltpu.make_async_copy(ins[slot], held.at[slot], arrive.at[slot]))
            writes.append(pltpu.make_async_copy(held.at[slot], out.at[:, pl.ds(start, width)], leave.at[slot]))
        for read in reads:
            read.start()
        for read, write in zip(reads, writes):
            read.wait()
            write.start()
        for write in writes:
            write.wait()

    return pl.pallas_call(
        kernel,
        in_specs=[SCALARS] + [ANY] * (count + len(saved)),
        out_specs=ANY,
        out_shape=jax.ShapeDtypeStruct(shape, pieces[0].dtype),
        scratch_shapes=[
            pltpu.VMEM((count, *pieces[0].shape), pieces[0].dtype),
            pltpu.SemaphoreType.DMA((count,)),
            pltpu.SemaphoreType.DMA((count,)),
        ],
        input_output_aliases={count + 1: 0} if saved else {},
        compiler_params=PARAMS,
        name="place",
    )(starts, *pieces, *saved)


def exchange(pieces, axis):
    count = len(pieces)
    return [pieces[0]] + [
        lax.ppermute(pieces[step], axis, [(index, index ^ step) for index in range(count)])
        for step in range(1, count)
    ]


def local(down_weight, owned_span):
    weight = down_weight[0]
    hidden, rows = weight.shape
    ep_count, tp_count, dp_count = (lax.axis_size(name) for name in ("ep", "tp", "dp"))
    per_expert = tp_count * dp_count
    block_rows = rows // tp_count
    me, mine, replica = (lax.axis_index(name) for name in ("ep", "tp", "dp"))
    table = lax.dynamic_index_in_dim(owned_span, replica, 2, keepdims=False)
    experts = table // per_expert
    spans = jnp.where(experts == me, table % per_expert - replica * tp_count, 0)
    steps = jnp.arange(ep_count, dtype=jnp.int32)
    spans_ep = jnp.take(jnp.sum(spans, axis=1), steps ^ me)
    spans_tp = jnp.take(jnp.sum(spans, axis=0), steps ^ mine)
    row_experts = lax.dynamic_index_in_dim(experts, me, 0, keepdims=False)
    column_experts = lax.dynamic_index_in_dim(experts, mine, 1, keepdims=False)
    picks = jnp.take(row_experts, steps ^ mine) ^ me
    picks_x = jnp.take(column_experts, steps ^ me) ^ me
    columns = (steps ^ mine) * hidden
    columns_x = (steps ^ mine ^ me ^ jnp.take(column_experts, me)) * hidden
    unit = hidden // (TP_FIRST + sum(EP_FIRST))
    shape = (block_rows, tp_count * hidden)

    offsets = {"X": 0}
    start = TP_FIRST * unit
    for chunk, share in enumerate(EP_FIRST):
        offsets[str(chunk)] = start
        start += share * unit
    moved = {}
    saved = []
    for event in ORDER:
        stage, chunk = event
        first = chunk == "X"
        if stage == "A":
            width = (TP_FIRST if first else EP_FIRST[int(chunk)]) * unit
            sent = pick_rows(weight, spans_tp if first else spans_ep, offsets[chunk], width, block_rows)
            moved[chunk] = exchange(sent, "tp" if first else "ep")
        elif stage == "H":
            moved[chunk] = exchange(moved[chunk], "ep")
        elif stage == "B":
            sent = choose(moved[chunk], picks_x if first else picks)
            moved[chunk] = exchange(sent, "ep" if first else "tp")
        else:
            places = (columns_x if first else columns) + offsets[chunk]
            saved = [place(saved, moved[chunk], places, shape)]
    return saved[0][None, None]


def solution(mesh):
    return jax.shard_map(
        local,
        mesh=mesh,
        in_specs=(P("ep", "tp", "dp"), P()),
        out_specs=P("ep", "tp", "dp", None),
        check_vma=False,
    )
```

time: 540 us -> 399 us (0.74)
  blocking collectives: 277 us -> 0 us
  starting transfers between devices: 6.32 us -> 100 us
  local copies, waits for them, and re-layouts: 97.4 us -> 6.18 us
  waiting for transfers between devices: 139 us -> 210 us
  Pallas kernels: 0 us -> 70.3 us
  other arithmetic: 18.7 us -> 6.28 us
    all_to_all x1 -> x0, blocking collectives: 277 us -> none  [local(): lax.all_to_all(regrouped, 'tp', split_axis=0, concat_axis=0, tiled=True)]
    ppermute x0 -> x45, waiting for transfers between devices: none -> 210 us  [exchange(): lax.ppermute(pieces[step], axis, [(index, index ^ step) for index in rang...]
    all_to_all x1 -> x0, waiting for transfers between devices: 139 us -> none  [local(): lax.all_to_all(blocks_out, 'ep', split_axis=0, concat_axis=0, tiled=True)]
    ppermute x0 -> x45, starting transfers between devices: none -> 100 us  [exchange(): lax.ppermute(pieces[step], axis, [(index, index ^ step) for index in rang...]
    pallas_call x0 -> x21, Pallas kernels: none -> 70.3 us  [the longest x7 28 us: pick_rows(): pl.pallas_call(kernel, grid_spec=pltpu.PrefetchScalarGridSpec(num_scalar_...]
    gather x6 -> x4, local copies, waits for them, and re-layouts: 46.9 us -> 2.56 us  [the longest x1 0.64 us: local(): picks_x = jnp.take(column_experts, steps ^ me) ^ me]
    transpose x2 -> x0, local copies, waits for them, and re-layouts: 33.3 us -> none  [the longest x1 16.7 us: local(): jnp.transpose(columns_in, (1, 0, 2))]
    select_n x3 -> x4, other arithmetic: 18.6 us -> 1.13 us  [the longest x2 0.59 us: local(): spans_ep = jnp.take(jnp.sum(spans, axis=1), steps ^ me)]
  transfers between devices with their start and end apart: 1 -> 45, of which waited for: 1 -> 11; matrix products, arithmetic and copies ran while one was open for 0% -> 2% of each run, Pallas kernels for 0% -> 16%
where the time goes in v1:
time: 399 us; the launch traced here: 394 us
  waiting for transfers between devices  210 us (53%)
  starting transfers between devices  100 us (25%)
  Pallas kernels  70.3 us (18%)
  other arithmetic  6.28 us (2%)
  local copies, waits for them, and re-layouts  6.18 us (2%)
    ppermute x45, waiting for transfers between devices, exchange(): lax.ppermute(pieces[step], axis, [(index, index ^ step) for index in rang...  210 us
    ppermute x45, starting transfers between devices, exchange(): lax.ppermute(pieces[step], axis, [(index, index ^ step) for index in rang...  100 us
    pallas_call x7, Pallas kernels, pick_rows(): pl.pallas_call(kernel, grid_spec=pltpu.PrefetchScalarGridSpec(num_scalar_...  28 us
    pallas_call x7, Pallas kernels, choose(): pl.pallas_call(kernel, in_specs=[SCALARS] + [ANY] * count, out_specs=[ANY...  21.2 us
    pallas_call x7, Pallas kernels, place(): pl.pallas_call(kernel, in_specs=[SCALARS] + [ANY] * (count + len(saved)),...  21.1 us
  transfers between devices with their start and end apart: 45, of which 11 were waited for; matrix products, arithmetic and copies ran while one was open for 2% of the time, Pallas kernels for 16%

profile of v1, /device:TPU:0, one launch (start us, length us, event | category | flops | bytes accessed | tf_op | source)
XLA Modules:
  0.0 394.4 jit_solution(5461920534351478051)
XLA Ops:
  5.0 3.0 collective-permute-start.39
  32.1 4.5 %collective-permute-start.43 = (bf16[384,256]{1,0:T(8,128)(2,1)}, bf16[384,256]{1,0:T(8,128)(2,1)}, u32[]{:S(2)}, u32[]{:S(2)}) collective-permute-start(bf16[384,256]{1,0:T(8,128)(2,1)} %get-tuple-element.116), channel_id=1, source_target_pairs={{0,4},{2,6},{4,0},{6,2},{1,5},{3,7},{5,1},{7,3},{8,12},{10,14},{12... | collective-permute-start | bytes 589832 | tf_op jit(solution)/shard_map/ppermute | solution.py:120
  40.2 3.3 pick_rows.12
  47.2 4.9 %pick_rows.8 = (bf16[384,768]{1,0:T(8,128)(2,1)}, bf16[384,768]{1,0:T(8,128)(2,1)}, bf16[384,768]{1,0:T(8,128)(2,1)}, bf16[384,768]{1,0:T(8,128)(2,1)}) custom-call(s32[4]{0:T(128)} %broadcast_select_fusion.1.spans_ref, bf16[4096,1536]{1,0:T(8,128)(2,1)} %bitcast.12), custom_call_target="tpu_custom_call" | custom-call | tf_op jit(solution)/shard_map/pick_rows/pallas_call | solution.py:36
  59.6 3.2 collective-permute-done.44.refs_3_
  66.3 5.5 %pick_rows.11 = (bf16[384,1024]{1,0:T(8,128)(2,1)}, bf16[384,1024]{1,0:T(8,128)(2,1)}, bf16[384,1024]{1,0:T(8,128)(2,1)}, bf16[384,1024]{1,0:T(8,128)(2,1)}) custom-call(s32[4]{0:T(128)} %broadcast_select_fusion.1.spans_ref, bf16[4096,1536]{1,0:T(8,128)(2,1)} %bitcast.13), custom_call_target="tpu_custom_call" | custom-call | tf_op jit(solution)/shard_map/pick_rows/pallas_call | solution.py:36
  73.4 9.0 %collective-permute-done.18.refs_1_ = bf16[384,256]{1,0:T(8,128)(2,1)} collective-permute-done((bf16[384,256]{1,0:T(8,128)(2,1)}, bf16[384,256]{1,0:T(8,128)(2,1)}, u32[]{:S(2)}, u32[]{:S(2)}) %collective-permute-start.18) | collective-permute-done | bytes 196640 | tf_op jit(solution)/shard_map/ppermute | solution.py:120
  84.4 3.1 collective-permute-done.20.refs_3_
  90.4 5.4 %pick_rows.10 = (bf16[384,1024]{1,0:T(8,128)(2,1)}, bf16[384,1024]{1,0:T(8,128)(2,1)}, bf16[384,1024]{1,0:T(8,128)(2,1)}, bf16[384,1024]{1,0:T(8,128)(2,1)}) custom-call(s32[4]{0:T(128)} %broadcast_select_fusion.1.spans_ref, bf16[4096,1536]{1,0:T(8,128)(2,1)} %bitcast.14), custom_call_target="tpu_custom_call" | custom-call | tf_op jit(solution)/shard_map/pick_rows/pallas_call | solution.py:36
  95.8 47.6 %collective-permute-done.7.refs_2_ = bf16[384,768]{1,0:T(8,128)(2,1)} collective-permute-done((bf16[384,768]{1,0:T(8,128)(2,1)}, bf16[384,768]{1,0:T(8,128)(2,1)}, u32[]{:S(2)}, u32[]{:S(2)}) %collective-permute-start.7) | collective-permute-done | bytes 589856 | tf_op jit(solution)/shard_map/ppermute | solution.py:120
  153.1 3.5 choose.11
  156.6 9.9 %collective-permute-done.36.refs_1_ = bf16[384,512]{1,0:T(8,128)(2,1)} collective-permute-done((bf16[384,512]{1,0:T(8,128)(2,1)}, bf16[384,512]{1,0:T(8,128)(2,1)}, u32[]{:S(2)}, u32[]{:S(2)}) %collective-permute-start.36) | collective-permute-done | bytes 393248 | tf_op jit(solution)/shard_map/ppermute | solution.py:120
  166.5 3.2 choose.8
  172.8 6.6 %collective-permute-done.22.refs_2_ = bf16[384,1024]{1,0:T(8,128)(2,1)} collective-permute-done((bf16[384,1024]{1,0:T(8,128)(2,1)}, bf16[384,1024]{1,0:T(8,128)(2,1)}, u32[]{:S(2)}, u32[]{:S(2)}) %collective-permute-start.22) | collective-permute-done | bytes 786464 | tf_op jit(solution)/shard_map/ppermute | solution.py:120
  179.3 3.8 collective-permute-start.32
  183.2 3.6 choose.10
  186.8 53.8 %collective-permute-done.38.refs_3_ = bf16[384,512]{1,0:T(8,128)(2,1)} collective-permute-done((bf16[384,512]{1,0:T(8,128)(2,1)}, bf16[384,512]{1,0:T(8,128)(2,1)}, u32[]{:S(2)}, u32[]{:S(2)}) %collective-permute-start.38) | collective-permute-done | bytes 393248 | tf_op jit(solution)/shard_map/ppermute | solution.py:120
  240.6 42.0 %collective-permute-start.24 = (bf16[384,1024]{1,0:T(8,128)(2,1)}, bf16[384,1024]{1,0:T(8,128)(2,1)S(1)}, u32[]{:S(2)}, u32[]{:S(2)}) collective-permute-start(bf16[384,1024]{1,0:T(8,128)(2,1)} %get-tuple-element.91), channel_id=1, source_target_pairs={{0,2},{2,0},{4,6},{6,4},{1,3},{3,1},{5,7},{7,5},{8,10},{10,8},{12,... | collective-permute-start | bytes 2359304 | tf_op jit(solution)/shard_map/ppermute | solution.py:120
  294.3 23.0 %collective-permute-done.24.refs_1_ = bf16[384,1024]{1,0:T(8,128)(2,1)S(1)} collective-permute-done((bf16[384,1024]{1,0:T(8,128)(2,1)}, bf16[384,1024]{1,0:T(8,128)(2,1)S(1)}, u32[]{:S(2)}, u32[]{:S(2)}) %collective-permute-start.24) | collective-permute-done | bytes 786464 | tf_op jit(solution)/shard_map/ppermute | solution.py:120
  317.3 33.3 %collective-permute-done.25.refs_2_ = bf16[384,1024]{1,0:T(8,128)(2,1)} collective-permute-done((bf16[384,1024]{1,0:T(8,128)(2,1)}, bf16[384,1024]{1,0:T(8,128)(2,1)}, u32[]{:S(2)}, u32[]{:S(2)}) %collective-permute-start.25) | collective-permute-done | bytes 786464 | tf_op jit(solution)/shard_map/ppermute | solution.py:120
  359.6 3.5 place.9.refs_4_
  363.1 3.5 place.10.refs_4_
  369.3 3.2 place.12.refs_4_
  372.6 19.0 %collective-permute-done.4.refs_2_ = bf16[384,256]{1,0:T(8,128)(2,1)} collective-permute-done((bf16[384,256]{1,0:T(8,128)(2,1)}, bf16[384,256]{1,0:T(8,128)(2,1)}, u32[]{:S(2)}, u32[]{:S(2)}) %collective-permute-start.4) | collective-permute-done | bytes 196640 | tf_op jit(solution)/shard_map/ppermute | solution.py:120
  (141 shorter events, 91.7 us)
Async XLA Ops:
  53.6 34.8 %collective-permute-start.6 = (bf16[384,768]{1,0:T(8,128)(2,1)}, bf16[384,768]{1,0:T(8,128)(2,1)S(1)}, u32[]{:S(2)}, u32[]{:S(2)}) collective-permute-start(bf16[384,768]{1,0:T(8,128)(2,1)} %get-tuple-element.71), channel_id=1, source_target_pairs={{0,8},{8,0},{16,24},{24,16},{1,9},{9,1},{17,25},{25,17},{2,10},{10... | collective-permute-start | bytes 1769480 | tf_op jit(solution)/shard_map/ppermute | solution.py:120
  63.5 20.3 %collective-permute-start.19 = (bf16[384,256]{1,0:T(8,128)(2,1)}, bf16[384,256]{1,0:T(8,128)(2,1)}, u32[]{:S(2)}, u32[]{:S(2)}) collective-permute-start(bf16[384,256]{1,0:T(8,128)(2,1)} %get-tuple-element.84), channel_id=1, source_target_pairs={{0,16},{8,24},{16,0},{24,8},{1,17},{9,25},{17,1},{25,9},{2,18},{10... | collective-permute-start | bytes 589832 | tf_op jit(solution)/shard_map/ppermute | solution.py:120
  65.1 22.4 %collective-permute-start.20 = (bf16[384,256]{1,0:T(8,128)(2,1)}, bf16[384,256]{1,0:T(8,128)(2,1)}, u32[]{:S(2)}, u32[]{:S(2)}) collective-permute-start(bf16[384,256]{1,0:T(8,128)(2,1)} %get-tuple-element.85), channel_id=1, source_target_pairs={{0,24},{8,16},{16,8},{24,0},{1,25},{9,17},{17,9},{25,1},{2,26},{10... | collective-permute-start | bytes 589832 | tf_op jit(solution)/shard_map/ppermute | solution.py:120
  71.9 74.0 %collective-permute-start.27 = (bf16[384,1024]{1,0:T(8,128)(2,1)}, bf16[384,1024]{1,0:T(8,128)(2,1)}, u32[]{:S(2)}, u32[]{:S(2)}) collective-permute-start(bf16[384,1024]{1,0:T(8,128)(2,1)} %get-tuple-element.95), channel_id=1, source_target_pairs={{0,8},{8,0},{16,24},{24,16},{1,9},{9,1},{17,25},{25,17},{2,10},{10... | collective-permute-start | bytes 2359304 | tf_op jit(solution)/shard_map/ppermute | solution.py:120
  82.4 67.5 %collective-permute-start.28 = (bf16[384,1024]{1,0:T(8,128)(2,1)}, bf16[384,1024]{1,0:T(8,128)(2,1)}, u32[]{:S(2)}, u32[]{:S(2)}) collective-permute-start(bf16[384,1024]{1,0:T(8,128)(2,1)} %get-tuple-element.96), channel_id=1, source_target_pairs={{0,16},{8,24},{16,0},{24,8},{1,17},{9,25},{17,1},{25,9},{2,18},{10... | collective-permute-start | bytes 2359304 | tf_op jit(solution)/shard_map/ppermute | solution.py:120
  83.9 59.6 %collective-permute-start.7 = (bf16[384,768]{1,0:T(8,128)(2,1)}, bf16[384,768]{1,0:T(8,128)(2,1)}, u32[]{:S(2)}, u32[]{:S(2)}) collective-permute-start(bf16[384,768]{1,0:T(8,128)(2,1)} %get-tuple-element.72), channel_id=1, source_target_pairs={{0,16},{8,24},{16,0},{24,8},{1,17},{9,25},{17,1},{25,9},{2,18},{10... | collective-permute-start | bytes 1769480 | tf_op jit(solution)/shard_map/ppermute | solution.py:120
  87.5 57.3 %collective-permute-start.8 = (bf16[384,768]{1,0:T(8,128)(2,1)}, bf16[384,768]{1,0:T(8,128)(2,1)}, u32[]{:S(2)}, u32[]{:S(2)}) collective-permute-start(bf16[384,768]{1,0:T(8,128)(2,1)} %get-tuple-element.73), channel_id=1, source_target_pairs={{0,24},{8,16},{16,8},{24,0},{1,25},{9,17},{17,9},{25,1},{2,26},{10... | collective-permute-start | bytes 1769480 | tf_op jit(solution)/shard_map/ppermute | solution.py:120
  88.4 61.9 %collective-permute-start.29 = (bf16[384,1024]{1,0:T(8,128)(2,1)}, bf16[384,1024]{1,0:T(8,128)(2,1)}, u32[]{:S(2)}, u32[]{:S(2)}) collective-permute-start(bf16[384,1024]{1,0:T(8,128)(2,1)} %get-tuple-element.97), channel_id=1, source_target_pairs={{0,24},{8,16},{16,8},{24,0},{1,25},{9,17},{17,9},{25,1},{2,26},{10... | collective-permute-start | bytes 2359304 | tf_op jit(solution)/shard_map/ppermute | solution.py:120
  143.5 29.0 %collective-permute-start.21 = (bf16[384,1024]{1,0:T(8,128)(2,1)}, bf16[384,1024]{1,0:T(8,128)(2,1)S(1)}, u32[]{:S(2)}, u32[]{:S(2)}) collective-permute-start(bf16[384,1024]{1,0:T(8,128)(2,1)} %get-tuple-element.87), channel_id=1, source_target_pairs={{0,8},{8,0},{16,24},{24,16},{1,9},{9,1},{17,25},{25,17},{2,10},{10... | collective-permute-start | bytes 2359304 | tf_op jit(solution)/shard_map/ppermute | solution.py:120
  144.8 34.5 %collective-permute-start.22 = (bf16[384,1024]{1,0:T(8,128)(2,1)}, bf16[384,1024]{1,0:T(8,128)(2,1)}, u32[]{:S(2)}, u32[]{:S(2)}) collective-permute-start(bf16[384,1024]{1,0:T(8,128)(2,1)} %get-tuple-element.88), channel_id=1, source_target_pairs={{0,16},{8,24},{16,0},{24,8},{1,17},{9,25},{17,1},{25,9},{2,18},{10... | collective-permute-start | bytes 2359304 | tf_op jit(solution)/shard_map/ppermute | solution.py:120
  145.9 37.3 %collective-permute-start.23 = (bf16[384,1024]{1,0:T(8,128)(2,1)}, bf16[384,1024]{1,0:T(8,128)(2,1)}, u32[]{:S(2)}, u32[]{:S(2)}) collective-permute-start(bf16[384,1024]{1,0:T(8,128)(2,1)} %get-tuple-element.89), channel_id=1, source_target_pairs={{0,24},{8,16},{16,8},{24,0},{1,25},{9,17},{17,9},{25,1},{2,26},{10... | collective-permute-start | bytes 2359304 | tf_op jit(solution)/shard_map/ppermute | solution.py:120
  166.5 117.0 %collective-permute-start.30 = (bf16[384,1024]{1,0:T(8,128)(2,1)}, bf16[384,1024]{1,0:T(8,128)(2,1)}, u32[]{:S(2)}, u32[]{:S(2)}) collective-permute-start(bf16[384,1024]{1,0:T(8,128)(2,1)} %get-tuple-element.99), channel_id=1, source_target_pairs={{0,2},{2,0},{4,6},{6,4},{1,3},{3,1},{5,7},{7,5},{8,10},{10,8},{12,... | collective-permute-start | bytes 2359304 | tf_op jit(solution)/shard_map/ppermute | solution.py:120
  169.8 112.8 %collective-permute-start.10 = (bf16[384,768]{1,0:T(8,128)(2,1)}, bf16[384,768]{1,0:T(8,128)(2,1)}, u32[]{:S(2)}, u32[]{:S(2)}) collective-permute-start(bf16[384,768]{1,0:T(8,128)(2,1)} %get-tuple-element.76), channel_id=1, source_target_pairs={{0,4},{2,6},{4,0},{6,2},{1,5},{3,7},{5,1},{7,3},{8,12},{10,14},{12... | collective-permute-start | bytes 1769480 | tf_op jit(solution)/shard_map/ppermute | solution.py:120
  172.5 113.0 %collective-permute-start.31 = (bf16[384,1024]{1,0:T(8,128)(2,1)}, bf16[384,1024]{1,0:T(8,128)(2,1)}, u32[]{:S(2)}, u32[]{:S(2)}) collective-permute-start(bf16[384,1024]{1,0:T(8,128)(2,1)} %get-tuple-element.100), channel_id=1, source_target_pairs={{0,4},{2,6},{4,0},{6,2},{1,5},{3,7},{5,1},{7,3},{8,12},{10,14},{12... | collective-permute-start | bytes 2359304 | tf_op jit(solution)/shard_map/ppermute | solution.py:120
  179.3 108.5 %collective-permute-start.32 = (bf16[384,1024]{1,0:T(8,128)(2,1)}, bf16[384,1024]{1,0:T(8,128)(2,1)}, u32[]{:S(2)}, u32[]{:S(2)}) collective-permute-start(bf16[384,1024]{1,0:T(8,128)(2,1)} %get-tuple-element.101), channel_id=1, source_target_pairs={{0,6},{2,4},{4,2},{6,0},{1,7},{3,5},{5,3},{7,1},{8,14},{10,12},{12... | collective-permute-start | bytes 2359304 | tf_op jit(solution)/shard_map/ppermute | solution.py:120
  183.1 57.4 %collective-permute-start.38 = (bf16[384,512]{1,0:T(8,128)(2,1)}, bf16[384,512]{1,0:T(8,128)(2,1)}, u32[]{:S(2)}, u32[]{:S(2)}) collective-permute-start(bf16[384,512]{1,0:T(8,128)(2,1)} %get-tuple-element.109), channel_id=1, source_target_pairs={{0,6},{2,4},{4,2},{6,0},{1,7},{3,5},{5,3},{7,1},{8,14},{10,12},{12... | collective-permute-start | bytes 1179656 | tf_op jit(solution)/shard_map/ppermute | solution.py:120
  240.6 76.8 %collective-permute-start.24 = (bf16[384,1024]{1,0:T(8,128)(2,1)}, bf16[384,1024]{1,0:T(8,128)(2,1)S(1)}, u32[]{:S(2)}, u32[]{:S(2)}) collective-permute-start(bf16[384,1024]{1,0:T(8,128)(2,1)} %get-tuple-element.91), channel_id=1, source_target_pairs={{0,2},{2,0},{4,6},{6,4},{1,3},{3,1},{5,7},{7,5},{8,10},{10,8},{12,... | collective-permute-start | bytes 2359304 | tf_op jit(solution)/shard_map/ppermute | solution.py:120
  282.6 68.0 %collective-permute-start.25 = (bf16[384,1024]{1,0:T(8,128)(2,1)}, bf16[384,1024]{1,0:T(8,128)(2,1)}, u32[]{:S(2)}, u32[]{:S(2)}) collective-permute-start(bf16[384,1024]{1,0:T(8,128)(2,1)} %get-tuple-element.92), channel_id=1, source_target_pairs={{0,4},{2,6},{4,0},{6,2},{1,5},{3,7},{5,1},{7,3},{8,12},{10,14},{12... | collective-permute-start | bytes 2359304 | tf_op jit(solution)/shard_map/ppermute | solution.py:120
  283.5 67.1 %collective-permute-start.26 = (bf16[384,1024]{1,0:T(8,128)(2,1)}, bf16[384,1024]{1,0:T(8,128)(2,1)}, u32[]{:S(2)}, u32[]{:S(2)}) collective-permute-start(bf16[384,1024]{1,0:T(8,128)(2,1)} %get-tuple-element.93), channel_id=1, source_target_pairs={{0,6},{2,4},{4,2},{6,0},{1,7},{3,5},{5,3},{7,1},{8,14},{10,12},{12... | collective-permute-start | bytes 2359304 | tf_op jit(solution)/shard_map/ppermute | solution.py:120
  285.5 83.8 %collective-permute-start.11 = (bf16[384,768]{1,0:T(8,128)(2,1)}, bf16[384,768]{1,0:T(8,128)(2,1)}, u32[]{:S(2)}, u32[]{:S(2)}) collective-permute-start(bf16[384,768]{1,0:T(8,128)(2,1)} %get-tuple-element.77), channel_id=1, source_target_pairs={{0,6},{2,4},{4,2},{6,0},{1,7},{3,5},{5,3},{7,1},{8,14},{10,12},{12... | collective-permute-start | bytes 1769480 | tf_op jit(solution)/shard_map/ppermute | solution.py:120
  287.8 81.5 %collective-permute-start.9 = (bf16[384,768]{1,0:T(8,128)(2,1)}, bf16[384,768]{1,0:T(8,128)(2,1)}, u32[]{:S(2)}, u32[]{:S(2)}) collective-permute-start(bf16[384,768]{1,0:T(8,128)(2,1)} %get-tuple-element.75), channel_id=1, source_target_pairs={{0,2},{2,0},{4,6},{6,4},{1,3},{3,1},{5,7},{7,5},{8,10},{10,8},{12,... | collective-permute-start | bytes 1769480 | tf_op jit(solution)/shard_map/ppermute | solution.py:120
  317.3 55.2 %collective-permute-start.3 = (bf16[384,256]{1,0:T(8,128)(2,1)}, bf16[384,256]{1,0:T(8,128)(2,1)S(1)}, u32[]{:S(2)}, u32[]{:S(2)}) collective-permute-start(bf16[384,256]{1,0:T(8,128)(2,1)} %get-tuple-element.67), channel_id=1, source_target_pairs={{0,2},{2,0},{4,6},{6,4},{1,3},{3,1},{5,7},{7,5},{8,10},{10,8},{12,... | collective-permute-start | bytes 589832 | tf_op jit(solution)/shard_map/ppermute | solution.py:120
  350.6 41.0 %collective-permute-start.4 = (bf16[384,256]{1,0:T(8,128)(2,1)}, bf16[384,256]{1,0:T(8,128)(2,1)}, u32[]{:S(2)}, u32[]{:S(2)}) collective-permute-start(bf16[384,256]{1,0:T(8,128)(2,1)} %get-tuple-element.68), channel_id=1, source_target_pairs={{0,4},{2,6},{4,0},{6,2},{1,5},{3,7},{5,1},{7,3},{8,12},{10,14},{12... | collective-permute-start | bytes 589832 | tf_op jit(solution)/shard_map/ppermute | solution.py:120
  350.6 41.0 %collective-permute-start.5 = (bf16[384,256]{1,0:T(8,128)(2,1)}, bf16[384,256]{1,0:T(8,128)(2,1)}, u32[]{:S(2)}, u32[]{:S(2)}) collective-permute-start(bf16[384,256]{1,0:T(8,128)(2,1)} %get-tuple-element.69), channel_id=1, source_target_pairs={{0,6},{2,4},{4,2},{6,0},{1,7},{3,5},{5,3},{7,1},{8,14},{10,12},{12... | collective-permute-start | bytes 589832 | tf_op jit(solution)/shard_map/ppermute | solution.py:120
  (36 other events, 536.5 us)

commit v2 on v1

--- a/solution.py
+++ b/solution.py
@@ -6,24 +6,46 @@
 from jax.sharding import PartitionSpec as P
 
 
-TP_FIRST = 1
-EP_FIRST = (1, 2, 4, 4, 3, 1)
+SHARES = {"X": 1, "Y": 3, "0": 2, "1": 4, "2": 8, "3": 8, "4": 4, "5": 2}
+TP_FIRST = "XY"
 ORDER = (
-    "AX", "A0", "A1", "B0", "A2", "B1", "HX", "A3", "C0", "B2", "A4",
-    "C1", "B3", "A5", "BX", "B4", "B5", "C2", "C3", "CX", "C4", "C5",
+    "AX", "AY", "A0", "A1", "B0", "HX", "A2", "B1", "HY", "A3", "C0", "B2", "A4",
+    "BX", "C1", "BY", "A5", "B3", "B4", "B5", "C2", "CX", "CY", "C3", "C4", "C5",
 )
 ANY = pl.BlockSpec(memory_space=pl.ANY)
 SCALARS = pl.BlockSpec(memory_space=pltpu.SMEM)
 PARAMS = pltpu.CompilerParams(vmem_limit_bytes=66_000_000)
 
 
-def tile_of(width):
-    return 256 if width % 256 == 0 else 128
+def tile_of(offset, width):
+    return 256 if offset % 256 == 0 and width % 256 == 0 else 128
+
+
+def spread(hidden):
+    total = sum(SHARES.values())
+    columns = hidden // 128
+    edges, done = [0], 0
+    for share in SHARES.values():
+        done += share
+        edges.append(-(-done * columns // total) * 128)
+    return {chunk: (low, high - low) for chunk, low, high in zip(SHARES, edges, edges[1:])}
+
+
+def axis_of(stage, chunk):
+    if stage == "A":
+        return "tp" if chunk in TP_FIRST else "ep"
+    if stage == "B":
+        return "ep" if chunk in TP_FIRST else "tp"
+    return "ep" if stage == "H" else None
+
+
+def steps_of(axis, count):
+    return range(count - 1, 0, -1) if axis == "tp" else range(1, count)
 
 
 def pick_rows(weight, spans, offset, width, block_rows):
     count = spans.shape[0]
-    tile = tile_of(width)
+    tile = tile_of(offset, width)
     rows = weight.shape[1]
 
     def kernel(spans_ref, weight_ref, *refs):
@@ -116,10 +138,10 @@
 
 def exchange(pieces, axis):
     count = len(pieces)
-    return [pieces[0]] + [
-        lax.ppermute(pieces[step], axis, [(index, index ^ step) for index in range(count)])
-        for step in range(1, count)
-    ]
+    moved = {0: pieces[0]}
+    for step in steps_of(axis, count):
+        moved[step] = lax.ppermute(pieces[step], axis, [(index, index ^ step) for index in range(count)])
+    return [moved[step] for step in range(count)]
 
 
 def local(down_weight, owned_span):
@@ -141,31 +163,25 @@
     picks_x = jnp.take(column_experts, steps ^ me) ^ me
     columns = (steps ^ mine) * hidden
     columns_x = (steps ^ mine ^ me ^ jnp.take(column_experts, me)) * hidden
-    unit = hidden // (TP_FIRST + sum(EP_FIRST))
     shape = (block_rows, tp_count * hidden)
+    chunks = spread(hidden)
 
-    offsets = {"X": 0}
-    start = TP_FIRST * unit
-    for chunk, share in enumerate(EP_FIRST):
-        offsets[str(chunk)] = start
-        start += share * unit
     moved = {}
     saved = []
-    for event in ORDER:
-        stage, chunk = event
-        first = chunk == "X"
+    for stage, chunk in ORDER:
+        first = chunk in TP_FIRST
+        offset, width = chunks[chunk]
         if stage == "A":
-            width = (TP_FIRST if first else EP_FIRST[int(chunk)]) * unit
-            sent = pick_rows(weight, spans_tp if first else spans_ep, offsets[chunk], width, block_rows)
-            moved[chunk] = exchange(sent, "tp" if first else "ep")
+            sent = pick_rows(weight, spans_tp if first else spans_ep, offset, width, block_rows)
         elif stage == "H":
-            moved[chunk] = exchange(moved[chunk], "ep")
+            sent = moved[chunk]
         elif stage == "B":
             sent = choose(moved[chunk], picks_x if first else picks)
-            moved[chunk] = exchange(sent, "ep" if first else "tp")
         else:
-            places = (columns_x if first else columns) + offsets[chunk]
+            places = (columns_x if first else columns) + offset
             saved = [place(saved, moved[chunk], places, shape)]
+            continue
+        moved[chunk] = exchange(sent, axis_of(stage, chunk))
     return saved[0][None, None]
 
 

time: 399 us -> 398 us (level)
  the two profiles are of different devices: /device:TPU:0 before, /device:TPU:22 now
where the time goes in v2:
time: 398 us; the launch traced here: 397 us
  waiting for transfers between devices  242 us (61%)
  Pallas kernels  76.5 us (19%)
  starting transfers between devices  66.7 us (17%)
  other arithmetic  6.07 us (2%)
  local copies, waits for them, and re-layouts  4.72 us (1%)
    ppermute x54, waiting for transfers between devices, exchange(): lax.ppermute(pieces[step], axis, [(index, index ^ step) for index in rang...  242 us
    ppermute x54, starting transfers between devices, exchange(): lax.ppermute(pieces[step], axis, [(index, index ^ step) for index in rang...  66.7 us
    pallas_call x8, Pallas kernels, pick_rows(): pl.pallas_call(kernel, grid_spec=pltpu.PrefetchScalarGridSpec(num_scalar_...  30 us
    pallas_call x8, Pallas kernels, choose(): pl.pallas_call(kernel, in_specs=[SCALARS] + [ANY] * count, out_specs=[ANY...  23.3 us
    pallas_call x8, Pallas kernels, place(): pl.pallas_call(kernel, in_specs=[SCALARS] + [ANY] * (count + len(saved)),...  23.1 us
  transfers between devices with their start and end apart: 54, of which 20 were waited for; matrix products, arithmetic and copies ran while one was open for 2% of the time, Pallas kernels for 18%

profile of v2, /device:TPU:22, one launch (start us, length us, event | category | flops | bytes accessed | tf_op | source)
XLA Modules:
  0.0 396.9 jit_solution(10041421612462623552)
XLA Ops:
  32.6 3.4 pick_rows.14
  36.0 4.1 %pick_rows.11 = (bf16[384,384]{1,0:T(8,128)(2,1)}, bf16[384,384]{1,0:T(8,128)(2,1)}, bf16[384,384]{1,0:T(8,128)(2,1)}, bf16[384,384]{1,0:T(8,128)(2,1)}) custom-call(s32[4]{0:T(128)} %broadcast_select_fusion.spans_ref, bf16[4096,1536]{1,0:T(8,128)(2,1)} %bitcast.12), custom_call_target="tpu_custom_call" | custom-call | tf_op jit(solution)/shard_map/pick_rows/pallas_call | solution.py:58
  61.5 4.7 %collective-permute-done.20 = bf16[384,384]{1,0:T(8,128)(2,1)} collective-permute-done((bf16[384,384]{1,0:T(8,128)(2,1)}, bf16[384,384]{1,0:T(8,128)(2,1)}, u32[]{:S(2)}, u32[]{:S(2)}) %collective-permute-start.20) | collective-permute-done | bytes 294944 | tf_op jit(solution)/shard_map/ppermute | solution.py:143
  67.4 12.8 %collective-permute-done.22 = bf16[384,384]{1,0:T(8,128)(2,1)} collective-permute-done((bf16[384,384]{1,0:T(8,128)(2,1)}, bf16[384,384]{1,0:T(8,128)(2,1)}, u32[]{:S(2)}, u32[]{:S(2)}) %collective-permute-start.22) | collective-permute-done | bytes 294944 | tf_op jit(solution)/shard_map/ppermute | solution.py:143
  81.5 3.3 pick_rows.9
  89.9 11.4 %collective-permute-done.43.refs_2_ = bf16[384,512]{1,0:T(8,128)(2,1)} collective-permute-done((bf16[384,512]{1,0:T(8,128)(2,1)}, bf16[384,512]{1,0:T(8,128)(2,1)}, u32[]{:S(2)}, u32[]{:S(2)}) %collective-permute-start.43) | collective-permute-done | bytes 393248 | tf_op jit(solution)/shard_map/ppermute | solution.py:143
  103.0 5.5 %pick_rows.13 = (bf16[384,1024]{1,0:T(8,128)(2,1)}, bf16[384,1024]{1,0:T(8,128)(2,1)}, bf16[384,1024]{1,0:T(8,128)(2,1)}, bf16[384,1024]{1,0:T(8,128)(2,1)}) custom-call(s32[4]{0:T(128)} %broadcast_select_fusion.1.spans_ref, bf16[4096,1536]{1,0:T(8,128)(2,1)} %bitcast.14), custom_call_target="tpu_custom_call" | custom-call | tf_op jit(solution)/shard_map/pick_rows/pallas_call | solution.py:58
  108.9 4.0 %collective-permute-done.7.refs_2_ = bf16[384,512]{1,0:T(8,128)(2,1)} collective-permute-done((bf16[384,512]{1,0:T(8,128)(2,1)}, bf16[384,512]{1,0:T(8,128)(2,1)}, u32[]{:S(2)}, u32[]{:S(2)}) %collective-permute-start.7) | collective-permute-done | bytes 393248 | tf_op jit(solution)/shard_map/ppermute | solution.py:143
  116.5 4.1 %collective-permute-done.19.refs_1_ = bf16[384,384]{1,0:T(8,128)(2,1)} collective-permute-done((bf16[384,384]{1,0:T(8,128)(2,1)}, bf16[384,384]{1,0:T(8,128)(2,1)}, u32[]{:S(2)}, u32[]{:S(2)}) %collective-permute-start.19) | collective-permute-done | bytes 294944 | tf_op jit(solution)/shard_map/ppermute | solution.py:143
  125.7 31.1 %collective-permute-done.21.refs_2_ = bf16[384,384]{1,0:T(8,128)(2,1)} collective-permute-done((bf16[384,384]{1,0:T(8,128)(2,1)}, bf16[384,384]{1,0:T(8,128)(2,1)}, u32[]{:S(2)}, u32[]{:S(2)}) %collective-permute-start.21) | collective-permute-done | bytes 294944 | tf_op jit(solution)/shard_map/ppermute | solution.py:143
  156.8 5.3 %pick_rows.10 = (bf16[384,1024]{1,0:T(8,128)(2,1)}, bf16[384,1024]{1,0:T(8,128)(2,1)}, bf16[384,1024]{1,0:T(8,128)(2,1)}, bf16[384,1024]{1,0:T(8,128)(2,1)}) custom-call(s32[4]{0:T(128)} %broadcast_select_fusion.1.spans_ref, bf16[4096,1536]{1,0:T(8,128)(2,1)} %bitcast.15), custom_call_target="tpu_custom_call" | custom-call | tf_op jit(solution)/shard_map/pick_rows/pallas_call | solution.py:58
  167.0 3.6 collective-permute-start.14
  171.6 3.6 choose.13
  175.2 14.0 %collective-permute-done.46.refs_2_ = bf16[384,512]{1,0:T(8,128)(2,1)} collective-permute-done((bf16[384,512]{1,0:T(8,128)(2,1)}, bf16[384,512]{1,0:T(8,128)(2,1)}, u32[]{:S(2)}, u32[]{:S(2)}) %collective-permute-start.46) | collective-permute-done | bytes 393248 | tf_op jit(solution)/shard_map/ppermute | solution.py:143
  193.8 3.8 collective-permute-done.47.refs_3_
  204.0 12.2 %collective-permute-done.10.refs_2_ = bf16[384,512]{1,0:T(8,128)(2,1)} collective-permute-done((bf16[384,512]{1,0:T(8,128)(2,1)}, bf16[384,512]{1,0:T(8,128)(2,1)}, u32[]{:S(2)}, u32[]{:S(2)}) %collective-permute-start.10) | collective-permute-done | bytes 393248 | tf_op jit(solution)/shard_map/ppermute | solution.py:143
  218.5 3.5 choose.10
  228.2 41.0 %collective-permute-done.40.refs_2_ = bf16[384,1024]{1,0:T(8,128)(2,1)} collective-permute-done((bf16[384,1024]{1,0:T(8,128)(2,1)}, bf16[384,1024]{1,0:T(8,128)(2,1)}, u32[]{:S(2)}, u32[]{:S(2)}) %collective-permute-start.40) | collective-permute-done | bytes 786464 | tf_op jit(solution)/shard_map/ppermute | solution.py:143
  270.9 56.3 %collective-permute-done.41.refs_3_ = bf16[384,1024]{1,0:T(8,128)(2,1)} collective-permute-done((bf16[384,1024]{1,0:T(8,128)(2,1)}, bf16[384,1024]{1,0:T(8,128)(2,1)}, u32[]{:S(2)}, u32[]{:S(2)}) %collective-permute-start.41) | collective-permute-done | bytes 786464 | tf_op jit(solution)/shard_map/ppermute | solution.py:143
  334.2 9.9 %collective-permute-done.16.refs_2_ = bf16[384,1024]{1,0:T(8,128)(2,1)} collective-permute-done((bf16[384,1024]{1,0:T(8,128)(2,1)}, bf16[384,1024]{1,0:T(8,128)(2,1)}, u32[]{:S(2)}, u32[]{:S(2)}) %collective-permute-start.16) | collective-permute-done | bytes 786464 | tf_op jit(solution)/shard_map/ppermute | solution.py:143
  344.1 3.4 collective-permute-start.4
  347.4 21.9 %collective-permute-done.17.refs_3_ = bf16[384,1024]{1,0:T(8,128)(2,1)} collective-permute-done((bf16[384,1024]{1,0:T(8,128)(2,1)}, bf16[384,1024]{1,0:T(8,128)(2,1)}, u32[]{:S(2)}, u32[]{:S(2)}) %collective-permute-start.17) | collective-permute-done | bytes 786464 | tf_op jit(solution)/shard_map/ppermute | solution.py:143
  378.4 3.5 place.10.refs_4_
  387.1 3.5 place.13.refs_4_
  (160 shorter events, 126.0 us)
Async XLA Ops:
  48.2 40.3 %collective-permute-start.42 = (bf16[384,512]{1,0:T(8,128)(2,1)}, bf16[384,512]{1,0:T(8,128)(2,1)S(1)}, u32[]{:S(2)}, u32[]{:S(2)}) collective-permute-start(bf16[384,512]{1,0:T(8,128)(2,1)} %get-tuple-element.119), channel_id=1, source_target_pairs={{0,8},{8,0},{16,24},{24,16},{1,9},{9,1},{17,25},{25,17},{2,10},{10... | collective-permute-start | bytes 1179656 | tf_op jit(solution)/shard_map/ppermute | solution.py:143
  50.6 29.6 %collective-permute-start.22 = (bf16[384,384]{1,0:T(8,128)(2,1)}, bf16[384,384]{1,0:T(8,128)(2,1)}, u32[]{:S(2)}, u32[]{:S(2)}) collective-permute-start(bf16[384,384]{1,0:T(8,128)(2,1)} %get-tuple-element.97), channel_id=1, source_target_pairs={{0,6},{2,4},{4,2},{6,0},{1,7},{3,5},{5,3},{7,1},{8,14},{10,12},{12... | collective-permute-start | bytes 884744 | tf_op jit(solution)/shard_map/ppermute | solution.py:143
  58.6 26.3 %collective-permute-start.51 = (bf16[384,256]{1,0:T(8,128)(2,1)}, bf16[384,256]{1,0:T(8,128)(2,1)}, u32[]{:S(2)}, u32[]{:S(2)}) collective-permute-start(bf16[384,256]{1,0:T(8,128)(2,1)} %get-tuple-element.131), channel_id=1, source_target_pairs={{0,2},{2,0},{4,6},{6,4},{1,3},{3,1},{5,7},{7,5},{8,10},{10,8},{12,... | collective-permute-start | bytes 589832 | tf_op jit(solution)/shard_map/ppermute | solution.py:143
  87.1 25.9 %collective-permute-start.7 = (bf16[384,512]{1,0:T(8,128)(2,1)}, bf16[384,512]{1,0:T(8,128)(2,1)}, u32[]{:S(2)}, u32[]{:S(2)}) collective-permute-start(bf16[384,512]{1,0:T(8,128)(2,1)} %get-tuple-element.80), channel_id=1, source_target_pairs={{0,16},{8,24},{16,0},{24,8},{1,17},{9,25},{17,1},{25,9},{2,18},{10... | collective-permute-start | bytes 1179656 | tf_op jit(solution)/shard_map/ppermute | solution.py:143
  88.5 26.5 %collective-permute-start.8 = (bf16[384,512]{1,0:T(8,128)(2,1)}, bf16[384,512]{1,0:T(8,128)(2,1)}, u32[]{:S(2)}, u32[]{:S(2)}) collective-permute-start(bf16[384,512]{1,0:T(8,128)(2,1)} %get-tuple-element.81), channel_id=1, source_target_pairs={{0,24},{8,16},{16,8},{24,0},{1,25},{9,17},{17,9},{25,1},{2,26},{10... | collective-permute-start | bytes 1179656 | tf_op jit(solution)/shard_map/ppermute | solution.py:143
  108.5 58.6 %collective-permute-start.36 = (bf16[384,1024]{1,0:T(8,128)(2,1)}, bf16[384,1024]{1,0:T(8,128)(2,1)}, u32[]{:S(2)}, u32[]{:S(2)}) collective-permute-start(bf16[384,1024]{1,0:T(8,128)(2,1)} %get-tuple-element.111), channel_id=1, source_target_pairs={{0,8},{8,0},{16,24},{24,16},{1,9},{9,1},{17,25},{25,17},{2,10},{10... | collective-permute-start | bytes 2359304 | tf_op jit(solution)/shard_map/ppermute | solution.py:143
  108.9 58.1 %collective-permute-start.37 = (bf16[384,1024]{1,0:T(8,128)(2,1)}, bf16[384,1024]{1,0:T(8,128)(2,1)}, u32[]{:S(2)}, u32[]{:S(2)}) collective-permute-start(bf16[384,1024]{1,0:T(8,128)(2,1)} %get-tuple-element.112), channel_id=1, source_target_pairs={{0,16},{8,24},{16,0},{24,8},{1,17},{9,25},{17,1},{25,9},{2,18},{10... | collective-permute-start | bytes 2359304 | tf_op jit(solution)/shard_map/ppermute | solution.py:143
  113.0 43.8 %collective-permute-start.21 = (bf16[384,384]{1,0:T(8,128)(2,1)}, bf16[384,384]{1,0:T(8,128)(2,1)}, u32[]{:S(2)}, u32[]{:S(2)}) collective-permute-start(bf16[384,384]{1,0:T(8,128)(2,1)} %collective-permute-done.20), channel_id=1, source_target_pairs={{0,16},{8,24},{16,0},{24,8},{1,17},{9,25},{17,1},{25,9},{2,18},{10... | collective-permute-start | bytes 884744 | tf_op jit(solution)/shard_map/ppermute | solution.py:143
  115.0 55.7 %collective-permute-start.38 = (bf16[384,1024]{1,0:T(8,128)(2,1)}, bf16[384,1024]{1,0:T(8,128)(2,1)}, u32[]{:S(2)}, u32[]{:S(2)}) collective-permute-start(bf16[384,1024]{1,0:T(8,128)(2,1)} %get-tuple-element.113), channel_id=1, source_target_pairs={{0,24},{8,16},{16,8},{24,0},{1,25},{9,17},{17,9},{25,1},{2,26},{10... | collective-permute-start | bytes 2359304 | tf_op jit(solution)/shard_map/ppermute | solution.py:143
  120.5 41.6 %collective-permute-start.23 = (bf16[384,384]{1,0:T(8,128)(2,1)}, bf16[384,384]{1,0:T(8,128)(2,1)}, u32[]{:S(2)}, u32[]{:S(2)}) collective-permute-start(bf16[384,384]{1,0:T(8,128)(2,1)} %collective-permute-done.22), channel_id=1, source_target_pairs={{0,24},{8,16},{16,8},{24,0},{1,25},{9,17},{17,9},{25,1},{2,26},{10... | collective-permute-start | bytes 884744 | tf_op jit(solution)/shard_map/ppermute | solution.py:143
  162.1 38.3 %collective-permute-start.12 = (bf16[384,1024]{1,0:T(8,128)(2,1)}, bf16[384,1024]{1,0:T(8,128)(2,1)S(1)}, u32[]{:S(2)}, u32[]{:S(2)}) collective-permute-start(bf16[384,1024]{1,0:T(8,128)(2,1)} %get-tuple-element.87), channel_id=1, source_target_pairs={{0,8},{8,0},{16,24},{24,16},{1,9},{9,1},{17,25},{25,17},{2,10},{10... | collective-permute-start | bytes 2359304 | tf_op jit(solution)/shard_map/ppermute | solution.py:143
  167.0 34.3 %collective-permute-start.13 = (bf16[384,1024]{1,0:T(8,128)(2,1)}, bf16[384,1024]{1,0:T(8,128)(2,1)}, u32[]{:S(2)}, u32[]{:S(2)}) collective-permute-start(bf16[384,1024]{1,0:T(8,128)(2,1)} %get-tuple-element.88), channel_id=1, source_target_pairs={{0,16},{8,24},{16,0},{24,8},{1,17},{9,25},{17,1},{25,9},{2,18},{10... | collective-permute-start | bytes 2359304 | tf_op jit(solution)/shard_map/ppermute | solution.py:143
  167.0 35.2 %collective-permute-start.14 = (bf16[384,1024]{1,0:T(8,128)(2,1)}, bf16[384,1024]{1,0:T(8,128)(2,1)}, u32[]{:S(2)}, u32[]{:S(2)}) collective-permute-start(bf16[384,1024]{1,0:T(8,128)(2,1)} %get-tuple-element.89), channel_id=1, source_target_pairs={{0,24},{8,16},{16,8},{24,0},{1,25},{9,17},{17,9},{25,1},{2,26},{10... | collective-permute-start | bytes 2359304 | tf_op jit(solution)/shard_map/ppermute | solution.py:143
  170.6 27.0 %collective-permute-start.47 = (bf16[384,512]{1,0:T(8,128)(2,1)}, bf16[384,512]{1,0:T(8,128)(2,1)}, u32[]{:S(2)}, u32[]{:S(2)}) collective-permute-start(bf16[384,512]{1,0:T(8,128)(2,1)} %get-tuple-element.125), channel_id=1, source_target_pairs={{0,6},{2,4},{4,2},{6,0},{1,7},{3,5},{5,3},{7,1},{8,14},{10,12},{12... | collective-permute-start | bytes 1179656 | tf_op jit(solution)/shard_map/ppermute | solution.py:143
  189.2 36.8 %collective-permute-start.39 = (bf16[384,1024]{1,0:T(8,128)(2,1)}, bf16[384,1024]{1,0:T(8,128)(2,1)}, u32[]{:S(2)}, u32[]{:S(2)}) collective-permute-start(bf16[384,1024]{1,0:T(8,128)(2,1)} %get-tuple-element.115), channel_id=1, source_target_pairs={{0,2},{2,0},{4,6},{6,4},{1,3},{3,1},{5,7},{7,5},{8,10},{10,8},{12,... | collective-permute-start | bytes 2359304 | tf_op jit(solution)/shard_map/ppermute | solution.py:143
  216.2 53.0 %collective-permute-start.40 = (bf16[384,1024]{1,0:T(8,128)(2,1)}, bf16[384,1024]{1,0:T(8,128)(2,1)}, u32[]{:S(2)}, u32[]{:S(2)}) collective-permute-start(bf16[384,1024]{1,0:T(8,128)(2,1)} %get-tuple-element.116), channel_id=1, source_target_pairs={{0,4},{2,6},{4,0},{6,2},{1,5},{3,7},{5,1},{7,3},{8,12},{10,14},{12... | collective-permute-start | bytes 2359304 | tf_op jit(solution)/shard_map/ppermute | solution.py:143
  216.2 111.0 %collective-permute-start.41 = (bf16[384,1024]{1,0:T(8,128)(2,1)}, bf16[384,1024]{1,0:T(8,128)(2,1)}, u32[]{:S(2)}, u32[]{:S(2)}) collective-permute-start(bf16[384,1024]{1,0:T(8,128)(2,1)} %get-tuple-element.117), channel_id=1, source_target_pairs={{0,6},{2,4},{4,2},{6,0},{1,7},{3,5},{5,3},{7,1},{8,14},{10,12},{12... | collective-permute-start | bytes 2359304 | tf_op jit(solution)/shard_map/ppermute | solution.py:143
  222.0 110.0 %collective-permute-start.15 = (bf16[384,1024]{1,0:T(8,128)(2,1)}, bf16[384,1024]{1,0:T(8,128)(2,1)S(1)}, u32[]{:S(2)}, u32[]{:S(2)}) collective-permute-start(bf16[384,1024]{1,0:T(8,128)(2,1)} %get-tuple-element.91), channel_id=1, source_target_pairs={{0,2},{2,0},{4,6},{6,4},{1,3},{3,1},{5,7},{7,5},{8,10},{10,8},{12,... | collective-permute-start | bytes 2359304 | tf_op jit(solution)/shard_map/ppermute | solution.py:143
  224.2 119.9 %collective-permute-start.16 = (bf16[384,1024]{1,0:T(8,128)(2,1)}, bf16[384,1024]{1,0:T(8,128)(2,1)}, u32[]{:S(2)}, u32[]{:S(2)}) collective-permute-start(bf16[384,1024]{1,0:T(8,128)(2,1)} %get-tuple-element.92), channel_id=1, source_target_pairs={{0,4},{2,6},{4,0},{6,2},{1,5},{3,7},{5,1},{7,3},{8,12},{10,14},{12... | collective-permute-start | bytes 2359304 | tf_op jit(solution)/shard_map/ppermute | solution.py:143
  226.0 143.3 %collective-permute-start.17 = (bf16[384,1024]{1,0:T(8,128)(2,1)}, bf16[384,1024]{1,0:T(8,128)(2,1)}, u32[]{:S(2)}, u32[]{:S(2)}) collective-permute-start(bf16[384,1024]{1,0:T(8,128)(2,1)} %get-tuple-element.93), channel_id=1, source_target_pairs={{0,6},{2,4},{4,2},{6,0},{1,7},{3,5},{5,3},{7,1},{8,14},{10,12},{12... | collective-permute-start | bytes 2359304 | tf_op jit(solution)/shard_map/ppermute | solution.py:143
  269.2 121.4 %collective-permute-start.11 = (bf16[384,512]{1,0:T(8,128)(2,1)}, bf16[384,512]{1,0:T(8,128)(2,1)}, u32[]{:S(2)}, u32[]{:S(2)}) collective-permute-start(bf16[384,512]{1,0:T(8,128)(2,1)} %get-tuple-element.85), channel_id=1, source_target_pairs={{0,6},{2,4},{4,2},{6,0},{1,7},{3,5},{5,3},{7,1},{8,14},{10,12},{12... | collective-permute-start | bytes 1179656 | tf_op jit(solution)/shard_map/ppermute | solution.py:143
  327.2 63.5 %collective-permute-start.9 = (bf16[384,512]{1,0:T(8,128)(2,1)}, bf16[384,512]{1,0:T(8,128)(2,1)}, u32[]{:S(2)}, u32[]{:S(2)}) collective-permute-start(bf16[384,512]{1,0:T(8,128)(2,1)} %get-tuple-element.83), channel_id=1, source_target_pairs={{0,2},{2,0},{4,6},{6,4},{1,3},{3,1},{5,7},{7,5},{8,10},{10,8},{12,... | collective-permute-start | bytes 1179656 | tf_op jit(solution)/shard_map/ppermute | solution.py:143
  332.1 61.4 %collective-permute-start.3 = (bf16[384,256]{1,0:T(8,128)(2,1)}, bf16[384,256]{1,0:T(8,128)(2,1)S(1)}, u32[]{:S(2)}, u32[]{:S(2)}) collective-permute-start(bf16[384,256]{1,0:T(8,128)(2,1)} %get-tuple-element.75), channel_id=1, source_target_pairs={{0,2},{2,0},{4,6},{6,4},{1,3},{3,1},{5,7},{7,5},{8,10},{10,8},{12,... | collective-permute-start | bytes 589832 | tf_op jit(solution)/shard_map/ppermute | solution.py:143
  344.1 49.5 %collective-permute-start.4 = (bf16[384,256]{1,0:T(8,128)(2,1)}, bf16[384,256]{1,0:T(8,128)(2,1)}, u32[]{:S(2)}, u32[]{:S(2)}) collective-permute-start(bf16[384,256]{1,0:T(8,128)(2,1)} %get-tuple-element.76), channel_id=1, source_target_pairs={{0,4},{2,6},{4,0},{6,2},{1,5},{3,7},{5,1},{7,3},{8,12},{10,14},{12... | collective-permute-start | bytes 589832 | tf_op jit(solution)/shard_map/ppermute | solution.py:143
  (44 other events, 805.4 us)

commit v3 on v2

v3 whole, which is shorter than its diff:
```python
import jax
import jax.numpy as jnp
from jax import lax
from jax.experimental import pallas as pl
from jax.experimental.pallas import tpu as pltpu
from jax.sharding import PartitionSpec as P


SHARES = {"X": 1, "Y": 3, "0": 2, "1": 4, "2": 8, "3": 8, "4": 4, "5": 2}
TP_FIRST = "XY"
ORDER = (
    "AX", "AY", "A0", "A1", "B0", "HX", "A2", "B1", "HY", "A3", "C0", "B2", "A4",
    "BX", "C1", "BY", "A5", "B3", "B4", "B5", "C2", "CX", "CY", "C3", "C4", "C5",
)
ANY = pl.BlockSpec(memory_space=pl.ANY)
SCALARS = pl.BlockSpec(memory_space=pltpu.SMEM)
WHOLE = pl.BlockSpec(memory_space=pltpu.VMEM)


def position():
    return lax.axis_index("ep"), lax.axis_index("tp"), lax.axis_index("dp")


def expert_of(owned, row, column, replica, sizes):
    return lax.div(owned[row, replica, column], sizes[1] * sizes[2])


def span_of(owned, expert, row, column, replica, sizes):
    span = owned[row, replica, column] - (expert * sizes[2] + replica) * sizes[1]
    return jnp.where((span >= 0) & (span < sizes[1]), span, 0)


def tile_of(offset, width):
    return 256 if offset % 256 == 0 and width % 256 == 0 else 128


def spread(hidden):
    total = sum(SHARES.values())
    columns = hidden // 128
    edges, done = [0], 0
    for share in SHARES.values():
        done += share
        edges.append(-(-done * columns // total) * 128)
    return {chunk: (low, high - low) for chunk, low, high in zip(SHARES, edges, edges[1:])}


def axis_of(stage, chunk):
    if stage == "A":
        return "tp" if chunk in TP_FIRST else "ep"
    if stage == "B":
        return "ep" if chunk in TP_FIRST else "tp"
    return "ep" if stage == "H" else None


def steps_of(axis, count):
    return range(count - 1, 0, -1) if axis == "tp" else range(1, count)


def pick_rows(weight, owned, sizes, first, offset, width):
    count = sizes[1]
    tile = tile_of(offset, width)
    rows = weight.shape[1]
    block_rows = rows // count

    def kernel(owned_ref, weight_ref, *refs):
        outs, turned = refs[:-1], refs[-1]
        me, mine, replica = position()
        turned[...] = weight_ref[...].T
        for step, out in enumerate(outs):
            owners = [(line, mine ^ step) if first else (me ^ step, line) for line in range(count)]
            span = sum(span_of(owned_ref, me, row, column, replica, sizes) for row, column in owners)
            out[...] = turned[pl.ds(pl.multiple_of(span * block_rows, 16), block_rows), :]

    return pl.pallas_call(
        kernel,
        grid=(width // tile,),
        in_specs=[SCALARS, pl.BlockSpec((tile, rows), lambda step: (offset // tile + step, 0))],
        out_specs=[pl.BlockSpec((block_rows, tile), lambda step: (0, step))] * count,
        out_shape=[jax.ShapeDtypeStruct((block_rows, width), weight.dtype)] * count,
        scratch_shapes=[pltpu.VMEM((rows, tile), weight.dtype)],
        name="pick_rows",
    )(owned, weight)


def choose(pieces, owned, sizes, first):
    count = len(pieces)

    def kernel(owned_ref, *refs):
        ins, outs = refs[:count], refs[count:]
        me, mine, replica = position()
        for step in range(count):
            row, column = (me ^ step, mine) if first else (me, mine ^ step)
            pick = expert_of(owned_ref, row, column, replica, sizes) ^ me
            for source in range(count):
                @pl.when(pick == source)
                def _():
                    outs[step][...] = ins[source][...]

    return pl.pallas_call(
        kernel,
        in_specs=[SCALARS] + [WHOLE] * count,
        out_specs=[WHOLE] * count,
        out_shape=[jax.ShapeDtypeStruct(piece.shape, piece.dtype) for piece in pieces],
        name="choose",
    )(owned, *pieces)


def place(saved, pieces, owned, sizes, first, offset, hidden):
    count = len(pieces)
    block_rows, width = pieces[0].shape

    def kernel(owned_ref, *refs):
        ins, out, sems = refs[:count], refs[-2], refs[-1]
        me, mine, replica = position()
        turn = mine ^ me ^ expert_of(owned_ref, me, mine, replica, sizes) if first else mine
        copies = []
        for step in range(count):
            start = pl.multiple_of((turn ^ step) * hidden + offset, 128)
            copies.append(pltpu.make_async_copy(ins[step], out.at[:, pl.ds(start, width)], sems.at[step]))
        for copy in copies:
            copy.start()
        for copy in copies:
            copy.wait()

    return pl.pallas_call(
        kernel,
        in_specs=[SCALARS] + [WHOLE] * count + [ANY] * len(saved),
        out_specs=ANY,
        out_shape=jax.ShapeDtypeStruct((block_rows, count * hidden), pieces[0].dtype),
        scratch_shapes=[pltpu.SemaphoreType.DMA((count,))],
        input_output_aliases={count + 1: 0} if saved else {},
        name="place",
    )(owned, *pieces, *saved)


def exchange(pieces, axis):
    count = len(pieces)
    moved = {0: pieces[0]}
    for step in steps_of(axis, count):
        moved[step] = lax.ppermute(pieces[step], axis, [(index, index ^ step) for index in range(count)])
    return [moved[step] for step in range(count)]


def local(down_weight, owned_span):
    weight = down_weight[0]
    hidden = weight.shape[0]
    owned = jnp.transpose(owned_span, (0, 2, 1))
    sizes = tuple(lax.axis_size(name) for name in ("ep", "tp", "dp"))
    chunks = spread(hidden)

    moved = {}
    saved = []
    for stage, chunk in ORDER:
        first = chunk in TP_FIRST
        offset, width = chunks[chunk]
        if stage == "A":
            sent = pick_rows(weight, owned, sizes, first, offset, width)
        elif stage == "H":
            sent = moved[chunk]
        elif stage == "B":
            sent = choose(moved[chunk], owned, sizes, first)
        else:
            saved = [place(saved, moved[chunk], owned, sizes, first, offset, hidden)]
            continue
        moved[chunk] = exchange(sent, axis_of(stage, chunk))
    return saved[0][None, None]


def solution(mesh):
    return jax.shard_map(
        local,
        mesh=mesh,
        in_specs=(P("ep", "tp", "dp"), P()),
        out_specs=P("ep", "tp", "dp", None),
        check_vma=False,
    )
```

time: 398 us -> 391 us (0.982)
  the two profiles are of different devices: /device:TPU:22 before, /device:TPU:0 now
where the time goes in v3:
time: 391 us; the launch traced here: 386 us
  waiting for transfers between devices  174 us (45%)
  starting transfers between devices  143 us (37%)
  Pallas kernels  67.6 us (17%)
    ppermute x54, waiting for transfers between devices, exchange(): lax.ppermute(pieces[step], axis, [(index, index ^ step) for index in rang...  174 us
    ppermute x54, starting transfers between devices, exchange(): lax.ppermute(pieces[step], axis, [(index, index ^ step) for index in rang...  143 us
    pallas_call x8, Pallas kernels, pick_rows(): pl.pallas_call(kernel, grid=(width // tile,), in_specs=[SCALARS, pl.Block...  24.7 us
    pallas_call x8, Pallas kernels, choose(): pl.pallas_call(kernel, in_specs=[SCALARS] + [WHOLE] * count, out_specs=[W...  22.3 us
    pallas_call x8, Pallas kernels, place(): pl.pallas_call(kernel, in_specs=[SCALARS] + [WHOLE] * count + [ANY] * len...  20.6 us
  transfers between devices with their start and end apart: 54, of which 14 were waited for; matrix products, arithmetic and copies ran while one was open for 0% of the time, Pallas kernels for 16%

profile of v3, /device:TPU:0, one launch (start us, length us, event | category | flops | bytes accessed | tf_op | source)
XLA Modules:
  0.0 385.7 jit_solution(9609845711976558570)
XLA Ops:
  15.7 4.5 %collective-permute-done.29 = bf16[384,128]{1,0:T(8,128)(2,1)S(1)} collective-permute-done((bf16[384,128]{1,0:T(8,128)(2,1)S(1)}, bf16[384,128]{1,0:T(8,128)(2,1)S(1)}, u32[]{:S(2)}, u32[]{:S(2)}) %collective-permute-start.29) | collective-permute-done | bytes 98336 | tf_op jit(solution)/shard_map/ppermute | solution.py:140
  28.4 3.3 pick_rows.11
  33.8 3.5 collective-permute-start.18
  56.7 6.7 %collective-permute-start.53 = (bf16[384,256]{1,0:T(8,128)(2,1)}, bf16[384,256]{1,0:T(8,128)(2,1)S(1)}, u32[]{:S(2)}, u32[]{:S(2)}) collective-permute-start(bf16[384,256]{1,0:T(8,128)(2,1)} %get-tuple-element.132), channel_id=1, source_target_pairs={{0,6},{2,4},{4,2},{6,0},{1,7},{3,5},{5,3},{7,1},{8,14},{10,12},{12... | collective-permute-start | bytes 589832 | tf_op jit(solution)/shard_map/ppermute | solution.py:140
  67.9 9.8 %collective-permute-done.52.refs_2_ = bf16[384,256]{1,0:T(8,128)(2,1)S(1)} collective-permute-done((bf16[384,256]{1,0:T(8,128)(2,1)}, bf16[384,256]{1,0:T(8,128)(2,1)S(1)}, u32[]{:S(2)}, u32[]{:S(2)}) %collective-permute-start.52) | collective-permute-done | bytes 196640 | tf_op jit(solution)/shard_map/ppermute | solution.py:140
  81.3 4.8 %pick_rows.13 = (bf16[384,1024]{1,0:T(8,128)(2,1)}, bf16[384,1024]{1,0:T(8,128)(2,1)}, bf16[384,1024]{1,0:T(8,128)(2,1)}, bf16[384,1024]{1,0:T(8,128)(2,1)}) custom-call(s32[4,2,4]{2,1,0:T(2,128)} %bitcast.19, bf16[4096,1536]{1,0:T(8,128)(2,1)} %bitcast.9), custom_call_target="tpu_custom_call" | custom-call | tf_op jit(solution)/shard_map/pick_rows/pallas_call | solution.py:74
  91.7 9.3 %collective-permute-done.7.refs_2_ = bf16[384,512]{1,0:T(8,128)(2,1)S(1)} collective-permute-done((bf16[384,512]{1,0:T(8,128)(2,1)}, bf16[384,512]{1,0:T(8,128)(2,1)S(1)}, u32[]{:S(2)}, u32[]{:S(2)}) %collective-permute-start.7) | collective-permute-done | bytes 393248 | tf_op jit(solution)/shard_map/ppermute | solution.py:140
  102.7 18.9 %collective-permute-done.19.refs_1_ = bf16[384,384]{1,0:T(8,128)(2,1)} collective-permute-done((bf16[384,384]{1,0:T(8,128)(2,1)}, bf16[384,384]{1,0:T(8,128)(2,1)}, u32[]{:S(2)}, u32[]{:S(2)}) %collective-permute-start.19) | collective-permute-done | bytes 294944 | tf_op jit(solution)/shard_map/ppermute | solution.py:140
  125.5 20.2 %collective-permute-done.21.refs_2_ = bf16[384,384]{1,0:T(8,128)(2,1)} collective-permute-done((bf16[384,384]{1,0:T(8,128)(2,1)}, bf16[384,384]{1,0:T(8,128)(2,1)}, u32[]{:S(2)}, u32[]{:S(2)}) %collective-permute-start.21) | collective-permute-done | bytes 294944 | tf_op jit(solution)/shard_map/ppermute | solution.py:140
  145.8 9.6 %collective-permute-start.45 = (bf16[384,512]{1,0:T(8,128)(2,1)}, bf16[384,512]{1,0:T(8,128)(2,1)S(1)}, u32[]{:S(2)}, u32[]{:S(2)}) collective-permute-start(bf16[384,512]{1,0:T(8,128)(2,1)} %get-tuple-element.122), channel_id=1, source_target_pairs={{0,2},{2,0},{4,6},{6,4},{1,3},{3,1},{5,7},{7,5},{8,10},{10,8},{12,... | collective-permute-start | bytes 1179656 | tf_op jit(solution)/shard_map/ppermute | solution.py:140
  155.3 4.7 %pick_rows.10 = (bf16[384,1024]{1,0:T(8,128)(2,1)}, bf16[384,1024]{1,0:T(8,128)(2,1)}, bf16[384,1024]{1,0:T(8,128)(2,1)}, bf16[384,1024]{1,0:T(8,128)(2,1)}) custom-call(s32[4,2,4]{2,1,0:T(2,128)} %bitcast.21, bf16[4096,1536]{1,0:T(8,128)(2,1)} %bitcast.10), custom_call_target="tpu_custom_call" | custom-call | tf_op jit(solution)/shard_map/pick_rows/pallas_call | solution.py:74
  170.5 3.8 choose.13
  174.3 17.3 %collective-permute-done.46.refs_2_ = bf16[384,512]{1,0:T(8,128)(2,1)} collective-permute-done((bf16[384,512]{1,0:T(8,128)(2,1)}, bf16[384,512]{1,0:T(8,128)(2,1)}, u32[]{:S(2)}, u32[]{:S(2)}) %collective-permute-start.46) | collective-permute-done | bytes 393248 | tf_op jit(solution)/shard_map/ppermute | solution.py:140
  194.4 5.3 %collective-permute-start.10 = (bf16[384,512]{1,0:T(8,128)(2,1)}, bf16[384,512]{1,0:T(8,128)(2,1)S(1)}, u32[]{:S(2)}, u32[]{:S(2)}) collective-permute-start(bf16[384,512]{1,0:T(8,128)(2,1)} %get-tuple-element.83), channel_id=1, source_target_pairs={{0,4},{2,6},{4,0},{6,2},{1,5},{3,7},{5,1},{7,3},{8,12},{10,14},{12... | collective-permute-start | bytes 1179656 | tf_op jit(solution)/shard_map/ppermute | solution.py:140
  202.6 3.2 collective-permute-start.25
  205.9 9.8 %collective-permute-done.10.refs_2_ = bf16[384,512]{1,0:T(8,128)(2,1)S(1)} collective-permute-done((bf16[384,512]{1,0:T(8,128)(2,1)}, bf16[384,512]{1,0:T(8,128)(2,1)S(1)}, u32[]{:S(2)}, u32[]{:S(2)}) %collective-permute-start.10) | collective-permute-done | bytes 393248 | tf_op jit(solution)/shard_map/ppermute | solution.py:140
  215.7 3.3 collective-permute-start.40
  220.6 4.0 %choose.10 = (bf16[384,1024]{1,0:T(8,128)(2,1)}, bf16[384,1024]{1,0:T(8,128)(2,1)}, bf16[384,1024]{1,0:T(8,128)(2,1)}, bf16[384,1024]{1,0:T(8,128)(2,1)}) custom-call(s32[4,2,4]{2,1,0:T(2,128)} %bitcast.25, bf16[384,1024]{1,0:T(8,128)(2,1)} %get-tuple-element.85.refs_0_, bf16[384,1024]{1,0:T(8,128)(2,1)} %copy-done, bf16[384,1024]{1,0:T(8,128)(2,1)} %copy-done.2, ...), custom_call_target="tpu_custom_call" | custom-call | tf_op jit(solution)/shard_map/choose/pallas_call | solution.py:99
  228.9 44.2 %collective-permute-done.40.refs_2_ = bf16[384,1024]{1,0:T(8,128)(2,1)} collective-permute-done((bf16[384,1024]{1,0:T(8,128)(2,1)}, bf16[384,1024]{1,0:T(8,128)(2,1)}, u32[]{:S(2)}, u32[]{:S(2)}) %collective-permute-start.40) | collective-permute-done | bytes 786464 | tf_op jit(solution)/shard_map/ppermute | solution.py:140
  275.4 53.9 %collective-permute-start.9 = (bf16[384,512]{1,0:T(8,128)(2,1)}, bf16[384,512]{1,0:T(8,128)(2,1)}, u32[]{:S(2)}, u32[]{:S(2)}) collective-permute-start(bf16[384,512]{1,0:T(8,128)(2,1)} %get-tuple-element.82), channel_id=1, source_target_pairs={{0,2},{2,0},{4,6},{6,4},{1,3},{3,1},{5,7},{7,5},{8,10},{10,8},{12,... | collective-permute-start | bytes 1179656 | tf_op jit(solution)/shard_map/ppermute | solution.py:140
  331.7 13.9 %collective-permute-done.16.refs_2_ = bf16[384,1024]{1,0:T(8,128)(2,1)S(1)} collective-permute-done((bf16[384,1024]{1,0:T(8,128)(2,1)}, bf16[384,1024]{1,0:T(8,128)(2,1)S(1)}, u32[]{:S(2)}, u32[]{:S(2)}) %collective-permute-start.16) | collective-permute-done | bytes 786464 | tf_op jit(solution)/shard_map/ppermute | solution.py:140
  352.7 3.6 place.10.refs_4_
  360.4 3.6 place.13.refs_4_
  366.5 17.1 %collective-permute-done.4.refs_2_ = bf16[384,256]{1,0:T(8,128)(2,1)} collective-permute-done((bf16[384,256]{1,0:T(8,128)(2,1)}, bf16[384,256]{1,0:T(8,128)(2,1)}, u32[]{:S(2)}, u32[]{:S(2)}) %collective-permute-start.4) | collective-permute-done | bytes 196640 | tf_op jit(solution)/shard_map/ppermute | solution.py:140
  (186 shorter events, 107.4 us)
Async XLA Ops:
  49.2 30.3 %collective-permute-start.42 = (bf16[384,512]{1,0:T(8,128)(2,1)}, bf16[384,512]{1,0:T(8,128)(2,1)S(1)}, u32[]{:S(2)}, u32[]{:S(2)}) collective-permute-start(bf16[384,512]{1,0:T(8,128)(2,1)} %get-tuple-element.118), channel_id=1, source_target_pairs={{0,8},{8,0},{16,24},{24,16},{1,9},{9,1},{17,25},{25,17},{2,10},{10... | collective-permute-start | bytes 1179656 | tf_op jit(solution)/shard_map/ppermute | solution.py:140
  54.4 23.3 %collective-permute-start.52 = (bf16[384,256]{1,0:T(8,128)(2,1)}, bf16[384,256]{1,0:T(8,128)(2,1)S(1)}, u32[]{:S(2)}, u32[]{:S(2)}) collective-permute-start(bf16[384,256]{1,0:T(8,128)(2,1)} %get-tuple-element.131), channel_id=1, source_target_pairs={{0,4},{2,6},{4,0},{6,2},{1,5},{3,7},{5,1},{7,3},{8,12},{10,14},{12... | collective-permute-start | bytes 589832 | tf_op jit(solution)/shard_map/ppermute | solution.py:140
  86.1 79.7 %collective-permute-start.36 = (bf16[384,1024]{1,0:T(8,128)(2,1)}, bf16[384,1024]{1,0:T(8,128)(2,1)S(1)}, u32[]{:S(2)}, u32[]{:S(2)}) collective-permute-start(bf16[384,1024]{1,0:T(8,128)(2,1)} %get-tuple-element.110), channel_id=1, source_target_pairs={{0,8},{8,0},{16,24},{24,16},{1,9},{9,1},{17,25},{25,17},{2,10},{10... | collective-permute-start | bytes 2359304 | tf_op jit(solution)/shard_map/ppermute | solution.py:140
  86.5 35.1 %collective-permute-start.19 = (bf16[384,384]{1,0:T(8,128)(2,1)}, bf16[384,384]{1,0:T(8,128)(2,1)}, u32[]{:S(2)}, u32[]{:S(2)}) collective-permute-start(bf16[384,384]{1,0:T(8,128)(2,1)} %copy-done.33), channel_id=1, source_target_pairs={{0,8},{8,0},{16,24},{24,16},{1,9},{9,1},{17,25},{25,17},{2,10},{10... | collective-permute-start | bytes 884744 | tf_op jit(solution)/shard_map/ppermute | solution.py:140
  89.9 78.2 %collective-permute-start.37 = (bf16[384,1024]{1,0:T(8,128)(2,1)}, bf16[384,1024]{1,0:T(8,128)(2,1)S(1)}, u32[]{:S(2)}, u32[]{:S(2)}) collective-permute-start(bf16[384,1024]{1,0:T(8,128)(2,1)} %get-tuple-element.111), channel_id=1, source_target_pairs={{0,16},{8,24},{16,0},{24,8},{1,17},{9,25},{17,1},{25,9},{2,18},{10... | collective-permute-start | bytes 2359304 | tf_op jit(solution)/shard_map/ppermute | solution.py:140
  101.0 44.8 %collective-permute-start.21 = (bf16[384,384]{1,0:T(8,128)(2,1)}, bf16[384,384]{1,0:T(8,128)(2,1)}, u32[]{:S(2)}, u32[]{:S(2)}) collective-permute-start(bf16[384,384]{1,0:T(8,128)(2,1)} %copy-done.32), channel_id=1, source_target_pairs={{0,16},{8,24},{16,0},{24,8},{1,17},{9,25},{17,1},{25,9},{2,18},{10... | collective-permute-start | bytes 884744 | tf_op jit(solution)/shard_map/ppermute | solution.py:140
  102.1 67.0 %collective-permute-start.38 = (bf16[384,1024]{1,0:T(8,128)(2,1)}, bf16[384,1024]{1,0:T(8,128)(2,1)}, u32[]{:S(2)}, u32[]{:S(2)}) collective-permute-start(bf16[384,1024]{1,0:T(8,128)(2,1)} %get-tuple-element.112), channel_id=1, source_target_pairs={{0,24},{8,16},{16,8},{24,0},{1,25},{9,17},{17,9},{25,1},{2,26},{10... | collective-permute-start | bytes 2359304 | tf_op jit(solution)/shard_map/ppermute | solution.py:140
  121.6 38.4 %collective-permute-start.23 = (bf16[384,384]{1,0:T(8,128)(2,1)}, bf16[384,384]{1,0:T(8,128)(2,1)}, u32[]{:S(2)}, u32[]{:S(2)}) collective-permute-start(bf16[384,384]{1,0:T(8,128)(2,1)} %copy-done.34), channel_id=1, source_target_pairs={{0,24},{8,16},{16,8},{24,0},{1,25},{9,17},{17,9},{25,1},{2,26},{10... | collective-permute-start | bytes 884744 | tf_op jit(solution)/shard_map/ppermute | solution.py:140
  160.0 42.1 %collective-permute-start.12 = (bf16[384,1024]{1,0:T(8,128)(2,1)}, bf16[384,1024]{1,0:T(8,128)(2,1)S(1)}, u32[]{:S(2)}, u32[]{:S(2)}) collective-permute-start(bf16[384,1024]{1,0:T(8,128)(2,1)} %get-tuple-element.86), channel_id=1, source_target_pairs={{0,8},{8,0},{16,24},{24,16},{1,9},{9,1},{17,25},{25,17},{2,10},{10... | collective-permute-start | bytes 2359304 | tf_op jit(solution)/shard_map/ppermute | solution.py:140
  163.5 28.1 %collective-permute-start.46 = (bf16[384,512]{1,0:T(8,128)(2,1)}, bf16[384,512]{1,0:T(8,128)(2,1)}, u32[]{:S(2)}, u32[]{:S(2)}) collective-permute-start(bf16[384,512]{1,0:T(8,128)(2,1)} %get-tuple-element.123), channel_id=1, source_target_pairs={{0,4},{2,6},{4,0},{6,2},{1,5},{3,7},{5,1},{7,3},{8,12},{10,14},{12... | collective-permute-start | bytes 1179656 | tf_op jit(solution)/shard_map/ppermute | solution.py:140
  165.8 36.9 %collective-permute-start.13 = (bf16[384,1024]{1,0:T(8,128)(2,1)}, bf16[384,1024]{1,0:T(8,128)(2,1)S(1)}, u32[]{:S(2)}, u32[]{:S(2)}) collective-permute-start(bf16[384,1024]{1,0:T(8,128)(2,1)} %get-tuple-element.87), channel_id=1, source_target_pairs={{0,16},{8,24},{16,0},{24,8},{1,17},{9,25},{17,1},{25,9},{2,18},{10... | collective-permute-start | bytes 2359304 | tf_op jit(solution)/shard_map/ppermute | solution.py:140
  169.0 36.9 %collective-permute-start.14 = (bf16[384,1024]{1,0:T(8,128)(2,1)}, bf16[384,1024]{1,0:T(8,128)(2,1)S(1)}, u32[]{:S(2)}, u32[]{:S(2)}) collective-permute-start(bf16[384,1024]{1,0:T(8,128)(2,1)} %get-tuple-element.88), channel_id=1, source_target_pairs={{0,24},{8,16},{16,8},{24,0},{1,25},{9,17},{17,9},{25,1},{2,26},{10... | collective-permute-start | bytes 2359304 | tf_op jit(solution)/shard_map/ppermute | solution.py:140
  169.1 25.3 %collective-permute-start.47 = (bf16[384,512]{1,0:T(8,128)(2,1)}, bf16[384,512]{1,0:T(8,128)(2,1)}, u32[]{:S(2)}, u32[]{:S(2)}) collective-permute-start(bf16[384,512]{1,0:T(8,128)(2,1)} %get-tuple-element.124), channel_id=1, source_target_pairs={{0,6},{2,4},{4,2},{6,0},{1,7},{3,5},{5,3},{7,1},{8,14},{10,12},{12... | collective-permute-start | bytes 1179656 | tf_op jit(solution)/shard_map/ppermute | solution.py:140
  191.6 35.8 %collective-permute-start.39 = (bf16[384,1024]{1,0:T(8,128)(2,1)}, bf16[384,1024]{1,0:T(8,128)(2,1)S(1)}, u32[]{:S(2)}, u32[]{:S(2)}) collective-permute-start(bf16[384,1024]{1,0:T(8,128)(2,1)} %get-tuple-element.114), channel_id=1, source_target_pairs={{0,2},{2,0},{4,6},{6,4},{1,3},{3,1},{5,7},{7,5},{8,10},{10,8},{12,... | collective-permute-start | bytes 2359304 | tf_op jit(solution)/shard_map/ppermute | solution.py:140
  215.7 57.4 %collective-permute-start.40 = (bf16[384,1024]{1,0:T(8,128)(2,1)}, bf16[384,1024]{1,0:T(8,128)(2,1)}, u32[]{:S(2)}, u32[]{:S(2)}) collective-permute-start(bf16[384,1024]{1,0:T(8,128)(2,1)} %get-tuple-element.115), channel_id=1, source_target_pairs={{0,4},{2,6},{4,0},{6,2},{1,5},{3,7},{5,1},{7,3},{8,12},{10,14},{12... | collective-permute-start | bytes 2359304 | tf_op jit(solution)/shard_map/ppermute | solution.py:140
  219.0 56.3 %collective-permute-start.41 = (bf16[384,1024]{1,0:T(8,128)(2,1)}, bf16[384,1024]{1,0:T(8,128)(2,1)}, u32[]{:S(2)}, u32[]{:S(2)}) collective-permute-start(bf16[384,1024]{1,0:T(8,128)(2,1)} %get-tuple-element.116), channel_id=1, source_target_pairs={{0,6},{2,4},{4,2},{6,0},{1,7},{3,5},{5,3},{7,1},{8,14},{10,12},{12... | collective-permute-start | bytes 2359304 | tf_op jit(solution)/shard_map/ppermute | solution.py:140
  224.5 107.1 %collective-permute-start.15 = (bf16[384,1024]{1,0:T(8,128)(2,1)}, bf16[384,1024]{1,0:T(8,128)(2,1)S(1)}, u32[]{:S(2)}, u32[]{:S(2)}) collective-permute-start(bf16[384,1024]{1,0:T(8,128)(2,1)} %get-tuple-element.90), channel_id=1, source_target_pairs={{0,2},{2,0},{4,6},{6,4},{1,3},{3,1},{5,7},{7,5},{8,10},{10,8},{12,... | collective-permute-start | bytes 2359304 | tf_op jit(solution)/shard_map/ppermute | solution.py:140
  224.5 121.0 %collective-permute-start.16 = (bf16[384,1024]{1,0:T(8,128)(2,1)}, bf16[384,1024]{1,0:T(8,128)(2,1)S(1)}, u32[]{:S(2)}, u32[]{:S(2)}) collective-permute-start(bf16[384,1024]{1,0:T(8,128)(2,1)} %get-tuple-element.91), channel_id=1, source_target_pairs={{0,4},{2,6},{4,0},{6,2},{1,5},{3,7},{5,1},{7,3},{8,12},{10,14},{12... | collective-permute-start | bytes 2359304 | tf_op jit(solution)/shard_map/ppermute | solution.py:140
  227.4 118.2 %collective-permute-start.17 = (bf16[384,1024]{1,0:T(8,128)(2,1)}, bf16[384,1024]{1,0:T(8,128)(2,1)S(1)}, u32[]{:S(2)}, u32[]{:S(2)}) collective-permute-start(bf16[384,1024]{1,0:T(8,128)(2,1)} %get-tuple-element.92), channel_id=1, source_target_pairs={{0,6},{2,4},{4,2},{6,0},{1,7},{3,5},{5,3},{7,1},{8,14},{10,12},{12... | collective-permute-start | bytes 2359304 | tf_op jit(solution)/shard_map/ppermute | solution.py:140
  273.1 90.9 %collective-permute-start.11 = (bf16[384,512]{1,0:T(8,128)(2,1)}, bf16[384,512]{1,0:T(8,128)(2,1)}, u32[]{:S(2)}, u32[]{:S(2)}) collective-permute-start(bf16[384,512]{1,0:T(8,128)(2,1)} %get-tuple-element.84), channel_id=1, source_target_pairs={{0,6},{2,4},{4,2},{6,0},{1,7},{3,5},{5,3},{7,1},{8,14},{10,12},{12... | collective-permute-start | bytes 1179656 | tf_op jit(solution)/shard_map/ppermute | solution.py:140
  275.4 88.6 %collective-permute-start.9 = (bf16[384,512]{1,0:T(8,128)(2,1)}, bf16[384,512]{1,0:T(8,128)(2,1)}, u32[]{:S(2)}, u32[]{:S(2)}) collective-permute-start(bf16[384,512]{1,0:T(8,128)(2,1)} %get-tuple-element.82), channel_id=1, source_target_pairs={{0,2},{2,0},{4,6},{6,4},{1,3},{3,1},{5,7},{7,5},{8,10},{10,8},{12,... | collective-permute-start | bytes 1179656 | tf_op jit(solution)/shard_map/ppermute | solution.py:140
  331.6 34.9 %collective-permute-start.3 = (bf16[384,256]{1,0:T(8,128)(2,1)}, bf16[384,256]{1,0:T(8,128)(2,1)}, u32[]{:S(2)}, u32[]{:S(2)}) collective-permute-start(bf16[384,256]{1,0:T(8,128)(2,1)} %get-tuple-element.74), channel_id=1, source_target_pairs={{0,2},{2,0},{4,6},{6,4},{1,3},{3,1},{5,7},{7,5},{8,10},{10,8},{12,... | collective-permute-start | bytes 589832 | tf_op jit(solution)/shard_map/ppermute | solution.py:140
  345.6 38.0 %collective-permute-start.4 = (bf16[384,256]{1,0:T(8,128)(2,1)}, bf16[384,256]{1,0:T(8,128)(2,1)}, u32[]{:S(2)}, u32[]{:S(2)}) collective-permute-start(bf16[384,256]{1,0:T(8,128)(2,1)} %get-tuple-element.75), channel_id=1, source_target_pairs={{0,4},{2,6},{4,0},{6,2},{1,5},{3,7},{5,1},{7,3},{8,12},{10,14},{12... | collective-permute-start | bytes 589832 | tf_op jit(solution)/shard_map/ppermute | solution.py:140
  345.6 38.0 %collective-permute-start.5 = (bf16[384,256]{1,0:T(8,128)(2,1)}, bf16[384,256]{1,0:T(8,128)(2,1)}, u32[]{:S(2)}, u32[]{:S(2)}) collective-permute-start(bf16[384,256]{1,0:T(8,128)(2,1)} %get-tuple-element.76), channel_id=1, source_target_pairs={{0,6},{2,4},{4,2},{6,0},{1,7},{3,5},{5,3},{7,1},{8,14},{10,12},{12... | collective-permute-start | bytes 589832 | tf_op jit(solution)/shard_map/ppermute | solution.py:140
  (69 other events, 1509.3 us)

commit v4 on v3

--- a/solution.py
+++ b/solution.py
@@ -14,6 +14,7 @@
 )
 ANY = pl.BlockSpec(memory_space=pl.ANY)
 SCALARS = pl.BlockSpec(memory_space=pltpu.SMEM)
+PARAMS = pltpu.CompilerParams(vmem_limit_bytes=8 << 20)
 WHOLE = pl.BlockSpec(memory_space=pltpu.VMEM)
 
 
@@ -56,6 +57,10 @@
     return range(count - 1, 0, -1) if axis == "tp" else range(1, count)
 
 
+def in_vmem(pieces):
+    return [pltpu.with_memory_space_constraint(piece, pltpu.VMEM) for piece in pieces]
+
+
 def pick_rows(weight, owned, sizes, first, offset, width):
     count = sizes[1]
     tile = tile_of(offset, width)
@@ -66,18 +71,20 @@
         outs, turned = refs[:-1], refs[-1]
         me, mine, replica = position()
         turned[...] = weight_ref[...].T
+        columns = pl.ds(pl.multiple_of(pl.program_id(0) * tile, 128), tile)
         for step, out in enumerate(outs):
             owners = [(line, mine ^ step) if first else (me ^ step, line) for line in range(count)]
             span = sum(span_of(owned_ref, me, row, column, replica, sizes) for row, column in owners)
-            out[...] = turned[pl.ds(pl.multiple_of(span * block_rows, 16), block_rows), :]
+            out[:, columns] = turned[pl.ds(pl.multiple_of(span * block_rows, 16), block_rows), :]
 
     return pl.pallas_call(
         kernel,
         grid=(width // tile,),
         in_specs=[SCALARS, pl.BlockSpec((tile, rows), lambda step: (offset // tile + step, 0))],
-        out_specs=[pl.BlockSpec((block_rows, tile), lambda step: (0, step))] * count,
-        out_shape=[jax.ShapeDtypeStruct((block_rows, width), weight.dtype)] * count,
+        out_specs=[WHOLE] * count,
+        out_shape=[pltpu.VMEM((block_rows, width), weight.dtype)] * count,
         scratch_shapes=[pltpu.VMEM((rows, tile), weight.dtype)],
+        compiler_params=PARAMS,
         name="pick_rows",
     )(owned, weight)
 
@@ -100,9 +107,10 @@
         kernel,
         in_specs=[SCALARS] + [WHOLE] * count,
         out_specs=[WHOLE] * count,
-        out_shape=[jax.ShapeDtypeStruct(piece.shape, piece.dtype) for piece in pieces],
+        out_shape=[pltpu.VMEM(piece.shape, piece.dtype) for piece in pieces],
+        compiler_params=PARAMS,
         name="choose",
-    )(owned, *pieces)
+    )(owned, *in_vmem(pieces))
 
 
 def place(saved, pieces, owned, sizes, first, offset, hidden):
@@ -129,8 +137,9 @@
         out_shape=jax.ShapeDtypeStruct((block_rows, count * hidden), pieces[0].dtype),
         scratch_shapes=[pltpu.SemaphoreType.DMA((count,))],
         input_output_aliases={count + 1: 0} if saved else {},
+        compiler_params=PARAMS,
         name="place",
-    )(owned, *pieces, *saved)
+    )(owned, *in_vmem(pieces), *saved)
 
 
 def exchange(pieces, axis):
@@ -142,9 +151,9 @@
 
 
 def local(down_weight, owned_span):
-    weight = down_weight[0]
+    weight = pltpu.with_memory_space_constraint(down_weight[0], pltpu.HBM)
     hidden = weight.shape[0]
-    owned = jnp.transpose(owned_span, (0, 2, 1))
+    owned = pltpu.with_memory_space_constraint(jnp.transpose(owned_span, (0, 2, 1)), pltpu.HBM)
     sizes = tuple(lax.axis_size(name) for name in ("ep", "tp", "dp"))
     chunks = spread(hidden)
 

time: 391 us -> 383 us (0.980); the launches traced: 386 us -> 382 us
  waiting for transfers between devices: 174 us -> 203 us
  Pallas kernels: 67.6 us -> 39.9 us
  starting transfers between devices: 143 us -> 139 us
    ppermute x54, waiting for transfers between devices: 174 us -> 203 us  [exchange(): lax.ppermute(pieces[step], axis, [(index, index ^ step) for index in rang...]
    pallas_call x8, Pallas kernels: 22.3 us -> 7.47 us  [choose(): pl.pallas_call(kernel, in_specs=[SCALARS] + [WHOLE] * count, out_specs=[W...]
    pallas_call x8, Pallas kernels: 24.7 us -> 17.1 us  [pick_rows(): pl.pallas_call(kernel, grid=(width // tile,), in_specs=[SCALARS, pl.Block...]
    pallas_call x8, Pallas kernels: 20.6 us -> 15.2 us  [place(): pl.pallas_call(kernel, in_specs=[SCALARS] + [WHOLE] * count + [ANY] * len...]
    ppermute x54, starting transfers between devices: 143 us -> 139 us  [exchange(): lax.ppermute(pieces[step], axis, [(index, index ^ step) for index in rang...]
  transfers between devices with their start and end apart: 54 -> 54, of which waited for: 14 -> 17; matrix products, arithmetic and copies ran while one was open for 0% -> 0% of each run, Pallas kernels for 16% -> 10%
where the time goes in v4:
time: 383 us; the launch traced here: 382 us
  waiting for transfers between devices  203 us (53%)
  starting transfers between devices  139 us (36%)
  Pallas kernels  39.9 us (10%)
    ppermute x54, waiting for transfers between devices, exchange(): lax.ppermute(pieces[step], axis, [(index, index ^ step) for index in rang...  203 us
    ppermute x54, starting transfers between devices, exchange(): lax.ppermute(pieces[step], axis, [(index, index ^ step) for index in rang...  139 us
    pallas_call x8, Pallas kernels, pick_rows(): pl.pallas_call(kernel, grid=(width // tile,), in_specs=[SCALARS, pl.Block...  17.1 us
    pallas_call x8, Pallas kernels, place(): pl.pallas_call(kernel, in_specs=[SCALARS] + [WHOLE] * count + [ANY] * len...  15.2 us
  transfers between devices with their start and end apart: 54, of which 17 were waited for; matrix products, arithmetic and copies ran while one was open for 0% of the time, Pallas kernels for 10%

profile of v4, /device:TPU:0, one launch (start us, length us, event | category | flops | bytes accessed | tf_op | source)
XLA Modules:
  0.0 381.7 jit_solution(3977929239651888153)
XLA Ops:
  1.2 3.1 collective-permute-start.27
  13.4 5.3 %collective-permute-done.29 = bf16[384,128]{1,0:T(8,128)(2,1)S(1)} collective-permute-done((bf16[384,128]{1,0:T(8,128)(2,1)S(1)}, bf16[384,128]{1,0:T(8,128)(2,1)S(1)}, u32[]{:S(2)}, u32[]{:S(2)}) %collective-permute-start.29) | collective-permute-done | bytes 98336 | tf_op jit(solution)/shard_map/ppermute | solution.py:149
  32.1 3.3 collective-permute-start.18
  46.4 3.2 collective-permute-done.35.refs_3_
  52.5 3.9 %collective-permute-done.20 = bf16[384,384]{1,0:T(8,128)(2,1)S(1)} collective-permute-done((bf16[384,384]{1,0:T(8,128)(2,1)S(1)}, bf16[384,384]{1,0:T(8,128)(2,1)S(1)}, u32[]{:S(2)}, u32[]{:S(2)}) %collective-permute-start.20) | collective-permute-done | bytes 294944 | tf_op jit(solution)/shard_map/ppermute | solution.py:149
  56.4 5.0 %collective-permute-start.53 = (bf16[384,256]{1,0:T(8,128)(2,1)S(1)}, bf16[384,256]{1,0:T(8,128)(2,1)S(1)}, u32[]{:S(2)}, u32[]{:S(2)}) collective-permute-start(bf16[384,256]{1,0:T(8,128)(2,1)S(1)} %get-tuple-element.132), channel_id=1, source_target_pairs={{0,6},{2,4},{4,2},{6,0},{1,7},{3,5},{5,3},{7,1},{8,14},{10,12},{12... | collective-permute-start | bytes 589832 | tf_op jit(solution)/shard_map/ppermute | solution.py:149
  64.2 12.4 %collective-permute-done.52.refs_2_ = bf16[384,256]{1,0:T(8,128)(2,1)S(1)} collective-permute-done((bf16[384,256]{1,0:T(8,128)(2,1)S(1)}, bf16[384,256]{1,0:T(8,128)(2,1)S(1)}, u32[]{:S(2)}, u32[]{:S(2)}) %collective-permute-start.52) | collective-permute-done | bytes 196640 | tf_op jit(solution)/shard_map/ppermute | solution.py:149
  80.2 3.5 pick_rows.13
  90.0 9.2 %collective-permute-done.7.refs_2_ = bf16[384,512]{1,0:T(8,128)(2,1)S(1)} collective-permute-done((bf16[384,512]{1,0:T(8,128)(2,1)S(1)}, bf16[384,512]{1,0:T(8,128)(2,1)S(1)}, u32[]{:S(2)}, u32[]{:S(2)}) %collective-permute-start.7) | collective-permute-done | bytes 393248 | tf_op jit(solution)/shard_map/ppermute | solution.py:149
  100.1 20.2 %collective-permute-done.19.refs_1_ = bf16[384,384]{1,0:T(8,128)(2,1)S(1)} collective-permute-done((bf16[384,384]{1,0:T(8,128)(2,1)S(1)}, bf16[384,384]{1,0:T(8,128)(2,1)S(1)}, u32[]{:S(2)}, u32[]{:S(2)}) %collective-permute-start.19) | collective-permute-done | bytes 294944 | tf_op jit(solution)/shard_map/ppermute | solution.py:149
  122.0 21.7 %collective-permute-done.21.refs_2_ = bf16[384,384]{1,0:T(8,128)(2,1)S(1)} collective-permute-done((bf16[384,384]{1,0:T(8,128)(2,1)S(1)}, bf16[384,384]{1,0:T(8,128)(2,1)S(1)}, u32[]{:S(2)}, u32[]{:S(2)}) %collective-permute-start.21) | collective-permute-done | bytes 294944 | tf_op jit(solution)/shard_map/ppermute | solution.py:149
  143.7 8.2 %collective-permute-start.45 = (bf16[384,512]{1,0:T(8,128)(2,1)S(1)}, bf16[384,512]{1,0:T(8,128)(2,1)S(1)}, u32[]{:S(2)}, u32[]{:S(2)}) collective-permute-start(bf16[384,512]{1,0:T(8,128)(2,1)S(1)} %get-tuple-element.122), channel_id=1, source_target_pairs={{0,2},{2,0},{4,6},{6,4},{1,3},{3,1},{5,7},{7,5},{8,10},{10,8},{12,... | collective-permute-start | bytes 1179656 | tf_op jit(solution)/shard_map/ppermute | solution.py:149
  151.9 3.5 pick_rows.10
  155.5 4.0 %collective-permute-done.45.refs_1_ = bf16[384,512]{1,0:T(8,128)(2,1)S(1)} collective-permute-done((bf16[384,512]{1,0:T(8,128)(2,1)S(1)}, bf16[384,512]{1,0:T(8,128)(2,1)S(1)}, u32[]{:S(2)}, u32[]{:S(2)}) %collective-permute-start.45) | collective-permute-done | bytes 393248 | tf_op jit(solution)/shard_map/ppermute | solution.py:149
  159.4 4.7 %collective-permute-start.46 = (bf16[384,512]{1,0:T(8,128)(2,1)S(1)}, bf16[384,512]{1,0:T(8,128)(2,1)S(1)}, u32[]{:S(2)}, u32[]{:S(2)}) collective-permute-start(bf16[384,512]{1,0:T(8,128)(2,1)S(1)} %get-tuple-element.123), channel_id=1, source_target_pairs={{0,4},{2,6},{4,0},{6,2},{1,5},{3,7},{5,1},{7,3},{8,12},{10,14},{12... | collective-permute-start | bytes 1179656 | tf_op jit(solution)/shard_map/ppermute | solution.py:149
  166.3 21.6 %collective-permute-done.46.refs_2_ = bf16[384,512]{1,0:T(8,128)(2,1)S(1)} collective-permute-done((bf16[384,512]{1,0:T(8,128)(2,1)S(1)}, bf16[384,512]{1,0:T(8,128)(2,1)S(1)}, u32[]{:S(2)}, u32[]{:S(2)}) %collective-permute-start.46) | collective-permute-done | bytes 393248 | tf_op jit(solution)/shard_map/ppermute | solution.py:149
  188.9 8.0 %collective-permute-start.10 = (bf16[384,512]{1,0:T(8,128)(2,1)S(1)}, bf16[384,512]{1,0:T(8,128)(2,1)S(1)}, u32[]{:S(2)}, u32[]{:S(2)}) collective-permute-start(bf16[384,512]{1,0:T(8,128)(2,1)S(1)} %get-tuple-element.83), channel_id=1, source_target_pairs={{0,4},{2,6},{4,0},{6,2},{1,5},{3,7},{5,1},{7,3},{8,12},{10,14},{12... | collective-permute-start | bytes 1179656 | tf_op jit(solution)/shard_map/ppermute | solution.py:149
  201.4 9.8 %collective-permute-done.10.refs_2_ = bf16[384,512]{1,0:T(8,128)(2,1)S(1)} collective-permute-done((bf16[384,512]{1,0:T(8,128)(2,1)S(1)}, bf16[384,512]{1,0:T(8,128)(2,1)S(1)}, u32[]{:S(2)}, u32[]{:S(2)}) %collective-permute-start.10) | collective-permute-done | bytes 393248 | tf_op jit(solution)/shard_map/ppermute | solution.py:149
  211.2 3.4 collective-permute-start.40
  214.6 3.0 collective-permute-start.41
  223.1 46.7 %collective-permute-done.40.refs_2_ = bf16[384,1024]{1,0:T(8,128)(2,1)S(1)} collective-permute-done((bf16[384,1024]{1,0:T(8,128)(2,1)S(1)}, bf16[384,1024]{1,0:T(8,128)(2,1)S(1)}, u32[]{:S(2)}, u32[]{:S(2)}) %collective-permute-start.40) | collective-permute-done | bytes 786464 | tf_op jit(solution)/shard_map/ppermute | solution.py:149
  270.6 55.2 %collective-permute-start.9 = (bf16[384,512]{1,0:T(8,128)(2,1)S(1)}, bf16[384,512]{1,0:T(8,128)(2,1)S(1)}, u32[]{:S(2)}, u32[]{:S(2)}) collective-permute-start(bf16[384,512]{1,0:T(8,128)(2,1)S(1)} %get-tuple-element.82), channel_id=1, source_target_pairs={{0,2},{2,0},{4,6},{6,4},{1,3},{3,1},{5,7},{7,5},{8,10},{10,8},{12,... | collective-permute-start | bytes 1179656 | tf_op jit(solution)/shard_map/ppermute | solution.py:149
  326.8 15.4 %collective-permute-done.16.refs_2_ = bf16[384,1024]{1,0:T(8,128)(2,1)S(1)} collective-permute-done((bf16[384,1024]{1,0:T(8,128)(2,1)S(1)}, bf16[384,1024]{1,0:T(8,128)(2,1)S(1)}, u32[]{:S(2)}, u32[]{:S(2)}) %collective-permute-start.16) | collective-permute-done | bytes 786464 | tf_op jit(solution)/shard_map/ppermute | solution.py:149
  357.5 22.6 %collective-permute-done.4.refs_2_ = bf16[384,256]{1,0:T(8,128)(2,1)S(1)} collective-permute-done((bf16[384,256]{1,0:T(8,128)(2,1)S(1)}, bf16[384,256]{1,0:T(8,128)(2,1)S(1)}, u32[]{:S(2)}, u32[]{:S(2)}) %collective-permute-start.4) | collective-permute-done | bytes 196640 | tf_op jit(solution)/shard_map/ppermute | solution.py:149
  (108 shorter events, 84.6 us)
Async XLA Ops:
  44.8 33.2 %collective-permute-start.42 = (bf16[384,512]{1,0:T(8,128)(2,1)S(1)}, bf16[384,512]{1,0:T(8,128)(2,1)S(1)}, u32[]{:S(2)}, u32[]{:S(2)}) collective-permute-start(bf16[384,512]{1,0:T(8,128)(2,1)S(1)} %get-tuple-element.118), channel_id=1, source_target_pairs={{0,8},{8,0},{16,24},{24,16},{1,9},{9,1},{17,25},{25,17},{2,10},{10... | collective-permute-start | bytes 1179656 | tf_op jit(solution)/shard_map/ppermute | solution.py:149
  51.5 25.1 %collective-permute-start.52 = (bf16[384,256]{1,0:T(8,128)(2,1)S(1)}, bf16[384,256]{1,0:T(8,128)(2,1)S(1)}, u32[]{:S(2)}, u32[]{:S(2)}) collective-permute-start(bf16[384,256]{1,0:T(8,128)(2,1)S(1)} %get-tuple-element.131), channel_id=1, source_target_pairs={{0,4},{2,6},{4,0},{6,2},{1,5},{3,7},{5,1},{7,3},{8,12},{10,14},{12... | collective-permute-start | bytes 589832 | tf_op jit(solution)/shard_map/ppermute | solution.py:149
  85.7 78.4 %collective-permute-start.36 = (bf16[384,1024]{1,0:T(8,128)(2,1)S(1)}, bf16[384,1024]{1,0:T(8,128)(2,1)S(1)}, u32[]{:S(2)}, u32[]{:S(2)}) collective-permute-start(bf16[384,1024]{1,0:T(8,128)(2,1)S(1)} %get-tuple-element.110), channel_id=1, source_target_pairs={{0,8},{8,0},{16,24},{24,16},{1,9},{9,1},{17,25},{25,17},{2,10},{10... | collective-permute-start | bytes 2359304 | tf_op jit(solution)/shard_map/ppermute | solution.py:149
  85.7 34.6 %collective-permute-start.19 = (bf16[384,384]{1,0:T(8,128)(2,1)S(1)}, bf16[384,384]{1,0:T(8,128)(2,1)S(1)}, u32[]{:S(2)}, u32[]{:S(2)}) collective-permute-start(bf16[384,384]{1,0:T(8,128)(2,1)S(1)} %collective-permute-done.18), channel_id=1, source_target_pairs={{0,8},{8,0},{16,24},{24,16},{1,9},{9,1},{17,25},{25,17},{2,10},{10... | collective-permute-start | bytes 884744 | tf_op jit(solution)/shard_map/ppermute | solution.py:149
  88.6 76.6 %collective-permute-start.37 = (bf16[384,1024]{1,0:T(8,128)(2,1)S(1)}, bf16[384,1024]{1,0:T(8,128)(2,1)S(1)}, u32[]{:S(2)}, u32[]{:S(2)}) collective-permute-start(bf16[384,1024]{1,0:T(8,128)(2,1)S(1)} %get-tuple-element.111), channel_id=1, source_target_pairs={{0,16},{8,24},{16,0},{24,8},{1,17},{9,25},{17,1},{25,9},{2,18},{10... | collective-permute-start | bytes 2359304 | tf_op jit(solution)/shard_map/ppermute | solution.py:149
  99.2 44.5 %collective-permute-start.21 = (bf16[384,384]{1,0:T(8,128)(2,1)S(1)}, bf16[384,384]{1,0:T(8,128)(2,1)S(1)}, u32[]{:S(2)}, u32[]{:S(2)}) collective-permute-start(bf16[384,384]{1,0:T(8,128)(2,1)S(1)} %collective-permute-done.20), channel_id=1, source_target_pairs={{0,16},{8,24},{16,0},{24,8},{1,17},{9,25},{17,1},{25,9},{2,18},{10... | collective-permute-start | bytes 884744 | tf_op jit(solution)/shard_map/ppermute | solution.py:149
  100.1 65.1 %collective-permute-start.38 = (bf16[384,1024]{1,0:T(8,128)(2,1)S(1)}, bf16[384,1024]{1,0:T(8,128)(2,1)S(1)}, u32[]{:S(2)}, u32[]{:S(2)}) collective-permute-start(bf16[384,1024]{1,0:T(8,128)(2,1)S(1)} %get-tuple-element.112), channel_id=1, source_target_pairs={{0,24},{8,16},{16,8},{24,0},{1,25},{9,17},{17,9},{25,1},{2,26},{10... | collective-permute-start | bytes 2359304 | tf_op jit(solution)/shard_map/ppermute | solution.py:149
  120.2 35.1 %collective-permute-start.23 = (bf16[384,384]{1,0:T(8,128)(2,1)S(1)}, bf16[384,384]{1,0:T(8,128)(2,1)S(1)}, u32[]{:S(2)}, u32[]{:S(2)}) collective-permute-start(bf16[384,384]{1,0:T(8,128)(2,1)S(1)} %collective-permute-done.22), channel_id=1, source_target_pairs={{0,24},{8,16},{16,8},{24,0},{1,25},{9,17},{17,9},{25,1},{2,26},{10... | collective-permute-start | bytes 884744 | tf_op jit(solution)/shard_map/ppermute | solution.py:149
  155.4 42.4 %collective-permute-start.12 = (bf16[384,1024]{1,0:T(8,128)(2,1)S(1)}, bf16[384,1024]{1,0:T(8,128)(2,1)S(1)}, u32[]{:S(2)}, u32[]{:S(2)}) collective-permute-start(bf16[384,1024]{1,0:T(8,128)(2,1)S(1)} %get-tuple-element.86), channel_id=1, source_target_pairs={{0,8},{8,0},{16,24},{24,16},{1,9},{9,1},{17,25},{25,17},{2,10},{10... | collective-permute-start | bytes 2359304 | tf_op jit(solution)/shard_map/ppermute | solution.py:149
  159.4 28.5 %collective-permute-start.46 = (bf16[384,512]{1,0:T(8,128)(2,1)S(1)}, bf16[384,512]{1,0:T(8,128)(2,1)S(1)}, u32[]{:S(2)}, u32[]{:S(2)}) collective-permute-start(bf16[384,512]{1,0:T(8,128)(2,1)S(1)} %get-tuple-element.123), channel_id=1, source_target_pairs={{0,4},{2,6},{4,0},{6,2},{1,5},{3,7},{5,1},{7,3},{8,12},{10,14},{12... | collective-permute-start | bytes 1179656 | tf_op jit(solution)/shard_map/ppermute | solution.py:149
  164.1 33.8 %collective-permute-start.13 = (bf16[384,1024]{1,0:T(8,128)(2,1)S(1)}, bf16[384,1024]{1,0:T(8,128)(2,1)S(1)}, u32[]{:S(2)}, u32[]{:S(2)}) collective-permute-start(bf16[384,1024]{1,0:T(8,128)(2,1)S(1)} %get-tuple-element.87), channel_id=1, source_target_pairs={{0,16},{8,24},{16,0},{24,8},{1,17},{9,25},{17,1},{25,9},{2,18},{10... | collective-permute-start | bytes 2359304 | tf_op jit(solution)/shard_map/ppermute | solution.py:149
  165.2 34.2 %collective-permute-start.14 = (bf16[384,1024]{1,0:T(8,128)(2,1)S(1)}, bf16[384,1024]{1,0:T(8,128)(2,1)S(1)}, u32[]{:S(2)}, u32[]{:S(2)}) collective-permute-start(bf16[384,1024]{1,0:T(8,128)(2,1)S(1)} %get-tuple-element.88), channel_id=1, source_target_pairs={{0,24},{8,16},{16,8},{24,0},{1,25},{9,17},{17,9},{25,1},{2,26},{10... | collective-permute-start | bytes 2359304 | tf_op jit(solution)/shard_map/ppermute | solution.py:149
  165.2 23.6 %collective-permute-start.47 = (bf16[384,512]{1,0:T(8,128)(2,1)S(1)}, bf16[384,512]{1,0:T(8,128)(2,1)S(1)}, u32[]{:S(2)}, u32[]{:S(2)}) collective-permute-start(bf16[384,512]{1,0:T(8,128)(2,1)S(1)} %get-tuple-element.124), channel_id=1, source_target_pairs={{0,6},{2,4},{4,2},{6,0},{1,7},{3,5},{5,3},{7,1},{8,14},{10,12},{12... | collective-permute-start | bytes 1179656 | tf_op jit(solution)/shard_map/ppermute | solution.py:149
  187.9 32.2 %collective-permute-start.39 = (bf16[384,1024]{1,0:T(8,128)(2,1)S(1)}, bf16[384,1024]{1,0:T(8,128)(2,1)S(1)}, u32[]{:S(2)}, u32[]{:S(2)}) collective-permute-start(bf16[384,1024]{1,0:T(8,128)(2,1)S(1)} %get-tuple-element.114), channel_id=1, source_target_pairs={{0,2},{2,0},{4,6},{6,4},{1,3},{3,1},{5,7},{7,5},{8,10},{10,8},{12,... | collective-permute-start | bytes 2359304 | tf_op jit(solution)/shard_map/ppermute | solution.py:149
  211.2 58.6 %collective-permute-start.40 = (bf16[384,1024]{1,0:T(8,128)(2,1)S(1)}, bf16[384,1024]{1,0:T(8,128)(2,1)S(1)}, u32[]{:S(2)}, u32[]{:S(2)}) collective-permute-start(bf16[384,1024]{1,0:T(8,128)(2,1)S(1)} %get-tuple-element.115), channel_id=1, source_target_pairs={{0,4},{2,6},{4,0},{6,2},{1,5},{3,7},{5,1},{7,3},{8,12},{10,14},{12... | collective-permute-start | bytes 2359304 | tf_op jit(solution)/shard_map/ppermute | solution.py:149
  214.6 56.0 %collective-permute-start.41 = (bf16[384,1024]{1,0:T(8,128)(2,1)S(1)}, bf16[384,1024]{1,0:T(8,128)(2,1)S(1)}, u32[]{:S(2)}, u32[]{:S(2)}) collective-permute-start(bf16[384,1024]{1,0:T(8,128)(2,1)S(1)} %get-tuple-element.116), channel_id=1, source_target_pairs={{0,6},{2,4},{4,2},{6,0},{1,7},{3,5},{5,3},{7,1},{8,14},{10,12},{12... | collective-permute-start | bytes 2359304 | tf_op jit(solution)/shard_map/ppermute | solution.py:149
  218.6 108.1 %collective-permute-start.15 = (bf16[384,1024]{1,0:T(8,128)(2,1)S(1)}, bf16[384,1024]{1,0:T(8,128)(2,1)S(1)}, u32[]{:S(2)}, u32[]{:S(2)}) collective-permute-start(bf16[384,1024]{1,0:T(8,128)(2,1)S(1)} %get-tuple-element.90), channel_id=1, source_target_pairs={{0,2},{2,0},{4,6},{6,4},{1,3},{3,1},{5,7},{7,5},{8,10},{10,8},{12,... | collective-permute-start | bytes 2359304 | tf_op jit(solution)/shard_map/ppermute | solution.py:149
  218.7 123.5 %collective-permute-start.16 = (bf16[384,1024]{1,0:T(8,128)(2,1)S(1)}, bf16[384,1024]{1,0:T(8,128)(2,1)S(1)}, u32[]{:S(2)}, u32[]{:S(2)}) collective-permute-start(bf16[384,1024]{1,0:T(8,128)(2,1)S(1)} %get-tuple-element.91), channel_id=1, source_target_pairs={{0,4},{2,6},{4,0},{6,2},{1,5},{3,7},{5,1},{7,3},{8,12},{10,14},{12... | collective-permute-start | bytes 2359304 | tf_op jit(solution)/shard_map/ppermute | solution.py:149
  220.1 122.1 %collective-permute-start.17 = (bf16[384,1024]{1,0:T(8,128)(2,1)S(1)}, bf16[384,1024]{1,0:T(8,128)(2,1)S(1)}, u32[]{:S(2)}, u32[]{:S(2)}) collective-permute-start(bf16[384,1024]{1,0:T(8,128)(2,1)S(1)} %get-tuple-element.92), channel_id=1, source_target_pairs={{0,6},{2,4},{4,2},{6,0},{1,7},{3,5},{5,3},{7,1},{8,14},{10,12},{12... | collective-permute-start | bytes 2359304 | tf_op jit(solution)/shard_map/ppermute | solution.py:149
  269.8 84.5 %collective-permute-start.11 = (bf16[384,512]{1,0:T(8,128)(2,1)S(1)}, bf16[384,512]{1,0:T(8,128)(2,1)S(1)}, u32[]{:S(2)}, u32[]{:S(2)}) collective-permute-start(bf16[384,512]{1,0:T(8,128)(2,1)S(1)} %get-tuple-element.84), channel_id=1, source_target_pairs={{0,6},{2,4},{4,2},{6,0},{1,7},{3,5},{5,3},{7,1},{8,14},{10,12},{12... | collective-permute-start | bytes 1179656 | tf_op jit(solution)/shard_map/ppermute | solution.py:149
  270.6 83.7 %collective-permute-start.9 = (bf16[384,512]{1,0:T(8,128)(2,1)S(1)}, bf16[384,512]{1,0:T(8,128)(2,1)S(1)}, u32[]{:S(2)}, u32[]{:S(2)}) collective-permute-start(bf16[384,512]{1,0:T(8,128)(2,1)S(1)} %get-tuple-element.82), channel_id=1, source_target_pairs={{0,2},{2,0},{4,6},{6,4},{1,3},{3,1},{5,7},{7,5},{8,10},{10,8},{12,... | collective-permute-start | bytes 1179656 | tf_op jit(solution)/shard_map/ppermute | solution.py:149
  326.7 30.7 %collective-permute-start.3 = (bf16[384,256]{1,0:T(8,128)(2,1)S(1)}, bf16[384,256]{1,0:T(8,128)(2,1)S(1)}, u32[]{:S(2)}, u32[]{:S(2)}) collective-permute-start(bf16[384,256]{1,0:T(8,128)(2,1)S(1)} %get-tuple-element.74), channel_id=1, source_target_pairs={{0,2},{2,0},{4,6},{6,4},{1,3},{3,1},{5,7},{7,5},{8,10},{10,8},{12,... | collective-permute-start | bytes 589832 | tf_op jit(solution)/shard_map/ppermute | solution.py:149
  342.2 37.9 %collective-permute-start.4 = (bf16[384,256]{1,0:T(8,128)(2,1)S(1)}, bf16[384,256]{1,0:T(8,128)(2,1)S(1)}, u32[]{:S(2)}, u32[]{:S(2)}) collective-permute-start(bf16[384,256]{1,0:T(8,128)(2,1)S(1)} %get-tuple-element.75), channel_id=1, source_target_pairs={{0,4},{2,6},{4,0},{6,2},{1,5},{3,7},{5,1},{7,3},{8,12},{10,14},{12... | collective-permute-start | bytes 589832 | tf_op jit(solution)/shard_map/ppermute | solution.py:149
  342.2 37.9 %collective-permute-start.5 = (bf16[384,256]{1,0:T(8,128)(2,1)S(1)}, bf16[384,256]{1,0:T(8,128)(2,1)S(1)}, u32[]{:S(2)}, u32[]{:S(2)}) collective-permute-start(bf16[384,256]{1,0:T(8,128)(2,1)S(1)} %get-tuple-element.76), channel_id=1, source_target_pairs={{0,6},{2,4},{4,2},{6,0},{1,7},{3,5},{5,3},{7,1},{8,14},{10,12},{12... | collective-permute-start | bytes 589832 | tf_op jit(solution)/shard_map/ppermute | solution.py:149
  (30 other events, 463.4 us)

commit v5 on v4

--- a/solution.py
+++ b/solution.py
@@ -39,10 +39,10 @@
     total = sum(SHARES.values())
     columns = hidden // 128
     edges, done = [0], 0
-    for share in SHARES.values():
+    for left, share in zip(reversed(range(len(SHARES))), SHARES.values()):
         done += share
-        edges.append(-(-done * columns // total) * 128)
-    return {chunk: (low, high - low) for chunk, low, high in zip(SHARES, edges, edges[1:])}
+        edges.append(max(edges[-1] + 1, min(done * columns // total, columns - left)))
+    return {chunk: (low * 128, (high - low) * 128) for chunk, low, high in zip(SHARES, edges, edges[1:])}
 
 
 def axis_of(stage, chunk):
@@ -53,8 +53,23 @@
     return "ep" if stage == "H" else None
 
 
-def steps_of(axis, count):
-    return range(count - 1, 0, -1) if axis == "tp" else range(1, count)
+def steps_of(axis, count, chunk):
+    steps = list(range(1, count))
+    if axis == "tp" and chunk != ORDER[-1][1]:
+        steps.insert(0, steps.pop(count // 2 - 1))
+    return steps
+
+
+def partner_of(axis, index, step, count):
+    if axis == "ep":
+        return index ^ abs(step)
+    rank = index
+    shift = 1
+    while shift < count:
+        rank = rank ^ (rank >> shift)
+        shift *= 2
+    rank = (rank + step) & (count - 1)
+    return rank ^ (rank >> 1)
 
 
 def in_vmem(pieces):
@@ -73,7 +88,8 @@
         turned[...] = weight_ref[...].T
         columns = pl.ds(pl.multiple_of(pl.program_id(0) * tile, 128), tile)
         for step, out in enumerate(outs):
-            owners = [(line, mine ^ step) if first else (me ^ step, line) for line in range(count)]
+            row, column = me ^ step, partner_of("tp", mine, step, count)
+            owners = [(line, column) if first else (row, line) for line in range(count)]
             span = sum(span_of(owned_ref, me, row, column, replica, sizes) for row, column in owners)
             out[:, columns] = turned[pl.ds(pl.multiple_of(span * block_rows, 16), block_rows), :]
 
@@ -96,7 +112,7 @@
         ins, outs = refs[:count], refs[count:]
         me, mine, replica = position()
         for step in range(count):
-            row, column = (me ^ step, mine) if first else (me, mine ^ step)
+            row, column = (me ^ step, mine) if first else (me, partner_of("tp", mine, step, count))
             pick = expert_of(owned_ref, row, column, replica, sizes) ^ me
             for source in range(count):
                 @pl.when(pick == source)
@@ -117,13 +133,18 @@
     count = len(pieces)
     block_rows, width = pieces[0].shape
 
-    def kernel(owned_ref, *refs):
-        ins, out, sems = refs[:count], refs[-2], refs[-1]
+    table = [owned] if first else []
+
+    def kernel(*refs):
+        ins, out, sems = refs[len(table):len(table) + count], refs[-2], refs[-1]
         me, mine, replica = position()
-        turn = mine ^ me ^ expert_of(owned_ref, me, mine, replica, sizes) if first else mine
         copies = []
         for step in range(count):
-            start = pl.multiple_of((turn ^ step) * hidden + offset, 128)
+            crossed = step
+            if first:
+                crossed = me ^ step ^ expert_of(refs[0], me, mine, replica, sizes)
+            origin = partner_of("tp", mine, -crossed, count)
+            start = pl.multiple_of(origin * hidden + offset, 128)
             copies.append(pltpu.make_async_copy(ins[step], out.at[:, pl.ds(start, width)], sems.at[step]))
         for copy in copies:
             copy.start()
@@ -132,21 +153,22 @@
 
     return pl.pallas_call(
         kernel,
-        in_specs=[SCALARS] + [WHOLE] * count + [ANY] * len(saved),
+        in_specs=[SCALARS] * len(table) + [WHOLE] * count + [ANY] * len(saved),
         out_specs=ANY,
         out_shape=jax.ShapeDtypeStruct((block_rows, count * hidden), pieces[0].dtype),
         scratch_shapes=[pltpu.SemaphoreType.DMA((count,))],
-        input_output_aliases={count + 1: 0} if saved else {},
+        input_output_aliases={len(table) + count: 0} if saved else {},
         compiler_params=PARAMS,
         name="place",
-    )(owned, *in_vmem(pieces), *saved)
-
-
-def exchange(pieces, axis):
+    )(*table, *in_vmem(pieces), *saved)
+
+
+def exchange(pieces, axis, chunk):
     count = len(pieces)
     moved = {0: pieces[0]}
-    for step in steps_of(axis, count):
-        moved[step] = lax.ppermute(pieces[step], axis, [(index, index ^ step) for index in range(count)])
+    for step in steps_of(axis, count, chunk):
+        pairs = [(index, partner_of(axis, index, step, count)) for index in range(count)]
+        moved[step] = lax.ppermute(pieces[step], axis, pairs)
     return [moved[step] for step in range(count)]
 
 
@@ -171,7 +193,7 @@
         else:
             saved = [place(saved, moved[chunk], owned, sizes, first, offset, hidden)]
             continue
-        moved[chunk] = exchange(sent, axis_of(stage, chunk))
+        moved[chunk] = exchange(sent, axis_of(stage, chunk), chunk)
     return saved[0][None, None]
 
 

time: 383 us -> 358 us (0.935)
  waiting for transfers between devices: 203 us -> 113 us
  starting transfers between devices: 139 us -> 205 us
  Pallas kernels: 39.9 us -> 35.6 us
    ppermute x54, waiting for transfers between devices: 203 us -> 113 us  [exchange(): moved[step] = lax.ppermute(pieces[step], axis, pairs)]
    ppermute x54, starting transfers between devices: 139 us -> 205 us  [exchange(): moved[step] = lax.ppermute(pieces[step], axis, pairs)]
    pallas_call x8, Pallas kernels: 15.2 us -> 10.9 us  [place(): pl.pallas_call(kernel, in_specs=[SCALARS] * len(table) + [WHOLE] * count...]
  transfers between devices with their start and end apart: 54 -> 54, of which waited for: 17 -> 12; matrix products, arithmetic and copies ran while one was open for 0% -> 0% of each run, Pallas kernels for 10% -> 9%
where the time goes in v5:
time: 358 us; the launch traced here: 354 us
  starting transfers between devices  205 us (57%)
  waiting for transfers between devices  113 us (32%)
  Pallas kernels  35.6 us (10%)
    ppermute x54, starting transfers between devices, exchange(): moved[step] = lax.ppermute(pieces[step], axis, pairs)  205 us
    ppermute x54, waiting for transfers between devices, exchange(): moved[step] = lax.ppermute(pieces[step], axis, pairs)  113 us
    pallas_call x8, Pallas kernels, pick_rows(): pl.pallas_call(kernel, grid=(width // tile,), in_specs=[SCALARS, pl.Block...  17.1 us
    pallas_call x8, Pallas kernels, place(): pl.pallas_call(kernel, in_specs=[SCALARS] * len(table) + [WHOLE] * count...  10.9 us
    pallas_call x8, Pallas kernels, choose(): pl.pallas_call(kernel, in_specs=[SCALARS] + [WHOLE] * count, out_specs=[W...  7.52 us
  transfers between devices with their start and end apart: 54, of which 12 were waited for; matrix products, arithmetic and copies ran while one was open for 0% of the time, Pallas kernels for 9%

profile of v5, /device:TPU:0, one launch (start us, length us, event | category | flops | bytes accessed | tf_op | source)
XLA Modules:
  0.0 353.6 jit_solution(1978587109606802394)
XLA Ops:
  1.2 3.1 collective-permute-start.27
  23.9 2.5 pick_rows.11
  26.4 4.5 %collective-permute-done.30.refs_2_ = bf16[384,128]{1,0:T(8,128)(2,1)S(1)} collective-permute-done((bf16[384,128]{1,0:T(8,128)(2,1)S(1)}, bf16[384,128]{1,0:T(8,128)(2,1)S(1)}, u32[]{:S(2)}, u32[]{:S(2)}) %collective-permute-start.30) | collective-permute-done | bytes 98336 | tf_op jit(solution)/shard_map/ppermute | solution.py:171
  30.9 5.2 %collective-permute-start.18 = (bf16[384,384]{1,0:T(8,128)(2,1)S(1)}, bf16[384,384]{1,0:T(8,128)(2,1)S(1)}, u32[]{:S(2)}, u32[]{:S(2)}) collective-permute-start(bf16[384,384]{1,0:T(8,128)(2,1)S(1)} %get-tuple-element.94), channel_id=1, source_target_pairs={{0,2},{2,6},{4,0},{6,4},{1,3},{3,7},{5,1},{7,5},{8,10},{10,14},{12... | collective-permute-start | bytes 884744 | tf_op jit(solution)/shard_map/ppermute | solution.py:171
  50.5 3.8 %collective-permute-start.52 = (bf16[384,256]{1,0:T(8,128)(2,1)S(1)}, bf16[384,256]{1,0:T(8,128)(2,1)S(1)}, u32[]{:S(2)}, u32[]{:S(2)}) collective-permute-start(bf16[384,256]{1,0:T(8,128)(2,1)S(1)} %get-tuple-element.131), channel_id=1, source_target_pairs={{0,6},{2,4},{4,2},{6,0},{1,7},{3,5},{5,3},{7,1},{8,14},{10,12},{12... | collective-permute-start | bytes 589832 | tf_op jit(solution)/shard_map/ppermute | solution.py:171
  54.3 12.0 %collective-permute-start.53 = (bf16[384,256]{1,0:T(8,128)(2,1)S(1)}, bf16[384,256]{1,0:T(8,128)(2,1)S(1)}, u32[]{:S(2)}, u32[]{:S(2)}) collective-permute-start(bf16[384,256]{1,0:T(8,128)(2,1)S(1)} %get-tuple-element.132), channel_id=1, source_target_pairs={{0,4},{2,0},{4,6},{6,2},{1,5},{3,1},{5,7},{7,3},{8,12},{10,8},{12,... | collective-permute-start | bytes 589832 | tf_op jit(solution)/shard_map/ppermute | solution.py:171
  75.3 3.5 pick_rows.13
  78.7 8.9 %collective-permute-done.43.refs_2_ = bf16[384,512]{1,0:T(8,128)(2,1)S(1)} collective-permute-done((bf16[384,512]{1,0:T(8,128)(2,1)S(1)}, bf16[384,512]{1,0:T(8,128)(2,1)S(1)}, u32[]{:S(2)}, u32[]{:S(2)}) %collective-permute-start.43) | collective-permute-done | bytes 393248 | tf_op jit(solution)/shard_map/ppermute | solution.py:171
  92.5 9.8 %collective-permute-done.7.refs_2_ = bf16[384,512]{1,0:T(8,128)(2,1)S(1)} collective-permute-done((bf16[384,512]{1,0:T(8,128)(2,1)S(1)}, bf16[384,512]{1,0:T(8,128)(2,1)S(1)}, u32[]{:S(2)}, u32[]{:S(2)}) %collective-permute-start.7) | collective-permute-done | bytes 393248 | tf_op jit(solution)/shard_map/ppermute | solution.py:171
  102.7 2.8 collective-permute-start.38
  105.5 16.4 %collective-permute-done.19.refs_1_ = bf16[384,384]{1,0:T(8,128)(2,1)S(1)} collective-permute-done((bf16[384,384]{1,0:T(8,128)(2,1)S(1)}, bf16[384,384]{1,0:T(8,128)(2,1)S(1)}, u32[]{:S(2)}, u32[]{:S(2)}) %collective-permute-start.19) | collective-permute-done | bytes 294944 | tf_op jit(solution)/shard_map/ppermute | solution.py:171
  124.6 9.3 %collective-permute-done.21.refs_2_ = bf16[384,384]{1,0:T(8,128)(2,1)S(1)} collective-permute-done((bf16[384,384]{1,0:T(8,128)(2,1)S(1)}, bf16[384,384]{1,0:T(8,128)(2,1)S(1)}, u32[]{:S(2)}, u32[]{:S(2)}) %collective-permute-start.21) | collective-permute-done | bytes 294944 | tf_op jit(solution)/shard_map/ppermute | solution.py:171
  134.0 7.1 %collective-permute-start.45 = (bf16[384,512]{1,0:T(8,128)(2,1)S(1)}, bf16[384,512]{1,0:T(8,128)(2,1)S(1)}, u32[]{:S(2)}, u32[]{:S(2)}) collective-permute-start(bf16[384,512]{1,0:T(8,128)(2,1)S(1)} %get-tuple-element.122), channel_id=1, source_target_pairs={{0,2},{2,6},{4,0},{6,4},{1,3},{3,7},{5,1},{7,5},{8,10},{10,14},{12... | collective-permute-start | bytes 1179656 | tf_op jit(solution)/shard_map/ppermute | solution.py:171
  141.1 3.5 pick_rows.10
  145.7 11.0 %collective-permute-done.45.refs_1_ = bf16[384,512]{1,0:T(8,128)(2,1)S(1)} collective-permute-done((bf16[384,512]{1,0:T(8,128)(2,1)S(1)}, bf16[384,512]{1,0:T(8,128)(2,1)S(1)}, u32[]{:S(2)}, u32[]{:S(2)}) %collective-permute-start.45) | collective-permute-done | bytes 393248 | tf_op jit(solution)/shard_map/ppermute | solution.py:171
  156.7 4.7 %collective-permute-start.13 = (bf16[384,1024]{1,0:T(8,128)(2,1)S(1)}, bf16[384,1024]{1,0:T(8,128)(2,1)S(1)}, u32[]{:S(2)}, u32[]{:S(2)}) collective-permute-start(bf16[384,1024]{1,0:T(8,128)(2,1)S(1)} %get-tuple-element.87), channel_id=1, source_target_pairs={{0,16},{8,24},{16,0},{24,8},{1,17},{9,25},{17,1},{25,9},{2,18},{10... | collective-permute-start | bytes 2359304 | tf_op jit(solution)/shard_map/ppermute | solution.py:171
  162.5 7.1 %collective-permute-done.46.refs_2_ = bf16[384,512]{1,0:T(8,128)(2,1)S(1)} collective-permute-done((bf16[384,512]{1,0:T(8,128)(2,1)S(1)}, bf16[384,512]{1,0:T(8,128)(2,1)S(1)}, u32[]{:S(2)}, u32[]{:S(2)}) %collective-permute-start.46) | collective-permute-done | bytes 393248 | tf_op jit(solution)/shard_map/ppermute | solution.py:171
  169.6 18.2 %collective-permute-start.39 = (bf16[384,1024]{1,0:T(8,128)(2,1)S(1)}, bf16[384,1024]{1,0:T(8,128)(2,1)S(1)}, u32[]{:S(2)}, u32[]{:S(2)}) collective-permute-start(bf16[384,1024]{1,0:T(8,128)(2,1)S(1)} %get-tuple-element.114), channel_id=1, source_target_pairs={{0,2},{2,6},{4,0},{6,4},{1,3},{3,7},{5,1},{7,5},{8,10},{10,14},{12... | collective-permute-start | bytes 2359304 | tf_op jit(solution)/shard_map/ppermute | solution.py:171
  188.8 3.0 collective-permute-start.10
  196.3 19.8 %collective-permute-done.10.refs_2_ = bf16[384,512]{1,0:T(8,128)(2,1)S(1)} collective-permute-done((bf16[384,512]{1,0:T(8,128)(2,1)S(1)}, bf16[384,512]{1,0:T(8,128)(2,1)S(1)}, u32[]{:S(2)}, u32[]{:S(2)}) %collective-permute-start.10) | collective-permute-done | bytes 393248 | tf_op jit(solution)/shard_map/ppermute | solution.py:171
  216.2 42.1 %collective-permute-start.41 = (bf16[384,1024]{1,0:T(8,128)(2,1)S(1)}, bf16[384,1024]{1,0:T(8,128)(2,1)S(1)}, u32[]{:S(2)}, u32[]{:S(2)}) collective-permute-start(bf16[384,1024]{1,0:T(8,128)(2,1)S(1)} %get-tuple-element.116), channel_id=1, source_target_pairs={{0,4},{2,0},{4,6},{6,2},{1,5},{3,1},{5,7},{7,3},{8,12},{10,8},{12,... | collective-permute-start | bytes 2359304 | tf_op jit(solution)/shard_map/ppermute | solution.py:171
  262.4 41.7 %collective-permute-start.11 = (bf16[384,512]{1,0:T(8,128)(2,1)S(1)}, bf16[384,512]{1,0:T(8,128)(2,1)S(1)}, u32[]{:S(2)}, u32[]{:S(2)}) collective-permute-start(bf16[384,512]{1,0:T(8,128)(2,1)S(1)} %get-tuple-element.84), channel_id=1, source_target_pairs={{0,4},{2,0},{4,6},{6,2},{1,5},{3,1},{5,7},{7,3},{8,12},{10,8},{12,... | collective-permute-start | bytes 1179656 | tf_op jit(solution)/shard_map/ppermute | solution.py:171
  305.5 21.7 %collective-permute-done.15.refs_1_ = bf16[384,1024]{1,0:T(8,128)(2,1)S(1)} collective-permute-done((bf16[384,1024]{1,0:T(8,128)(2,1)S(1)}, bf16[384,1024]{1,0:T(8,128)(2,1)S(1)}, u32[]{:S(2)}, u32[]{:S(2)}) %collective-permute-start.15) | collective-permute-done | bytes 786464 | tf_op jit(solution)/shard_map/ppermute | solution.py:171
  328.3 14.3 %collective-permute-start.5 = (bf16[384,256]{1,0:T(8,128)(2,1)S(1)}, bf16[384,256]{1,0:T(8,128)(2,1)S(1)}, u32[]{:S(2)}, u32[]{:S(2)}) collective-permute-start(bf16[384,256]{1,0:T(8,128)(2,1)S(1)} %get-tuple-element.76), channel_id=1, source_target_pairs={{0,4},{2,0},{4,6},{6,2},{1,5},{3,1},{5,7},{7,3},{8,12},{10,8},{12,... | collective-permute-start | bytes 589832 | tf_op jit(solution)/shard_map/ppermute | solution.py:171
  (108 shorter events, 77.1 us)
Async XLA Ops:
  42.8 25.4 %collective-permute-start.22 = (bf16[384,384]{1,0:T(8,128)(2,1)S(1)}, bf16[384,384]{1,0:T(8,128)(2,1)S(1)}, u32[]{:S(2)}, u32[]{:S(2)}) collective-permute-start(bf16[384,384]{1,0:T(8,128)(2,1)S(1)} %get-tuple-element.96), channel_id=1, source_target_pairs={{0,4},{2,0},{4,6},{6,2},{1,5},{3,1},{5,7},{7,3},{8,12},{10,8},{12,... | collective-permute-start | bytes 884744 | tf_op jit(solution)/shard_map/ppermute | solution.py:171
  46.0 28.1 %collective-permute-start.42 = (bf16[384,512]{1,0:T(8,128)(2,1)S(1)}, bf16[384,512]{1,0:T(8,128)(2,1)S(1)}, u32[]{:S(2)}, u32[]{:S(2)}) collective-permute-start(bf16[384,512]{1,0:T(8,128)(2,1)S(1)} %get-tuple-element.118), channel_id=1, source_target_pairs={{0,8},{8,0},{16,24},{24,16},{1,9},{9,1},{17,25},{25,17},{2,10},{10... | collective-permute-start | bytes 1179656 | tf_op jit(solution)/shard_map/ppermute | solution.py:171
  72.3 30.0 %collective-permute-start.7 = (bf16[384,512]{1,0:T(8,128)(2,1)S(1)}, bf16[384,512]{1,0:T(8,128)(2,1)S(1)}, u32[]{:S(2)}, u32[]{:S(2)}) collective-permute-start(bf16[384,512]{1,0:T(8,128)(2,1)S(1)} %get-tuple-element.79), channel_id=1, source_target_pairs={{0,16},{8,24},{16,0},{24,8},{1,17},{9,25},{17,1},{25,9},{2,18},{10... | collective-permute-start | bytes 1179656 | tf_op jit(solution)/shard_map/ppermute | solution.py:171
  74.2 28.5 %collective-permute-start.8 = (bf16[384,512]{1,0:T(8,128)(2,1)S(1)}, bf16[384,512]{1,0:T(8,128)(2,1)S(1)}, u32[]{:S(2)}, u32[]{:S(2)}) collective-permute-start(bf16[384,512]{1,0:T(8,128)(2,1)S(1)} %get-tuple-element.80), channel_id=1, source_target_pairs={{0,24},{8,16},{16,8},{24,0},{1,25},{9,17},{17,9},{25,1},{2,26},{10... | collective-permute-start | bytes 1179656 | tf_op jit(solution)/shard_map/ppermute | solution.py:171
  87.6 69.1 %collective-permute-start.36 = (bf16[384,1024]{1,0:T(8,128)(2,1)S(1)}, bf16[384,1024]{1,0:T(8,128)(2,1)S(1)}, u32[]{:S(2)}, u32[]{:S(2)}) collective-permute-start(bf16[384,1024]{1,0:T(8,128)(2,1)S(1)} %get-tuple-element.110), channel_id=1, source_target_pairs={{0,8},{8,0},{16,24},{24,16},{1,9},{9,1},{17,25},{25,17},{2,10},{10... | collective-permute-start | bytes 2359304 | tf_op jit(solution)/shard_map/ppermute | solution.py:171
  88.9 33.0 %collective-permute-start.19 = (bf16[384,384]{1,0:T(8,128)(2,1)S(1)}, bf16[384,384]{1,0:T(8,128)(2,1)S(1)}, u32[]{:S(2)}, u32[]{:S(2)}) collective-permute-start(bf16[384,384]{1,0:T(8,128)(2,1)S(1)} %collective-permute-done.18), channel_id=1, source_target_pairs={{0,8},{8,0},{16,24},{24,16},{1,9},{9,1},{17,25},{25,17},{2,10},{10... | collective-permute-start | bytes 884744 | tf_op jit(solution)/shard_map/ppermute | solution.py:171
  90.7 70.7 %collective-permute-start.37 = (bf16[384,1024]{1,0:T(8,128)(2,1)S(1)}, bf16[384,1024]{1,0:T(8,128)(2,1)S(1)}, u32[]{:S(2)}, u32[]{:S(2)}) collective-permute-start(bf16[384,1024]{1,0:T(8,128)(2,1)S(1)} %get-tuple-element.111), channel_id=1, source_target_pairs={{0,16},{8,24},{16,0},{24,8},{1,17},{9,25},{17,1},{25,9},{2,18},{10... | collective-permute-start | bytes 2359304 | tf_op jit(solution)/shard_map/ppermute | solution.py:171
  102.3 31.7 %collective-permute-start.21 = (bf16[384,384]{1,0:T(8,128)(2,1)S(1)}, bf16[384,384]{1,0:T(8,128)(2,1)S(1)}, u32[]{:S(2)}, u32[]{:S(2)}) collective-permute-start(bf16[384,384]{1,0:T(8,128)(2,1)S(1)} %collective-permute-done.20), channel_id=1, source_target_pairs={{0,16},{8,24},{16,0},{24,8},{1,17},{9,25},{17,1},{25,9},{2,18},{10... | collective-permute-start | bytes 884744 | tf_op jit(solution)/shard_map/ppermute | solution.py:171
  102.7 58.7 %collective-permute-start.38 = (bf16[384,1024]{1,0:T(8,128)(2,1)S(1)}, bf16[384,1024]{1,0:T(8,128)(2,1)S(1)}, u32[]{:S(2)}, u32[]{:S(2)}) collective-permute-start(bf16[384,1024]{1,0:T(8,128)(2,1)S(1)} %get-tuple-element.112), channel_id=1, source_target_pairs={{0,24},{8,16},{16,8},{24,0},{1,25},{9,17},{17,9},{25,1},{2,26},{10... | collective-permute-start | bytes 2359304 | tf_op jit(solution)/shard_map/ppermute | solution.py:171
  144.6 48.2 %collective-permute-start.12 = (bf16[384,1024]{1,0:T(8,128)(2,1)S(1)}, bf16[384,1024]{1,0:T(8,128)(2,1)S(1)}, u32[]{:S(2)}, u32[]{:S(2)}) collective-permute-start(bf16[384,1024]{1,0:T(8,128)(2,1)S(1)} %get-tuple-element.86), channel_id=1, source_target_pairs={{0,8},{8,0},{16,24},{24,16},{1,9},{9,1},{17,25},{25,17},{2,10},{10... | collective-permute-start | bytes 2359304 | tf_op jit(solution)/shard_map/ppermute | solution.py:171
  156.7 37.6 %collective-permute-start.13 = (bf16[384,1024]{1,0:T(8,128)(2,1)S(1)}, bf16[384,1024]{1,0:T(8,128)(2,1)S(1)}, u32[]{:S(2)}, u32[]{:S(2)}) collective-permute-start(bf16[384,1024]{1,0:T(8,128)(2,1)S(1)} %get-tuple-element.87), channel_id=1, source_target_pairs={{0,16},{8,24},{16,0},{24,8},{1,17},{9,25},{17,1},{25,9},{2,18},{10... | collective-permute-start | bytes 2359304 | tf_op jit(solution)/shard_map/ppermute | solution.py:171
  161.4 34.2 %collective-permute-start.14 = (bf16[384,1024]{1,0:T(8,128)(2,1)S(1)}, bf16[384,1024]{1,0:T(8,128)(2,1)S(1)}, u32[]{:S(2)}, u32[]{:S(2)}) collective-permute-start(bf16[384,1024]{1,0:T(8,128)(2,1)S(1)} %get-tuple-element.88), channel_id=1, source_target_pairs={{0,24},{8,16},{16,8},{24,0},{1,25},{9,17},{17,9},{25,1},{2,26},{10... | collective-permute-start | bytes 2359304 | tf_op jit(solution)/shard_map/ppermute | solution.py:171
  161.4 27.4 %collective-permute-start.47 = (bf16[384,512]{1,0:T(8,128)(2,1)S(1)}, bf16[384,512]{1,0:T(8,128)(2,1)S(1)}, u32[]{:S(2)}, u32[]{:S(2)}) collective-permute-start(bf16[384,512]{1,0:T(8,128)(2,1)S(1)} %get-tuple-element.124), channel_id=1, source_target_pairs={{0,4},{2,0},{4,6},{6,2},{1,5},{3,1},{5,7},{7,3},{8,12},{10,8},{12,... | collective-permute-start | bytes 1179656 | tf_op jit(solution)/shard_map/ppermute | solution.py:171
  169.6 91.2 %collective-permute-start.39 = (bf16[384,1024]{1,0:T(8,128)(2,1)S(1)}, bf16[384,1024]{1,0:T(8,128)(2,1)S(1)}, u32[]{:S(2)}, u32[]{:S(2)}) collective-permute-start(bf16[384,1024]{1,0:T(8,128)(2,1)S(1)} %get-tuple-element.114), channel_id=1, source_target_pairs={{0,2},{2,6},{4,0},{6,4},{1,3},{3,7},{5,1},{7,5},{8,10},{10,14},{12... | collective-permute-start | bytes 2359304 | tf_op jit(solution)/shard_map/ppermute | solution.py:171
  188.8 27.3 %collective-permute-start.10 = (bf16[384,512]{1,0:T(8,128)(2,1)S(1)}, bf16[384,512]{1,0:T(8,128)(2,1)S(1)}, u32[]{:S(2)}, u32[]{:S(2)}) collective-permute-start(bf16[384,512]{1,0:T(8,128)(2,1)S(1)} %get-tuple-element.83), channel_id=1, source_target_pairs={{0,6},{2,4},{4,2},{6,0},{1,7},{3,5},{5,3},{7,1},{8,14},{10,12},{12... | collective-permute-start | bytes 1179656 | tf_op jit(solution)/shard_map/ppermute | solution.py:171
  194.4 65.0 %collective-permute-start.25 = (bf16[384,384]{1,0:T(8,128)(2,1)S(1)}, bf16[384,384]{1,0:T(8,128)(2,1)S(1)}, u32[]{:S(2)}, u32[]{:S(2)}) collective-permute-start(bf16[384,384]{1,0:T(8,128)(2,1)S(1)} %get-tuple-element.99), channel_id=1, source_target_pairs={{0,16},{8,24},{16,0},{24,8},{1,17},{9,25},{17,1},{25,9},{2,18},{10... | collective-permute-start | bytes 884744 | tf_op jit(solution)/shard_map/ppermute | solution.py:171
  195.6 63.8 %collective-permute-start.26 = (bf16[384,384]{1,0:T(8,128)(2,1)S(1)}, bf16[384,384]{1,0:T(8,128)(2,1)S(1)}, u32[]{:S(2)}, u32[]{:S(2)}) collective-permute-start(bf16[384,384]{1,0:T(8,128)(2,1)S(1)} %get-tuple-element.100), channel_id=1, source_target_pairs={{0,24},{8,16},{16,8},{24,0},{1,25},{9,17},{17,9},{25,1},{2,26},{10... | collective-permute-start | bytes 884744 | tf_op jit(solution)/shard_map/ppermute | solution.py:171
  216.2 46.2 %collective-permute-start.40 = (bf16[384,1024]{1,0:T(8,128)(2,1)S(1)}, bf16[384,1024]{1,0:T(8,128)(2,1)S(1)}, u32[]{:S(2)}, u32[]{:S(2)}) collective-permute-start(bf16[384,1024]{1,0:T(8,128)(2,1)S(1)} %get-tuple-element.115), channel_id=1, source_target_pairs={{0,6},{2,4},{4,2},{6,0},{1,7},{3,5},{5,3},{7,1},{8,14},{10,12},{12... | collective-permute-start | bytes 2359304 | tf_op jit(solution)/shard_map/ppermute | solution.py:171
  216.2 87.9 %collective-permute-start.41 = (bf16[384,1024]{1,0:T(8,128)(2,1)S(1)}, bf16[384,1024]{1,0:T(8,128)(2,1)S(1)}, u32[]{:S(2)}, u32[]{:S(2)}) collective-permute-start(bf16[384,1024]{1,0:T(8,128)(2,1)S(1)} %get-tuple-element.116), channel_id=1, source_target_pairs={{0,4},{2,0},{4,6},{6,2},{1,5},{3,1},{5,7},{7,3},{8,12},{10,8},{12,... | collective-permute-start | bytes 2359304 | tf_op jit(solution)/shard_map/ppermute | solution.py:171
  259.3 67.9 %collective-permute-start.15 = (bf16[384,1024]{1,0:T(8,128)(2,1)S(1)}, bf16[384,1024]{1,0:T(8,128)(2,1)S(1)}, u32[]{:S(2)}, u32[]{:S(2)}) collective-permute-start(bf16[384,1024]{1,0:T(8,128)(2,1)S(1)} %get-tuple-element.90), channel_id=1, source_target_pairs={{0,2},{2,6},{4,0},{6,4},{1,3},{3,7},{5,1},{7,5},{8,10},{10,14},{12... | collective-permute-start | bytes 2359304 | tf_op jit(solution)/shard_map/ppermute | solution.py:171
  259.4 67.9 %collective-permute-start.16 = (bf16[384,1024]{1,0:T(8,128)(2,1)S(1)}, bf16[384,1024]{1,0:T(8,128)(2,1)S(1)}, u32[]{:S(2)}, u32[]{:S(2)}) collective-permute-start(bf16[384,1024]{1,0:T(8,128)(2,1)S(1)} %get-tuple-element.91), channel_id=1, source_target_pairs={{0,6},{2,4},{4,2},{6,0},{1,7},{3,5},{5,3},{7,1},{8,14},{10,12},{12... | collective-permute-start | bytes 2359304 | tf_op jit(solution)/shard_map/ppermute | solution.py:171
  260.9 67.4 %collective-permute-start.17 = (bf16[384,1024]{1,0:T(8,128)(2,1)S(1)}, bf16[384,1024]{1,0:T(8,128)(2,1)S(1)}, u32[]{:S(2)}, u32[]{:S(2)}) collective-permute-start(bf16[384,1024]{1,0:T(8,128)(2,1)S(1)} %get-tuple-element.92), channel_id=1, source_target_pairs={{0,4},{2,0},{4,6},{6,2},{1,5},{3,1},{5,7},{7,3},{8,12},{10,8},{12,... | collective-permute-start | bytes 2359304 | tf_op jit(solution)/shard_map/ppermute | solution.py:171
  262.4 89.0 %collective-permute-start.11 = (bf16[384,512]{1,0:T(8,128)(2,1)S(1)}, bf16[384,512]{1,0:T(8,128)(2,1)S(1)}, u32[]{:S(2)}, u32[]{:S(2)}) collective-permute-start(bf16[384,512]{1,0:T(8,128)(2,1)S(1)} %get-tuple-element.84), channel_id=1, source_target_pairs={{0,4},{2,0},{4,6},{6,2},{1,5},{3,1},{5,7},{7,3},{8,12},{10,8},{12,... | collective-permute-start | bytes 1179656 | tf_op jit(solution)/shard_map/ppermute | solution.py:171
  304.0 47.4 %collective-permute-start.9 = (bf16[384,512]{1,0:T(8,128)(2,1)S(1)}, bf16[384,512]{1,0:T(8,128)(2,1)S(1)}, u32[]{:S(2)}, u32[]{:S(2)}) collective-permute-start(bf16[384,512]{1,0:T(8,128)(2,1)S(1)} %get-tuple-element.82), channel_id=1, source_target_pairs={{0,2},{2,6},{4,0},{6,4},{1,3},{3,7},{5,1},{7,5},{8,10},{10,14},{12... | collective-permute-start | bytes 1179656 | tf_op jit(solution)/shard_map/ppermute | solution.py:171
  (30 other events, 484.6 us)

commit v6 on v5

--- a/solution.py
+++ b/solution.py
@@ -6,12 +6,13 @@
 from jax.sharding import PartitionSpec as P
 
 
-SHARES = {"X": 1, "Y": 3, "0": 2, "1": 4, "2": 8, "3": 8, "4": 4, "5": 2}
+SHARES = {"X": 1, "Y": 3, "0": 2, "1": 4, "2": 6, "3": 8, "4": 6, "5": 2}
 TP_FIRST = "XY"
 ORDER = (
     "AX", "AY", "A0", "A1", "B0", "HX", "A2", "B1", "HY", "A3", "C0", "B2", "A4",
     "BX", "C1", "BY", "A5", "B3", "B4", "B5", "C2", "CX", "CY", "C3", "C4", "C5",
 )
+WORTH_CHUNKS = 1 << 19
 ANY = pl.BlockSpec(memory_space=pl.ANY)
 SCALARS = pl.BlockSpec(memory_space=pltpu.SMEM)
 PARAMS = pltpu.CompilerParams(vmem_limit_bytes=8 << 20)
@@ -35,14 +36,16 @@
     return 256 if offset % 256 == 0 and width % 256 == 0 else 128
 
 
-def spread(hidden):
+def plan_of(hidden, block_rows):
+    columns = hidden // 128
+    if hidden * block_rows < WORTH_CHUNKS or columns < len(SHARES):
+        return {"0": (0, hidden)}, ("A0", "B0", "C0")
     total = sum(SHARES.values())
-    columns = hidden // 128
     edges, done = [0], 0
     for left, share in zip(reversed(range(len(SHARES))), SHARES.values()):
         done += share
         edges.append(max(edges[-1] + 1, min(done * columns // total, columns - left)))
-    return {chunk: (low * 128, (high - low) * 128) for chunk, low, high in zip(SHARES, edges, edges[1:])}
+    return {chunk: (low * 128, (high - low) * 128) for chunk, low, high in zip(SHARES, edges, edges[1:])}, ORDER
 
 
 def axis_of(stage, chunk):
@@ -53,9 +56,9 @@
     return "ep" if stage == "H" else None
 
 
-def steps_of(axis, count, chunk):
+def steps_of(axis, count, last):
     steps = list(range(1, count))
-    if axis == "tp" and chunk != ORDER[-1][1]:
+    if axis == "tp" and not last:
         steps.insert(0, steps.pop(count // 2 - 1))
     return steps
 
@@ -163,10 +166,10 @@
     )(*table, *in_vmem(pieces), *saved)
 
 
-def exchange(pieces, axis, chunk):
+def exchange(pieces, axis, last):
     count = len(pieces)
     moved = {0: pieces[0]}
-    for step in steps_of(axis, count, chunk):
+    for step in steps_of(axis, count, last):
         pairs = [(index, partner_of(axis, index, step, count)) for index in range(count)]
         moved[step] = lax.ppermute(pieces[step], axis, pairs)
     return [moved[step] for step in range(count)]
@@ -177,11 +180,11 @@
     hidden = weight.shape[0]
     owned = pltpu.with_memory_space_constraint(jnp.transpose(owned_span, (0, 2, 1)), pltpu.HBM)
     sizes = tuple(lax.axis_size(name) for name in ("ep", "tp", "dp"))
-    chunks = spread(hidden)
+    chunks, order = plan_of(hidden, weight.shape[1] // sizes[1])
 
     moved = {}
     saved = []
-    for stage, chunk in ORDER:
+    for stage, chunk in order:
         first = chunk in TP_FIRST
         offset, width = chunks[chunk]
         if stage == "A":
@@ -193,15 +196,24 @@
         else:
             saved = [place(saved, moved[chunk], owned, sizes, first, offset, hidden)]
             continue
-        moved[chunk] = exchange(sent, axis_of(stage, chunk), chunk)
+        moved[chunk] = exchange(sent, axis_of(stage, chunk), chunk == order[-1][1])
     return saved[0][None, None]
 
 
 def solution(mesh):
-    return jax.shard_map(
+    step = jax.shard_map(
         local,
         mesh=mesh,
         in_specs=(P("ep", "tp", "dp"), P()),
         out_specs=P("ep", "tp", "dp", None),
         check_vma=False,
     )
+
+    def save(down_weight, owned_span):
+        sizes = mesh.shape
+        hidden = down_weight.shape[1] // sizes["tp"]
+        block_rows = down_weight.shape[2] // (sizes["dp"] * sizes["tp"])
+        _, _ = plan_of(hidden, block_rows)
+        return step(down_weight, owned_span)
+
+    return save

time: 358 us -> 364 us (1.017)
  waiting for transfers between devices: 113 us -> 126 us
  starting transfers between devices: 205 us -> 199 us
    ppermute x54, waiting for transfers between devices: 113 us -> 126 us  [exchange(): moved[step] = lax.ppermute(pieces[step], axis, pairs)]
    ppermute x54, starting transfers between devices: 205 us -> 199 us  [exchange(): moved[step] = lax.ppermute(pieces[step], axis, pairs)]
  transfers between devices with their start and end apart: 54 -> 54, of which waited for: 12 -> 16; matrix products, arithmetic and copies ran while one was open for 0% -> 0% of each run, Pallas kernels for 9% -> 9%
where the time goes in v6:
time: 364 us; the launch traced here: 362 us
  starting transfers between devices  199 us (55%)
  waiting for transfers between devices  126 us (35%)
  Pallas kernels  36.1 us (10%)
    ppermute x54, starting transfers between devices, exchange(): moved[step] = lax.ppermute(pieces[step], axis, pairs)  199 us
    ppermute x54, waiting for transfers between devices, exchange(): moved[step] = lax.ppermute(pieces[step], axis, pairs)  126 us
    pallas_call x8, Pallas kernels, pick_rows(): pl.pallas_call(kernel, grid=(width // tile,), in_specs=[SCALARS, pl.Block...  17.7 us
    pallas_call x8, Pallas kernels, place(): pl.pallas_call(kernel, in_specs=[SCALARS] * len(table) + [WHOLE] * count...  10.9 us
    pallas_call x8, Pallas kernels, choose(): pl.pallas_call(kernel, in_specs=[SCALARS] + [WHOLE] * count, out_specs=[W...  7.52 us
  transfers between devices with their start and end apart: 54, of which 16 were waited for; matrix products, arithmetic and copies ran while one was open for 0% of the time, Pallas kernels for 9%

profile of v6, /device:TPU:0, one launch (start us, length us, event | category | flops | bytes accessed | tf_op | source)
XLA Modules:
  0.0 361.7 jit_solution(11994229553484392475)
XLA Ops:
  1.2 3.1 collective-permute-start.27
  26.4 4.5 %collective-permute-done.30.refs_2_ = bf16[384,128]{1,0:T(8,128)(2,1)S(1)} collective-permute-done((bf16[384,128]{1,0:T(8,128)(2,1)S(1)}, bf16[384,128]{1,0:T(8,128)(2,1)S(1)}, u32[]{:S(2)}, u32[]{:S(2)}) %collective-permute-start.30) | collective-permute-done | bytes 98336 | tf_op jit(solution)/shard_map/ppermute | solution.py:174
  30.9 5.2 %collective-permute-start.18 = (bf16[384,384]{1,0:T(8,128)(2,1)S(1)}, bf16[384,384]{1,0:T(8,128)(2,1)S(1)}, u32[]{:S(2)}, u32[]{:S(2)}) collective-permute-start(bf16[384,384]{1,0:T(8,128)(2,1)S(1)} %get-tuple-element.94), channel_id=1, source_target_pairs={{0,2},{2,6},{4,0},{6,4},{1,3},{3,7},{5,1},{7,5},{8,10},{10,14},{12... | collective-permute-start | bytes 884744 | tf_op jit(solution)/shard_map/ppermute | solution.py:174
  50.4 3.9 %collective-permute-start.52 = (bf16[384,256]{1,0:T(8,128)(2,1)S(1)}, bf16[384,256]{1,0:T(8,128)(2,1)S(1)}, u32[]{:S(2)}, u32[]{:S(2)}) collective-permute-start(bf16[384,256]{1,0:T(8,128)(2,1)S(1)} %get-tuple-element.131), channel_id=1, source_target_pairs={{0,6},{2,4},{4,2},{6,0},{1,7},{3,5},{5,3},{7,1},{8,14},{10,12},{12... | collective-permute-start | bytes 589832 | tf_op jit(solution)/shard_map/ppermute | solution.py:174
  54.3 12.0 %collective-permute-start.53 = (bf16[384,256]{1,0:T(8,128)(2,1)S(1)}, bf16[384,256]{1,0:T(8,128)(2,1)S(1)}, u32[]{:S(2)}, u32[]{:S(2)}) collective-permute-start(bf16[384,256]{1,0:T(8,128)(2,1)S(1)} %get-tuple-element.132), channel_id=1, source_target_pairs={{0,4},{2,0},{4,6},{6,2},{1,5},{3,1},{5,7},{7,3},{8,12},{10,8},{12,... | collective-permute-start | bytes 589832 | tf_op jit(solution)/shard_map/ppermute | solution.py:174
  66.4 2.9 pick_rows.13
  79.3 7.8 %collective-permute-done.43.refs_2_ = bf16[384,512]{1,0:T(8,128)(2,1)S(1)} collective-permute-done((bf16[384,512]{1,0:T(8,128)(2,1)S(1)}, bf16[384,512]{1,0:T(8,128)(2,1)S(1)}, u32[]{:S(2)}, u32[]{:S(2)}) %collective-permute-start.43) | collective-permute-done | bytes 393248 | tf_op jit(solution)/shard_map/ppermute | solution.py:174
  87.9 8.1 %collective-permute-done.44.refs_3_ = bf16[384,512]{1,0:T(8,128)(2,1)S(1)} collective-permute-done((bf16[384,512]{1,0:T(8,128)(2,1)S(1)}, bf16[384,512]{1,0:T(8,128)(2,1)S(1)}, u32[]{:S(2)}, u32[]{:S(2)}) %collective-permute-start.44) | collective-permute-done | bytes 393248 | tf_op jit(solution)/shard_map/ppermute | solution.py:174
  99.4 19.7 %collective-permute-done.37.refs_2_ = bf16[384,768]{1,0:T(8,128)(2,1)S(1)} collective-permute-done((bf16[384,768]{1,0:T(8,128)(2,1)S(1)}, bf16[384,768]{1,0:T(8,128)(2,1)S(1)}, u32[]{:S(2)}, u32[]{:S(2)}) %collective-permute-start.37) | collective-permute-done | bytes 589856 | tf_op jit(solution)/shard_map/ppermute | solution.py:174
  125.7 13.4 %collective-permute-done.21.refs_2_ = bf16[384,384]{1,0:T(8,128)(2,1)S(1)} collective-permute-done((bf16[384,384]{1,0:T(8,128)(2,1)S(1)}, bf16[384,384]{1,0:T(8,128)(2,1)S(1)}, u32[]{:S(2)}, u32[]{:S(2)}) %collective-permute-start.21) | collective-permute-done | bytes 294944 | tf_op jit(solution)/shard_map/ppermute | solution.py:174
  139.1 6.0 %collective-permute-start.45 = (bf16[384,512]{1,0:T(8,128)(2,1)S(1)}, bf16[384,512]{1,0:T(8,128)(2,1)S(1)}, u32[]{:S(2)}, u32[]{:S(2)}) collective-permute-start(bf16[384,512]{1,0:T(8,128)(2,1)S(1)} %get-tuple-element.122), channel_id=1, source_target_pairs={{0,2},{2,6},{4,0},{6,4},{1,3},{3,7},{5,1},{7,5},{8,10},{10,14},{12... | collective-permute-start | bytes 1179656 | tf_op jit(solution)/shard_map/ppermute | solution.py:174
  145.1 3.5 pick_rows.10
  154.8 17.0 %collective-permute-done.45.refs_1_ = bf16[384,512]{1,0:T(8,128)(2,1)S(1)} collective-permute-done((bf16[384,512]{1,0:T(8,128)(2,1)S(1)}, bf16[384,512]{1,0:T(8,128)(2,1)S(1)}, u32[]{:S(2)}, u32[]{:S(2)}) %collective-permute-start.45) | collective-permute-done | bytes 393248 | tf_op jit(solution)/shard_map/ppermute | solution.py:174
  172.8 7.5 %collective-permute-start.39 = (bf16[384,768]{1,0:T(8,128)(2,1)S(1)}, bf16[384,768]{1,0:T(8,128)(2,1)S(1)}, u32[]{:S(2)}, u32[]{:S(2)}) collective-permute-start(bf16[384,768]{1,0:T(8,128)(2,1)S(1)} %get-tuple-element.114), channel_id=1, source_target_pairs={{0,2},{2,6},{4,0},{6,4},{1,3},{3,7},{5,1},{7,5},{8,10},{10,14},{12... | collective-permute-start | bytes 1769480 | tf_op jit(solution)/shard_map/ppermute | solution.py:174
  180.3 17.7 %collective-permute-done.47.refs_3_ = bf16[384,512]{1,0:T(8,128)(2,1)S(1)} collective-permute-done((bf16[384,512]{1,0:T(8,128)(2,1)S(1)}, bf16[384,512]{1,0:T(8,128)(2,1)S(1)}, u32[]{:S(2)}, u32[]{:S(2)}) %collective-permute-start.47) | collective-permute-done | bytes 393248 | tf_op jit(solution)/shard_map/ppermute | solution.py:174
  199.1 3.4 collective-permute-start.26
  209.0 3.8 %collective-permute-start.10 = (bf16[384,768]{1,0:T(8,128)(2,1)S(1)}, bf16[384,768]{1,0:T(8,128)(2,1)S(1)}, u32[]{:S(2)}, u32[]{:S(2)}) collective-permute-start(bf16[384,768]{1,0:T(8,128)(2,1)S(1)} %get-tuple-element.83), channel_id=1, source_target_pairs={{0,6},{2,4},{4,2},{6,0},{1,7},{3,5},{5,3},{7,1},{8,14},{10,12},{12... | collective-permute-start | bytes 1769480 | tf_op jit(solution)/shard_map/ppermute | solution.py:174
  213.9 7.5 %collective-permute-done.39.refs_1_ = bf16[384,768]{1,0:T(8,128)(2,1)S(1)} collective-permute-done((bf16[384,768]{1,0:T(8,128)(2,1)S(1)}, bf16[384,768]{1,0:T(8,128)(2,1)S(1)}, u32[]{:S(2)}, u32[]{:S(2)}) %collective-permute-start.39) | collective-permute-done | bytes 589856 | tf_op jit(solution)/shard_map/ppermute | solution.py:174
  221.5 6.9 %collective-permute-start.16 = (bf16[384,1024]{1,0:T(8,128)(2,1)S(1)}, bf16[384,1024]{1,0:T(8,128)(2,1)S(1)}, u32[]{:S(2)}, u32[]{:S(2)}) collective-permute-start(bf16[384,1024]{1,0:T(8,128)(2,1)S(1)} %get-tuple-element.91), channel_id=1, source_target_pairs={{0,6},{2,4},{4,2},{6,0},{1,7},{3,5},{5,3},{7,1},{8,14},{10,12},{12... | collective-permute-start | bytes 2359304 | tf_op jit(solution)/shard_map/ppermute | solution.py:174
  228.4 26.7 %collective-permute-start.17 = (bf16[384,1024]{1,0:T(8,128)(2,1)S(1)}, bf16[384,1024]{1,0:T(8,128)(2,1)S(1)}, u32[]{:S(2)}, u32[]{:S(2)}) collective-permute-start(bf16[384,1024]{1,0:T(8,128)(2,1)S(1)} %get-tuple-element.92), channel_id=1, source_target_pairs={{0,4},{2,0},{4,6},{6,2},{1,5},{3,1},{5,7},{7,3},{8,12},{10,8},{12,... | collective-permute-start | bytes 2359304 | tf_op jit(solution)/shard_map/ppermute | solution.py:174
  255.1 48.5 %collective-permute-start.9 = (bf16[384,768]{1,0:T(8,128)(2,1)S(1)}, bf16[384,768]{1,0:T(8,128)(2,1)S(1)}, u32[]{:S(2)}, u32[]{:S(2)}) collective-permute-start(bf16[384,768]{1,0:T(8,128)(2,1)S(1)} %get-tuple-element.82), channel_id=1, source_target_pairs={{0,2},{2,6},{4,0},{6,4},{1,3},{3,7},{5,1},{7,5},{8,10},{10,14},{12... | collective-permute-start | bytes 1769480 | tf_op jit(solution)/shard_map/ppermute | solution.py:174
  304.5 15.4 %collective-permute-done.15.refs_1_ = bf16[384,1024]{1,0:T(8,128)(2,1)S(1)} collective-permute-done((bf16[384,1024]{1,0:T(8,128)(2,1)S(1)}, bf16[384,1024]{1,0:T(8,128)(2,1)S(1)}, u32[]{:S(2)}, u32[]{:S(2)}) %collective-permute-start.15) | collective-permute-done | bytes 786464 | tf_op jit(solution)/shard_map/ppermute | solution.py:174
  325.4 20.2 %collective-permute-start.5 = (bf16[384,256]{1,0:T(8,128)(2,1)S(1)}, bf16[384,256]{1,0:T(8,128)(2,1)S(1)}, u32[]{:S(2)}, u32[]{:S(2)}) collective-permute-start(bf16[384,256]{1,0:T(8,128)(2,1)S(1)} %get-tuple-element.76), channel_id=1, source_target_pairs={{0,4},{2,0},{4,6},{6,2},{1,5},{3,1},{5,7},{7,3},{8,12},{10,8},{12,... | collective-permute-start | bytes 589832 | tf_op jit(solution)/shard_map/ppermute | solution.py:174
  354.2 3.6 %collective-permute-done.9.refs_1_ = bf16[384,768]{1,0:T(8,128)(2,1)S(1)} collective-permute-done((bf16[384,768]{1,0:T(8,128)(2,1)S(1)}, bf16[384,768]{1,0:T(8,128)(2,1)S(1)}, u32[]{:S(2)}, u32[]{:S(2)}) %collective-permute-start.9) | collective-permute-done | bytes 589856 | tf_op jit(solution)/shard_map/ppermute | solution.py:174
  (108 shorter events, 93.0 us)
Async XLA Ops:
  46.0 29.2 %collective-permute-start.42 = (bf16[384,512]{1,0:T(8,128)(2,1)S(1)}, bf16[384,512]{1,0:T(8,128)(2,1)S(1)}, u32[]{:S(2)}, u32[]{:S(2)}) collective-permute-start(bf16[384,512]{1,0:T(8,128)(2,1)S(1)} %get-tuple-element.118), channel_id=1, source_target_pairs={{0,8},{8,0},{16,24},{24,16},{1,9},{9,1},{17,25},{25,17},{2,10},{10... | collective-permute-start | bytes 1179656 | tf_op jit(solution)/shard_map/ppermute | solution.py:174
  73.4 45.8 %collective-permute-start.37 = (bf16[384,768]{1,0:T(8,128)(2,1)S(1)}, bf16[384,768]{1,0:T(8,128)(2,1)S(1)}, u32[]{:S(2)}, u32[]{:S(2)}) collective-permute-start(bf16[384,768]{1,0:T(8,128)(2,1)S(1)} %get-tuple-element.111), channel_id=1, source_target_pairs={{0,16},{8,24},{16,0},{24,8},{1,17},{9,25},{17,1},{25,9},{2,18},{10... | collective-permute-start | bytes 1769480 | tf_op jit(solution)/shard_map/ppermute | solution.py:174
  75.3 45.7 %collective-permute-start.38 = (bf16[384,768]{1,0:T(8,128)(2,1)S(1)}, bf16[384,768]{1,0:T(8,128)(2,1)S(1)}, u32[]{:S(2)}, u32[]{:S(2)}) collective-permute-start(bf16[384,768]{1,0:T(8,128)(2,1)S(1)} %get-tuple-element.112), channel_id=1, source_target_pairs={{0,24},{8,16},{16,8},{24,0},{1,25},{9,17},{17,9},{25,1},{2,26},{10... | collective-permute-start | bytes 1769480 | tf_op jit(solution)/shard_map/ppermute | solution.py:174
  87.2 62.7 %collective-permute-start.6 = (bf16[384,768]{1,0:T(8,128)(2,1)S(1)}, bf16[384,768]{1,0:T(8,128)(2,1)S(1)}, u32[]{:S(2)}, u32[]{:S(2)}) collective-permute-start(bf16[384,768]{1,0:T(8,128)(2,1)S(1)} %get-tuple-element.78), channel_id=1, source_target_pairs={{0,8},{8,0},{16,24},{24,16},{1,9},{9,1},{17,25},{25,17},{2,10},{10... | collective-permute-start | bytes 1769480 | tf_op jit(solution)/shard_map/ppermute | solution.py:174
  95.9 27.8 %collective-permute-start.19 = (bf16[384,384]{1,0:T(8,128)(2,1)S(1)}, bf16[384,384]{1,0:T(8,128)(2,1)S(1)}, u32[]{:S(2)}, u32[]{:S(2)}) collective-permute-start(bf16[384,384]{1,0:T(8,128)(2,1)S(1)} %collective-permute-done.18), channel_id=1, source_target_pairs={{0,8},{8,0},{16,24},{24,16},{1,9},{9,1},{17,25},{25,17},{2,10},{10... | collective-permute-start | bytes 884744 | tf_op jit(solution)/shard_map/ppermute | solution.py:174
  97.5 53.0 %collective-permute-start.7 = (bf16[384,768]{1,0:T(8,128)(2,1)S(1)}, bf16[384,768]{1,0:T(8,128)(2,1)S(1)}, u32[]{:S(2)}, u32[]{:S(2)}) collective-permute-start(bf16[384,768]{1,0:T(8,128)(2,1)S(1)} %get-tuple-element.79), channel_id=1, source_target_pairs={{0,16},{8,24},{16,0},{24,8},{1,17},{9,25},{17,1},{25,9},{2,18},{10... | collective-permute-start | bytes 1769480 | tf_op jit(solution)/shard_map/ppermute | solution.py:174
  121.0 27.6 %collective-permute-start.23 = (bf16[384,384]{1,0:T(8,128)(2,1)S(1)}, bf16[384,384]{1,0:T(8,128)(2,1)S(1)}, u32[]{:S(2)}, u32[]{:S(2)}) collective-permute-start(bf16[384,384]{1,0:T(8,128)(2,1)S(1)} %collective-permute-done.22), channel_id=1, source_target_pairs={{0,24},{8,16},{16,8},{24,0},{1,25},{9,17},{17,9},{25,1},{2,26},{10... | collective-permute-start | bytes 884744 | tf_op jit(solution)/shard_map/ppermute | solution.py:174
  123.7 28.4 %collective-permute-start.8 = (bf16[384,768]{1,0:T(8,128)(2,1)S(1)}, bf16[384,768]{1,0:T(8,128)(2,1)S(1)}, u32[]{:S(2)}, u32[]{:S(2)}) collective-permute-start(bf16[384,768]{1,0:T(8,128)(2,1)S(1)} %get-tuple-element.80), channel_id=1, source_target_pairs={{0,24},{8,16},{16,8},{24,0},{1,25},{9,17},{17,9},{25,1},{2,26},{10... | collective-permute-start | bytes 1769480 | tf_op jit(solution)/shard_map/ppermute | solution.py:174
  139.1 32.7 %collective-permute-start.45 = (bf16[384,512]{1,0:T(8,128)(2,1)S(1)}, bf16[384,512]{1,0:T(8,128)(2,1)S(1)}, u32[]{:S(2)}, u32[]{:S(2)}) collective-permute-start(bf16[384,512]{1,0:T(8,128)(2,1)S(1)} %get-tuple-element.122), channel_id=1, source_target_pairs={{0,2},{2,6},{4,0},{6,4},{1,3},{3,7},{5,1},{7,5},{8,10},{10,14},{12... | collective-permute-start | bytes 1179656 | tf_op jit(solution)/shard_map/ppermute | solution.py:174
  148.6 50.4 %collective-permute-start.12 = (bf16[384,1024]{1,0:T(8,128)(2,1)S(1)}, bf16[384,1024]{1,0:T(8,128)(2,1)S(1)}, u32[]{:S(2)}, u32[]{:S(2)}) collective-permute-start(bf16[384,1024]{1,0:T(8,128)(2,1)S(1)} %get-tuple-element.86), channel_id=1, source_target_pairs={{0,8},{8,0},{16,24},{24,16},{1,9},{9,1},{17,25},{25,17},{2,10},{10... | collective-permute-start | bytes 2359304 | tf_op jit(solution)/shard_map/ppermute | solution.py:174
  149.8 49.2 %collective-permute-start.13 = (bf16[384,1024]{1,0:T(8,128)(2,1)S(1)}, bf16[384,1024]{1,0:T(8,128)(2,1)S(1)}, u32[]{:S(2)}, u32[]{:S(2)}) collective-permute-start(bf16[384,1024]{1,0:T(8,128)(2,1)S(1)} %get-tuple-element.87), channel_id=1, source_target_pairs={{0,16},{8,24},{16,0},{24,8},{1,17},{9,25},{17,1},{25,9},{2,18},{10... | collective-permute-start | bytes 2359304 | tf_op jit(solution)/shard_map/ppermute | solution.py:174
  150.5 48.6 %collective-permute-start.14 = (bf16[384,1024]{1,0:T(8,128)(2,1)S(1)}, bf16[384,1024]{1,0:T(8,128)(2,1)S(1)}, u32[]{:S(2)}, u32[]{:S(2)}) collective-permute-start(bf16[384,1024]{1,0:T(8,128)(2,1)S(1)} %get-tuple-element.88), channel_id=1, source_target_pairs={{0,24},{8,16},{16,8},{24,0},{1,25},{9,17},{17,9},{25,1},{2,26},{10... | collective-permute-start | bytes 2359304 | tf_op jit(solution)/shard_map/ppermute | solution.py:174
  172.8 48.7 %collective-permute-start.39 = (bf16[384,768]{1,0:T(8,128)(2,1)S(1)}, bf16[384,768]{1,0:T(8,128)(2,1)S(1)}, u32[]{:S(2)}, u32[]{:S(2)}) collective-permute-start(bf16[384,768]{1,0:T(8,128)(2,1)S(1)} %get-tuple-element.114), channel_id=1, source_target_pairs={{0,2},{2,6},{4,0},{6,4},{1,3},{3,7},{5,1},{7,5},{8,10},{10,14},{12... | collective-permute-start | bytes 1769480 | tf_op jit(solution)/shard_map/ppermute | solution.py:174
  198.0 30.4 %collective-permute-start.40 = (bf16[384,768]{1,0:T(8,128)(2,1)S(1)}, bf16[384,768]{1,0:T(8,128)(2,1)S(1)}, u32[]{:S(2)}, u32[]{:S(2)}) collective-permute-start(bf16[384,768]{1,0:T(8,128)(2,1)S(1)} %get-tuple-element.115), channel_id=1, source_target_pairs={{0,6},{2,4},{4,2},{6,0},{1,7},{3,5},{5,3},{7,1},{8,14},{10,12},{12... | collective-permute-start | bytes 1769480 | tf_op jit(solution)/shard_map/ppermute | solution.py:174
  205.7 49.3 %collective-permute-start.41 = (bf16[384,768]{1,0:T(8,128)(2,1)S(1)}, bf16[384,768]{1,0:T(8,128)(2,1)S(1)}, u32[]{:S(2)}, u32[]{:S(2)}) collective-permute-start(bf16[384,768]{1,0:T(8,128)(2,1)S(1)} %get-tuple-element.116), channel_id=1, source_target_pairs={{0,4},{2,0},{4,6},{6,2},{1,5},{3,1},{5,7},{7,3},{8,12},{10,8},{12,... | collective-permute-start | bytes 1769480 | tf_op jit(solution)/shard_map/ppermute | solution.py:174
  209.0 46.1 %collective-permute-start.10 = (bf16[384,768]{1,0:T(8,128)(2,1)S(1)}, bf16[384,768]{1,0:T(8,128)(2,1)S(1)}, u32[]{:S(2)}, u32[]{:S(2)}) collective-permute-start(bf16[384,768]{1,0:T(8,128)(2,1)S(1)} %get-tuple-element.83), channel_id=1, source_target_pairs={{0,6},{2,4},{4,2},{6,0},{1,7},{3,5},{5,3},{7,1},{8,14},{10,12},{12... | collective-permute-start | bytes 1769480 | tf_op jit(solution)/shard_map/ppermute | solution.py:174
  213.9 106.0 %collective-permute-start.15 = (bf16[384,1024]{1,0:T(8,128)(2,1)S(1)}, bf16[384,1024]{1,0:T(8,128)(2,1)S(1)}, u32[]{:S(2)}, u32[]{:S(2)}) collective-permute-start(bf16[384,1024]{1,0:T(8,128)(2,1)S(1)} %get-tuple-element.90), channel_id=1, source_target_pairs={{0,2},{2,6},{4,0},{6,4},{1,3},{3,7},{5,1},{7,5},{8,10},{10,14},{12... | collective-permute-start | bytes 2359304 | tf_op jit(solution)/shard_map/ppermute | solution.py:174
  221.5 101.1 %collective-permute-start.16 = (bf16[384,1024]{1,0:T(8,128)(2,1)S(1)}, bf16[384,1024]{1,0:T(8,128)(2,1)S(1)}, u32[]{:S(2)}, u32[]{:S(2)}) collective-permute-start(bf16[384,1024]{1,0:T(8,128)(2,1)S(1)} %get-tuple-element.91), channel_id=1, source_target_pairs={{0,6},{2,4},{4,2},{6,0},{1,7},{3,5},{5,3},{7,1},{8,14},{10,12},{12... | collective-permute-start | bytes 2359304 | tf_op jit(solution)/shard_map/ppermute | solution.py:174
  228.4 97.1 %collective-permute-start.17 = (bf16[384,1024]{1,0:T(8,128)(2,1)S(1)}, bf16[384,1024]{1,0:T(8,128)(2,1)S(1)}, u32[]{:S(2)}, u32[]{:S(2)}) collective-permute-start(bf16[384,1024]{1,0:T(8,128)(2,1)S(1)} %get-tuple-element.92), channel_id=1, source_target_pairs={{0,4},{2,0},{4,6},{6,2},{1,5},{3,1},{5,7},{7,3},{8,12},{10,8},{12,... | collective-permute-start | bytes 2359304 | tf_op jit(solution)/shard_map/ppermute | solution.py:174
  255.1 99.1 %collective-permute-start.11 = (bf16[384,768]{1,0:T(8,128)(2,1)S(1)}, bf16[384,768]{1,0:T(8,128)(2,1)S(1)}, u32[]{:S(2)}, u32[]{:S(2)}) collective-permute-start(bf16[384,768]{1,0:T(8,128)(2,1)S(1)} %get-tuple-element.84), channel_id=1, source_target_pairs={{0,4},{2,0},{4,6},{6,2},{1,5},{3,1},{5,7},{7,3},{8,12},{10,8},{12,... | collective-permute-start | bytes 1769480 | tf_op jit(solution)/shard_map/ppermute | solution.py:174
  255.1 102.8 %collective-permute-start.9 = (bf16[384,768]{1,0:T(8,128)(2,1)S(1)}, bf16[384,768]{1,0:T(8,128)(2,1)S(1)}, u32[]{:S(2)}, u32[]{:S(2)}) collective-permute-start(bf16[384,768]{1,0:T(8,128)(2,1)S(1)} %get-tuple-element.82), channel_id=1, source_target_pairs={{0,2},{2,6},{4,0},{6,4},{1,3},{3,7},{5,1},{7,5},{8,10},{10,14},{12... | collective-permute-start | bytes 1769480 | tf_op jit(solution)/shard_map/ppermute | solution.py:174
  319.9 40.9 %collective-permute-start.3 = (bf16[384,256]{1,0:T(8,128)(2,1)S(1)}, bf16[384,256]{1,0:T(8,128)(2,1)S(1)}, u32[]{:S(2)}, u32[]{:S(2)}) collective-permute-start(bf16[384,256]{1,0:T(8,128)(2,1)S(1)} %get-tuple-element.74), channel_id=1, source_target_pairs={{0,2},{2,6},{4,0},{6,4},{1,3},{3,7},{5,1},{7,5},{8,10},{10,14},{12... | collective-permute-start | bytes 589832 | tf_op jit(solution)/shard_map/ppermute | solution.py:174
  322.6 38.2 %collective-permute-start.4 = (bf16[384,256]{1,0:T(8,128)(2,1)S(1)}, bf16[384,256]{1,0:T(8,128)(2,1)S(1)}, u32[]{:S(2)}, u32[]{:S(2)}) collective-permute-start(bf16[384,256]{1,0:T(8,128)(2,1)S(1)} %get-tuple-element.75), channel_id=1, source_target_pairs={{0,6},{2,4},{4,2},{6,0},{1,7},{3,5},{5,3},{7,1},{8,14},{10,12},{12... | collective-permute-start | bytes 589832 | tf_op jit(solution)/shard_map/ppermute | solution.py:174
  325.4 35.3 %collective-permute-start.5 = (bf16[384,256]{1,0:T(8,128)(2,1)S(1)}, bf16[384,256]{1,0:T(8,128)(2,1)S(1)}, u32[]{:S(2)}, u32[]{:S(2)}) collective-permute-start(bf16[384,256]{1,0:T(8,128)(2,1)S(1)} %get-tuple-element.76), channel_id=1, source_target_pairs={{0,4},{2,0},{4,6},{6,2},{1,5},{3,1},{5,7},{7,3},{8,12},{10,8},{12,... | collective-permute-start | bytes 589832 | tf_op jit(solution)/shard_map/ppermute | solution.py:174
  (30 other events, 465.8 us)

commit v7 on v6

--- a/solution.py
+++ b/solution.py
@@ -84,17 +84,22 @@
     tile = tile_of(offset, width)
     rows = weight.shape[1]
     block_rows = rows // count
+    lanes = block_rows % 128 == 0
 
     def kernel(owned_ref, weight_ref, *refs):
-        outs, turned = refs[:-1], refs[-1]
+        outs, turned = refs[:count], refs[count:]
         me, mine, replica = position()
-        turned[...] = weight_ref[...].T
+        if not lanes:
+            turned[0][...] = weight_ref[...].T
         columns = pl.ds(pl.multiple_of(pl.program_id(0) * tile, 128), tile)
         for step, out in enumerate(outs):
             row, column = me ^ step, partner_of("tp", mine, step, count)
             owners = [(line, column) if first else (row, line) for line in range(count)]
             span = sum(span_of(owned_ref, me, row, column, replica, sizes) for row, column in owners)
-            out[:, columns] = turned[pl.ds(pl.multiple_of(span * block_rows, 16), block_rows), :]
+            if lanes:
+                out[:, columns] = weight_ref[:, pl.ds(pl.multiple_of(span * block_rows, 128), block_rows)].T
+            else:
+                out[:, columns] = turned[0][pl.ds(pl.multiple_of(span * block_rows, 16), block_rows), :]
 
     return pl.pallas_call(
         kernel,
@@ -102,7 +107,7 @@
         in_specs=[SCALARS, pl.BlockSpec((tile, rows), lambda step: (offset // tile + step, 0))],
         out_specs=[WHOLE] * count,
         out_shape=[pltpu.VMEM((block_rows, width), weight.dtype)] * count,
-        scratch_shapes=[pltpu.VMEM((rows, tile), weight.dtype)],
+        scratch_shapes=[] if lanes else [pltpu.VMEM((rows, tile), weight.dtype)],
         compiler_params=PARAMS,
         name="pick_rows",
     )(owned, weight)

time: 364 us -> 364 us (level)
  no operation moved by 1% of the time
where the time goes in v7:
time: 364 us; the launch traced here: 362 us
  starting transfers between devices  199 us (55%)
  waiting for transfers between devices  127 us (35%)
  Pallas kernels  35.6 us (10%)
    ppermute x54, starting transfers between devices, exchange(): moved[step] = lax.ppermute(pieces[step], axis, pairs)  199 us
    ppermute x54, waiting for transfers between devices, exchange(): moved[step] = lax.ppermute(pieces[step], axis, pairs)  127 us
    pallas_call x8, Pallas kernels, pick_rows(): pl.pallas_call(kernel, grid=(width // tile,), in_specs=[SCALARS, pl.Block...  17.2 us
    pallas_call x8, Pallas kernels, place(): pl.pallas_call(kernel, in_specs=[SCALARS] * len(table) + [WHOLE] * count...  10.9 us
    pallas_call x8, Pallas kernels, choose(): pl.pallas_call(kernel, in_specs=[SCALARS] + [WHOLE] * count, out_specs=[W...  7.52 us
  transfers between devices with their start and end apart: 54, of which 16 were waited for; matrix products, arithmetic and copies ran while one was open for 0% of the time, Pallas kernels for 9%

profile of v7, /device:TPU:0, one launch (start us, length us, event | category | flops | bytes accessed | tf_op | source)
XLA Modules:
  0.0 361.6 jit_solution(9362683339136211212)
XLA Ops:
  1.2 3.1 collective-permute-start.27
  26.3 4.6 %collective-permute-done.30.refs_2_ = bf16[384,128]{1,0:T(8,128)(2,1)S(1)} collective-permute-done((bf16[384,128]{1,0:T(8,128)(2,1)S(1)}, bf16[384,128]{1,0:T(8,128)(2,1)S(1)}, u32[]{:S(2)}, u32[]{:S(2)}) %collective-permute-start.30) | collective-permute-done | bytes 98336 | tf_op jit(solution)/shard_map/ppermute | solution.py:179
  30.8 5.2 %collective-permute-start.18 = (bf16[384,384]{1,0:T(8,128)(2,1)S(1)}, bf16[384,384]{1,0:T(8,128)(2,1)S(1)}, u32[]{:S(2)}, u32[]{:S(2)}) collective-permute-start(bf16[384,384]{1,0:T(8,128)(2,1)S(1)} %get-tuple-element.94), channel_id=1, source_target_pairs={{0,2},{2,6},{4,0},{6,4},{1,3},{3,7},{5,1},{7,5},{8,10},{10,14},{12... | collective-permute-start | bytes 884744 | tf_op jit(solution)/shard_map/ppermute | solution.py:179
  50.3 8.8 %collective-permute-start.52 = (bf16[384,256]{1,0:T(8,128)(2,1)S(1)}, bf16[384,256]{1,0:T(8,128)(2,1)S(1)}, u32[]{:S(2)}, u32[]{:S(2)}) collective-permute-start(bf16[384,256]{1,0:T(8,128)(2,1)S(1)} %get-tuple-element.131), channel_id=1, source_target_pairs={{0,6},{2,4},{4,2},{6,0},{1,7},{3,5},{5,3},{7,1},{8,14},{10,12},{12... | collective-permute-start | bytes 589832 | tf_op jit(solution)/shard_map/ppermute | solution.py:179
  59.1 7.2 %collective-permute-start.53 = (bf16[384,256]{1,0:T(8,128)(2,1)S(1)}, bf16[384,256]{1,0:T(8,128)(2,1)S(1)}, u32[]{:S(2)}, u32[]{:S(2)}) collective-permute-start(bf16[384,256]{1,0:T(8,128)(2,1)S(1)} %get-tuple-element.132), channel_id=1, source_target_pairs={{0,4},{2,0},{4,6},{6,2},{1,5},{3,1},{5,7},{7,3},{8,12},{10,8},{12,... | collective-permute-start | bytes 589832 | tf_op jit(solution)/shard_map/ppermute | solution.py:179
  76.3 2.9 pick_rows.9
  79.1 7.9 %collective-permute-done.43.refs_2_ = bf16[384,512]{1,0:T(8,128)(2,1)S(1)} collective-permute-done((bf16[384,512]{1,0:T(8,128)(2,1)S(1)}, bf16[384,512]{1,0:T(8,128)(2,1)S(1)}, u32[]{:S(2)}, u32[]{:S(2)}) %collective-permute-start.43) | collective-permute-done | bytes 393248 | tf_op jit(solution)/shard_map/ppermute | solution.py:179
  87.8 8.0 %collective-permute-done.44.refs_3_ = bf16[384,512]{1,0:T(8,128)(2,1)S(1)} collective-permute-done((bf16[384,512]{1,0:T(8,128)(2,1)S(1)}, bf16[384,512]{1,0:T(8,128)(2,1)S(1)}, u32[]{:S(2)}, u32[]{:S(2)}) %collective-permute-start.44) | collective-permute-done | bytes 393248 | tf_op jit(solution)/shard_map/ppermute | solution.py:179
  99.3 19.7 %collective-permute-done.37.refs_2_ = bf16[384,768]{1,0:T(8,128)(2,1)S(1)} collective-permute-done((bf16[384,768]{1,0:T(8,128)(2,1)S(1)}, bf16[384,768]{1,0:T(8,128)(2,1)S(1)}, u32[]{:S(2)}, u32[]{:S(2)}) %collective-permute-start.37) | collective-permute-done | bytes 589856 | tf_op jit(solution)/shard_map/ppermute | solution.py:179
  125.6 13.4 %collective-permute-done.21.refs_2_ = bf16[384,384]{1,0:T(8,128)(2,1)S(1)} collective-permute-done((bf16[384,384]{1,0:T(8,128)(2,1)S(1)}, bf16[384,384]{1,0:T(8,128)(2,1)S(1)}, u32[]{:S(2)}, u32[]{:S(2)}) %collective-permute-start.21) | collective-permute-done | bytes 294944 | tf_op jit(solution)/shard_map/ppermute | solution.py:179
  139.0 6.0 %collective-permute-start.45 = (bf16[384,512]{1,0:T(8,128)(2,1)S(1)}, bf16[384,512]{1,0:T(8,128)(2,1)S(1)}, u32[]{:S(2)}, u32[]{:S(2)}) collective-permute-start(bf16[384,512]{1,0:T(8,128)(2,1)S(1)} %get-tuple-element.122), channel_id=1, source_target_pairs={{0,2},{2,6},{4,0},{6,4},{1,3},{3,7},{5,1},{7,5},{8,10},{10,14},{12... | collective-permute-start | bytes 1179656 | tf_op jit(solution)/shard_map/ppermute | solution.py:179
  145.0 3.3 pick_rows.10
  154.6 17.4 %collective-permute-done.45.refs_1_ = bf16[384,512]{1,0:T(8,128)(2,1)S(1)} collective-permute-done((bf16[384,512]{1,0:T(8,128)(2,1)S(1)}, bf16[384,512]{1,0:T(8,128)(2,1)S(1)}, u32[]{:S(2)}, u32[]{:S(2)}) %collective-permute-start.45) | collective-permute-done | bytes 393248 | tf_op jit(solution)/shard_map/ppermute | solution.py:179
  173.0 7.5 %collective-permute-start.39 = (bf16[384,768]{1,0:T(8,128)(2,1)S(1)}, bf16[384,768]{1,0:T(8,128)(2,1)S(1)}, u32[]{:S(2)}, u32[]{:S(2)}) collective-permute-start(bf16[384,768]{1,0:T(8,128)(2,1)S(1)} %get-tuple-element.114), channel_id=1, source_target_pairs={{0,2},{2,6},{4,0},{6,4},{1,3},{3,7},{5,1},{7,5},{8,10},{10,14},{12... | collective-permute-start | bytes 1769480 | tf_op jit(solution)/shard_map/ppermute | solution.py:179
  180.4 17.2 %collective-permute-done.47.refs_3_ = bf16[384,512]{1,0:T(8,128)(2,1)S(1)} collective-permute-done((bf16[384,512]{1,0:T(8,128)(2,1)S(1)}, bf16[384,512]{1,0:T(8,128)(2,1)S(1)}, u32[]{:S(2)}, u32[]{:S(2)}) %collective-permute-start.47) | collective-permute-done | bytes 393248 | tf_op jit(solution)/shard_map/ppermute | solution.py:179
  198.8 3.4 collective-permute-start.26
  208.7 3.8 %collective-permute-start.10 = (bf16[384,768]{1,0:T(8,128)(2,1)S(1)}, bf16[384,768]{1,0:T(8,128)(2,1)S(1)}, u32[]{:S(2)}, u32[]{:S(2)}) collective-permute-start(bf16[384,768]{1,0:T(8,128)(2,1)S(1)} %get-tuple-element.83), channel_id=1, source_target_pairs={{0,6},{2,4},{4,2},{6,0},{1,7},{3,5},{5,3},{7,1},{8,14},{10,12},{12... | collective-permute-start | bytes 1769480 | tf_op jit(solution)/shard_map/ppermute | solution.py:179
  213.6 8.5 %collective-permute-done.39.refs_1_ = bf16[384,768]{1,0:T(8,128)(2,1)S(1)} collective-permute-done((bf16[384,768]{1,0:T(8,128)(2,1)S(1)}, bf16[384,768]{1,0:T(8,128)(2,1)S(1)}, u32[]{:S(2)}, u32[]{:S(2)}) %collective-permute-start.39) | collective-permute-done | bytes 589856 | tf_op jit(solution)/shard_map/ppermute | solution.py:179
  222.1 6.8 %collective-permute-start.16 = (bf16[384,1024]{1,0:T(8,128)(2,1)S(1)}, bf16[384,1024]{1,0:T(8,128)(2,1)S(1)}, u32[]{:S(2)}, u32[]{:S(2)}) collective-permute-start(bf16[384,1024]{1,0:T(8,128)(2,1)S(1)} %get-tuple-element.91), channel_id=1, source_target_pairs={{0,6},{2,4},{4,2},{6,0},{1,7},{3,5},{5,3},{7,1},{8,14},{10,12},{12... | collective-permute-start | bytes 2359304 | tf_op jit(solution)/shard_map/ppermute | solution.py:179
  229.0 46.4 %collective-permute-start.17 = (bf16[384,1024]{1,0:T(8,128)(2,1)S(1)}, bf16[384,1024]{1,0:T(8,128)(2,1)S(1)}, u32[]{:S(2)}, u32[]{:S(2)}) collective-permute-start(bf16[384,1024]{1,0:T(8,128)(2,1)S(1)} %get-tuple-element.92), channel_id=1, source_target_pairs={{0,4},{2,0},{4,6},{6,2},{1,5},{3,1},{5,7},{7,3},{8,12},{10,8},{12,... | collective-permute-start | bytes 2359304 | tf_op jit(solution)/shard_map/ppermute | solution.py:179
  275.4 28.4 %collective-permute-start.9 = (bf16[384,768]{1,0:T(8,128)(2,1)S(1)}, bf16[384,768]{1,0:T(8,128)(2,1)S(1)}, u32[]{:S(2)}, u32[]{:S(2)}) collective-permute-start(bf16[384,768]{1,0:T(8,128)(2,1)S(1)} %get-tuple-element.82), channel_id=1, source_target_pairs={{0,2},{2,6},{4,0},{6,4},{1,3},{3,7},{5,1},{7,5},{8,10},{10,14},{12... | collective-permute-start | bytes 1769480 | tf_op jit(solution)/shard_map/ppermute | solution.py:179
  304.7 15.3 %collective-permute-done.15.refs_1_ = bf16[384,1024]{1,0:T(8,128)(2,1)S(1)} collective-permute-done((bf16[384,1024]{1,0:T(8,128)(2,1)S(1)}, bf16[384,1024]{1,0:T(8,128)(2,1)S(1)}, u32[]{:S(2)}, u32[]{:S(2)}) %collective-permute-start.15) | collective-permute-done | bytes 786464 | tf_op jit(solution)/shard_map/ppermute | solution.py:179
  325.6 20.2 %collective-permute-start.5 = (bf16[384,256]{1,0:T(8,128)(2,1)S(1)}, bf16[384,256]{1,0:T(8,128)(2,1)S(1)}, u32[]{:S(2)}, u32[]{:S(2)}) collective-permute-start(bf16[384,256]{1,0:T(8,128)(2,1)S(1)} %get-tuple-element.76), channel_id=1, source_target_pairs={{0,4},{2,0},{4,6},{6,2},{1,5},{3,1},{5,7},{7,3},{8,12},{10,8},{12,... | collective-permute-start | bytes 589832 | tf_op jit(solution)/shard_map/ppermute | solution.py:179
  354.4 3.6 %collective-permute-done.9.refs_1_ = bf16[384,768]{1,0:T(8,128)(2,1)S(1)} collective-permute-done((bf16[384,768]{1,0:T(8,128)(2,1)S(1)}, bf16[384,768]{1,0:T(8,128)(2,1)S(1)}, u32[]{:S(2)}, u32[]{:S(2)}) %collective-permute-start.9) | collective-permute-done | bytes 589856 | tf_op jit(solution)/shard_map/ppermute | solution.py:179
  (108 shorter events, 92.6 us)
Async XLA Ops:
  45.9 29.2 %collective-permute-start.42 = (bf16[384,512]{1,0:T(8,128)(2,1)S(1)}, bf16[384,512]{1,0:T(8,128)(2,1)S(1)}, u32[]{:S(2)}, u32[]{:S(2)}) collective-permute-start(bf16[384,512]{1,0:T(8,128)(2,1)S(1)} %get-tuple-element.118), channel_id=1, source_target_pairs={{0,8},{8,0},{16,24},{24,16},{1,9},{9,1},{17,25},{25,17},{2,10},{10... | collective-permute-start | bytes 1179656 | tf_op jit(solution)/shard_map/ppermute | solution.py:179
  73.3 45.8 %collective-permute-start.37 = (bf16[384,768]{1,0:T(8,128)(2,1)S(1)}, bf16[384,768]{1,0:T(8,128)(2,1)S(1)}, u32[]{:S(2)}, u32[]{:S(2)}) collective-permute-start(bf16[384,768]{1,0:T(8,128)(2,1)S(1)} %get-tuple-element.111), channel_id=1, source_target_pairs={{0,16},{8,24},{16,0},{24,8},{1,17},{9,25},{17,1},{25,9},{2,18},{10... | collective-permute-start | bytes 1769480 | tf_op jit(solution)/shard_map/ppermute | solution.py:179
  75.2 45.7 %collective-permute-start.38 = (bf16[384,768]{1,0:T(8,128)(2,1)S(1)}, bf16[384,768]{1,0:T(8,128)(2,1)S(1)}, u32[]{:S(2)}, u32[]{:S(2)}) collective-permute-start(bf16[384,768]{1,0:T(8,128)(2,1)S(1)} %get-tuple-element.112), channel_id=1, source_target_pairs={{0,24},{8,16},{16,8},{24,0},{1,25},{9,17},{17,9},{25,1},{2,26},{10... | collective-permute-start | bytes 1769480 | tf_op jit(solution)/shard_map/ppermute | solution.py:179
  87.1 62.4 %collective-permute-start.6 = (bf16[384,768]{1,0:T(8,128)(2,1)S(1)}, bf16[384,768]{1,0:T(8,128)(2,1)S(1)}, u32[]{:S(2)}, u32[]{:S(2)}) collective-permute-start(bf16[384,768]{1,0:T(8,128)(2,1)S(1)} %get-tuple-element.78), channel_id=1, source_target_pairs={{0,8},{8,0},{16,24},{24,16},{1,9},{9,1},{17,25},{25,17},{2,10},{10... | collective-permute-start | bytes 1769480 | tf_op jit(solution)/shard_map/ppermute | solution.py:179
  95.8 27.8 %collective-permute-start.19 = (bf16[384,384]{1,0:T(8,128)(2,1)S(1)}, bf16[384,384]{1,0:T(8,128)(2,1)S(1)}, u32[]{:S(2)}, u32[]{:S(2)}) collective-permute-start(bf16[384,384]{1,0:T(8,128)(2,1)S(1)} %collective-permute-done.18), channel_id=1, source_target_pairs={{0,8},{8,0},{16,24},{24,16},{1,9},{9,1},{17,25},{25,17},{2,10},{10... | collective-permute-start | bytes 884744 | tf_op jit(solution)/shard_map/ppermute | solution.py:179
  97.4 52.8 %collective-permute-start.7 = (bf16[384,768]{1,0:T(8,128)(2,1)S(1)}, bf16[384,768]{1,0:T(8,128)(2,1)S(1)}, u32[]{:S(2)}, u32[]{:S(2)}) collective-permute-start(bf16[384,768]{1,0:T(8,128)(2,1)S(1)} %get-tuple-element.79), channel_id=1, source_target_pairs={{0,16},{8,24},{16,0},{24,8},{1,17},{9,25},{17,1},{25,9},{2,18},{10... | collective-permute-start | bytes 1769480 | tf_op jit(solution)/shard_map/ppermute | solution.py:179
  120.9 27.4 %collective-permute-start.23 = (bf16[384,384]{1,0:T(8,128)(2,1)S(1)}, bf16[384,384]{1,0:T(8,128)(2,1)S(1)}, u32[]{:S(2)}, u32[]{:S(2)}) collective-permute-start(bf16[384,384]{1,0:T(8,128)(2,1)S(1)} %collective-permute-done.22), channel_id=1, source_target_pairs={{0,24},{8,16},{16,8},{24,0},{1,25},{9,17},{17,9},{25,1},{2,26},{10... | collective-permute-start | bytes 884744 | tf_op jit(solution)/shard_map/ppermute | solution.py:179
  123.6 28.2 %collective-permute-start.8 = (bf16[384,768]{1,0:T(8,128)(2,1)S(1)}, bf16[384,768]{1,0:T(8,128)(2,1)S(1)}, u32[]{:S(2)}, u32[]{:S(2)}) collective-permute-start(bf16[384,768]{1,0:T(8,128)(2,1)S(1)} %get-tuple-element.80), channel_id=1, source_target_pairs={{0,24},{8,16},{16,8},{24,0},{1,25},{9,17},{17,9},{25,1},{2,26},{10... | collective-permute-start | bytes 1769480 | tf_op jit(solution)/shard_map/ppermute | solution.py:179
  139.0 33.0 %collective-permute-start.45 = (bf16[384,512]{1,0:T(8,128)(2,1)S(1)}, bf16[384,512]{1,0:T(8,128)(2,1)S(1)}, u32[]{:S(2)}, u32[]{:S(2)}) collective-permute-start(bf16[384,512]{1,0:T(8,128)(2,1)S(1)} %get-tuple-element.122), channel_id=1, source_target_pairs={{0,2},{2,6},{4,0},{6,4},{1,3},{3,7},{5,1},{7,5},{8,10},{10,14},{12... | collective-permute-start | bytes 1179656 | tf_op jit(solution)/shard_map/ppermute | solution.py:179
  148.3 50.4 %collective-permute-start.12 = (bf16[384,1024]{1,0:T(8,128)(2,1)S(1)}, bf16[384,1024]{1,0:T(8,128)(2,1)S(1)}, u32[]{:S(2)}, u32[]{:S(2)}) collective-permute-start(bf16[384,1024]{1,0:T(8,128)(2,1)S(1)} %get-tuple-element.86), channel_id=1, source_target_pairs={{0,8},{8,0},{16,24},{24,16},{1,9},{9,1},{17,25},{25,17},{2,10},{10... | collective-permute-start | bytes 2359304 | tf_op jit(solution)/shard_map/ppermute | solution.py:179
  149.5 49.2 %collective-permute-start.13 = (bf16[384,1024]{1,0:T(8,128)(2,1)S(1)}, bf16[384,1024]{1,0:T(8,128)(2,1)S(1)}, u32[]{:S(2)}, u32[]{:S(2)}) collective-permute-start(bf16[384,1024]{1,0:T(8,128)(2,1)S(1)} %get-tuple-element.87), channel_id=1, source_target_pairs={{0,16},{8,24},{16,0},{24,8},{1,17},{9,25},{17,1},{25,9},{2,18},{10... | collective-permute-start | bytes 2359304 | tf_op jit(solution)/shard_map/ppermute | solution.py:179
  150.2 48.6 %collective-permute-start.14 = (bf16[384,1024]{1,0:T(8,128)(2,1)S(1)}, bf16[384,1024]{1,0:T(8,128)(2,1)S(1)}, u32[]{:S(2)}, u32[]{:S(2)}) collective-permute-start(bf16[384,1024]{1,0:T(8,128)(2,1)S(1)} %get-tuple-element.88), channel_id=1, source_target_pairs={{0,24},{8,16},{16,8},{24,0},{1,25},{9,17},{17,9},{25,1},{2,26},{10... | collective-permute-start | bytes 2359304 | tf_op jit(solution)/shard_map/ppermute | solution.py:179
  173.0 49.2 %collective-permute-start.39 = (bf16[384,768]{1,0:T(8,128)(2,1)S(1)}, bf16[384,768]{1,0:T(8,128)(2,1)S(1)}, u32[]{:S(2)}, u32[]{:S(2)}) collective-permute-start(bf16[384,768]{1,0:T(8,128)(2,1)S(1)} %get-tuple-element.114), channel_id=1, source_target_pairs={{0,2},{2,6},{4,0},{6,4},{1,3},{3,7},{5,1},{7,5},{8,10},{10,14},{12... | collective-permute-start | bytes 1769480 | tf_op jit(solution)/shard_map/ppermute | solution.py:179
  197.7 31.3 %collective-permute-start.40 = (bf16[384,768]{1,0:T(8,128)(2,1)S(1)}, bf16[384,768]{1,0:T(8,128)(2,1)S(1)}, u32[]{:S(2)}, u32[]{:S(2)}) collective-permute-start(bf16[384,768]{1,0:T(8,128)(2,1)S(1)} %get-tuple-element.115), channel_id=1, source_target_pairs={{0,6},{2,4},{4,2},{6,0},{1,7},{3,5},{5,3},{7,1},{8,14},{10,12},{12... | collective-permute-start | bytes 1769480 | tf_op jit(solution)/shard_map/ppermute | solution.py:179
  205.4 69.9 %collective-permute-start.41 = (bf16[384,768]{1,0:T(8,128)(2,1)S(1)}, bf16[384,768]{1,0:T(8,128)(2,1)S(1)}, u32[]{:S(2)}, u32[]{:S(2)}) collective-permute-start(bf16[384,768]{1,0:T(8,128)(2,1)S(1)} %get-tuple-element.116), channel_id=1, source_target_pairs={{0,4},{2,0},{4,6},{6,2},{1,5},{3,1},{5,7},{7,3},{8,12},{10,8},{12,... | collective-permute-start | bytes 1769480 | tf_op jit(solution)/shard_map/ppermute | solution.py:179
  208.7 66.7 %collective-permute-start.10 = (bf16[384,768]{1,0:T(8,128)(2,1)S(1)}, bf16[384,768]{1,0:T(8,128)(2,1)S(1)}, u32[]{:S(2)}, u32[]{:S(2)}) collective-permute-start(bf16[384,768]{1,0:T(8,128)(2,1)S(1)} %get-tuple-element.83), channel_id=1, source_target_pairs={{0,6},{2,4},{4,2},{6,0},{1,7},{3,5},{5,3},{7,1},{8,14},{10,12},{12... | collective-permute-start | bytes 1769480 | tf_op jit(solution)/shard_map/ppermute | solution.py:179
  213.6 106.5 %collective-permute-start.15 = (bf16[384,1024]{1,0:T(8,128)(2,1)S(1)}, bf16[384,1024]{1,0:T(8,128)(2,1)S(1)}, u32[]{:S(2)}, u32[]{:S(2)}) collective-permute-start(bf16[384,1024]{1,0:T(8,128)(2,1)S(1)} %get-tuple-element.90), channel_id=1, source_target_pairs={{0,2},{2,6},{4,0},{6,4},{1,3},{3,7},{5,1},{7,5},{8,10},{10,14},{12... | collective-permute-start | bytes 2359304 | tf_op jit(solution)/shard_map/ppermute | solution.py:179
  222.1 100.6 %collective-permute-start.16 = (bf16[384,1024]{1,0:T(8,128)(2,1)S(1)}, bf16[384,1024]{1,0:T(8,128)(2,1)S(1)}, u32[]{:S(2)}, u32[]{:S(2)}) collective-permute-start(bf16[384,1024]{1,0:T(8,128)(2,1)S(1)} %get-tuple-element.91), channel_id=1, source_target_pairs={{0,6},{2,4},{4,2},{6,0},{1,7},{3,5},{5,3},{7,1},{8,14},{10,12},{12... | collective-permute-start | bytes 2359304 | tf_op jit(solution)/shard_map/ppermute | solution.py:179
  229.0 96.6 %collective-permute-start.17 = (bf16[384,1024]{1,0:T(8,128)(2,1)S(1)}, bf16[384,1024]{1,0:T(8,128)(2,1)S(1)}, u32[]{:S(2)}, u32[]{:S(2)}) collective-permute-start(bf16[384,1024]{1,0:T(8,128)(2,1)S(1)} %get-tuple-element.92), channel_id=1, source_target_pairs={{0,4},{2,0},{4,6},{6,2},{1,5},{3,1},{5,7},{7,3},{8,12},{10,8},{12,... | collective-permute-start | bytes 2359304 | tf_op jit(solution)/shard_map/ppermute | solution.py:179
  275.3 79.0 %collective-permute-start.11 = (bf16[384,768]{1,0:T(8,128)(2,1)S(1)}, bf16[384,768]{1,0:T(8,128)(2,1)S(1)}, u32[]{:S(2)}, u32[]{:S(2)}) collective-permute-start(bf16[384,768]{1,0:T(8,128)(2,1)S(1)} %get-tuple-element.84), channel_id=1, source_target_pairs={{0,4},{2,0},{4,6},{6,2},{1,5},{3,1},{5,7},{7,3},{8,12},{10,8},{12,... | collective-permute-start | bytes 1769480 | tf_op jit(solution)/shard_map/ppermute | solution.py:179
  275.4 82.6 %collective-permute-start.9 = (bf16[384,768]{1,0:T(8,128)(2,1)S(1)}, bf16[384,768]{1,0:T(8,128)(2,1)S(1)}, u32[]{:S(2)}, u32[]{:S(2)}) collective-permute-start(bf16[384,768]{1,0:T(8,128)(2,1)S(1)} %get-tuple-element.82), channel_id=1, source_target_pairs={{0,2},{2,6},{4,0},{6,4},{1,3},{3,7},{5,1},{7,5},{8,10},{10,14},{12... | collective-permute-start | bytes 1769480 | tf_op jit(solution)/shard_map/ppermute | solution.py:179
  320.0 40.7 %collective-permute-start.3 = (bf16[384,256]{1,0:T(8,128)(2,1)S(1)}, bf16[384,256]{1,0:T(8,128)(2,1)S(1)}, u32[]{:S(2)}, u32[]{:S(2)}) collective-permute-start(bf16[384,256]{1,0:T(8,128)(2,1)S(1)} %get-tuple-element.74), channel_id=1, source_target_pairs={{0,2},{2,6},{4,0},{6,4},{1,3},{3,7},{5,1},{7,5},{8,10},{10,14},{12... | collective-permute-start | bytes 589832 | tf_op jit(solution)/shard_map/ppermute | solution.py:179
  322.8 37.9 %collective-permute-start.4 = (bf16[384,256]{1,0:T(8,128)(2,1)S(1)}, bf16[384,256]{1,0:T(8,128)(2,1)S(1)}, u32[]{:S(2)}, u32[]{:S(2)}) collective-permute-start(bf16[384,256]{1,0:T(8,128)(2,1)S(1)} %get-tuple-element.75), channel_id=1, source_target_pairs={{0,6},{2,4},{4,2},{6,0},{1,7},{3,5},{5,3},{7,1},{8,14},{10,12},{12... | collective-permute-start | bytes 589832 | tf_op jit(solution)/shard_map/ppermute | solution.py:179
  325.6 35.1 %collective-permute-start.5 = (bf16[384,256]{1,0:T(8,128)(2,1)S(1)}, bf16[384,256]{1,0:T(8,128)(2,1)S(1)}, u32[]{:S(2)}, u32[]{:S(2)}) collective-permute-start(bf16[384,256]{1,0:T(8,128)(2,1)S(1)} %get-tuple-element.76), channel_id=1, source_target_pairs={{0,4},{2,0},{4,6},{6,2},{1,5},{3,1},{5,7},{7,3},{8,12},{10,8},{12,... | collective-permute-start | bytes 589832 | tf_op jit(solution)/shard_map/ppermute | solution.py:179
  (30 other events, 465.5 us)

commit v8 on v6

--- a/solution.py
+++ b/solution.py
@@ -10,7 +10,7 @@
 TP_FIRST = "XY"
 ORDER = (
     "AX", "AY", "A0", "A1", "B0", "HX", "A2", "B1", "HY", "A3", "C0", "B2", "A4",
-    "BX", "C1", "BY", "A5", "B3", "B4", "B5", "C2", "CX", "CY", "C3", "C4", "C5",
+    "BX", "C1", "BY", "A5", "B3", "B4", "B5", "C2", "CX", "CY", "C3", "C4", "C5", "D5",
 )
 WORTH_CHUNKS = 1 << 19
 ANY = pl.BlockSpec(memory_space=pl.ANY)
@@ -132,7 +132,8 @@
     )(owned, *in_vmem(pieces))
 
 
-def place(saved, pieces, owned, sizes, first, offset, hidden):
+def place(saved, landed, owned, sizes, first, offset, hidden):
+    steps, pieces = tuple(landed), tuple(landed.values())
     count = len(pieces)
     block_rows, width = pieces[0].shape
 
@@ -142,13 +143,13 @@
         ins, out, sems = refs[len(table):len(table) + count], refs[-2], refs[-1]
         me, mine, replica = position()
         copies = []
-        for step in range(count):
+        for slot, step in enumerate(steps):
             crossed = step
             if first:
                 crossed = me ^ step ^ expert_of(refs[0], me, mine, replica, sizes)
-            origin = partner_of("tp", mine, -crossed, count)
+            origin = partner_of("tp", mine, -crossed, sizes[1])
             start = pl.multiple_of(origin * hidden + offset, 128)
-            copies.append(pltpu.make_async_copy(ins[step], out.at[:, pl.ds(start, width)], sems.at[step]))
+            copies.append(pltpu.make_async_copy(ins[slot], out.at[:, pl.ds(start, width)], sems.at[slot]))
         for copy in copies:
             copy.start()
         for copy in copies:
@@ -158,7 +159,7 @@
         kernel,
         in_specs=[SCALARS] * len(table) + [WHOLE] * count + [ANY] * len(saved),
         out_specs=ANY,
-        out_shape=jax.ShapeDtypeStruct((block_rows, count * hidden), pieces[0].dtype),
+        out_shape=jax.ShapeDtypeStruct((block_rows, sizes[1] * hidden), pieces[0].dtype),
         scratch_shapes=[pltpu.SemaphoreType.DMA((count,))],
         input_output_aliases={len(table) + count: 0} if saved else {},
         compiler_params=PARAMS,
@@ -194,7 +195,10 @@
         elif stage == "B":
             sent = choose(moved[chunk], owned, sizes, first)
         else:
-            saved = [place(saved, moved[chunk], owned, sizes, first, offset, hidden)]
+            early = sizes[1] // 2 if "D" + chunk in order else sizes[1]
+            landed = list(enumerate(moved[chunk]))
+            landed = landed[early:] if stage == "D" else landed[:early]
+            saved = [place(saved, dict(landed), owned, sizes, first, offset, hidden)]
             continue
         moved[chunk] = exchange(sent, axis_of(stage, chunk), chunk == order[-1][1])
     return saved[0][None, None]

time: 364 us -> 363 us (level)
    pallas_call x8 -> x9, Pallas kernels: 10.9 us -> 11.5 us  [place(): pl.pallas_call(kernel, in_specs=[SCALARS] * len(table) + [WHOLE] * count...]
  transfers between devices with their start and end apart: 54 -> 54, of which waited for: 16 -> 16; matrix products, arithmetic and copies ran while one was open for 0% -> 0% of each run, Pallas kernels for 9% -> 10%
where the time goes in v8:
time: 363 us; the launch traced here: 362 us
  starting transfers between devices  199 us (55%)
  waiting for transfers between devices  126 us (35%)
  Pallas kernels  36.8 us (10%)
    ppermute x54, starting transfers between devices, exchange(): moved[step] = lax.ppermute(pieces[step], axis, pairs)  199 us
    ppermute x54, waiting for transfers between devices, exchange(): moved[step] = lax.ppermute(pieces[step], axis, pairs)  126 us
    pallas_call x8, Pallas kernels, pick_rows(): pl.pallas_call(kernel, grid=(width // tile,), in_specs=[SCALARS, pl.Block...  17.7 us
    pallas_call x9, Pallas kernels, place(): pl.pallas_call(kernel, in_specs=[SCALARS] * len(table) + [WHOLE] * count...  11.5 us
    pallas_call x8, Pallas kernels, choose(): pl.pallas_call(kernel, in_specs=[SCALARS] + [WHOLE] * count, out_specs=[W...  7.52 us
  transfers between devices with their start and end apart: 54, of which 16 were waited for; matrix products, arithmetic and copies ran while one was open for 0% of the time, Pallas kernels for 10%

profile of v8, /device:TPU:0, one launch (start us, length us, event | category | flops | bytes accessed | tf_op | source)
XLA Modules:
  0.0 362.3 jit_solution(1015995039759057182)
XLA Ops:
  1.2 3.1 collective-permute-start.27
  26.4 4.5 %collective-permute-done.30.refs_2_ = bf16[384,128]{1,0:T(8,128)(2,1)S(1)} collective-permute-done((bf16[384,128]{1,0:T(8,128)(2,1)S(1)}, bf16[384,128]{1,0:T(8,128)(2,1)S(1)}, u32[]{:S(2)}, u32[]{:S(2)}) %collective-permute-start.30) | collective-permute-done | bytes 98336 | tf_op jit(solution)/shard_map/ppermute | solution.py:175
  30.9 5.2 %collective-permute-start.18 = (bf16[384,384]{1,0:T(8,128)(2,1)S(1)}, bf16[384,384]{1,0:T(8,128)(2,1)S(1)}, u32[]{:S(2)}, u32[]{:S(2)}) collective-permute-start(bf16[384,384]{1,0:T(8,128)(2,1)S(1)} %get-tuple-element.94), channel_id=1, source_target_pairs={{0,2},{2,6},{4,0},{6,4},{1,3},{3,7},{5,1},{7,5},{8,10},{10,14},{12... | collective-permute-start | bytes 884744 | tf_op jit(solution)/shard_map/ppermute | solution.py:175
  50.4 3.9 %collective-permute-start.52 = (bf16[384,256]{1,0:T(8,128)(2,1)S(1)}, bf16[384,256]{1,0:T(8,128)(2,1)S(1)}, u32[]{:S(2)}, u32[]{:S(2)}) collective-permute-start(bf16[384,256]{1,0:T(8,128)(2,1)S(1)} %get-tuple-element.131), channel_id=1, source_target_pairs={{0,6},{2,4},{4,2},{6,0},{1,7},{3,5},{5,3},{7,1},{8,14},{10,12},{12... | collective-permute-start | bytes 589832 | tf_op jit(solution)/shard_map/ppermute | solution.py:175
  54.3 12.0 %collective-permute-start.53 = (bf16[384,256]{1,0:T(8,128)(2,1)S(1)}, bf16[384,256]{1,0:T(8,128)(2,1)S(1)}, u32[]{:S(2)}, u32[]{:S(2)}) collective-permute-start(bf16[384,256]{1,0:T(8,128)(2,1)S(1)} %get-tuple-element.132), channel_id=1, source_target_pairs={{0,4},{2,0},{4,6},{6,2},{1,5},{3,1},{5,7},{7,3},{8,12},{10,8},{12,... | collective-permute-start | bytes 589832 | tf_op jit(solution)/shard_map/ppermute | solution.py:175
  66.4 2.9 pick_rows.13
  79.3 7.8 %collective-permute-done.43.refs_2_ = bf16[384,512]{1,0:T(8,128)(2,1)S(1)} collective-permute-done((bf16[384,512]{1,0:T(8,128)(2,1)S(1)}, bf16[384,512]{1,0:T(8,128)(2,1)S(1)}, u32[]{:S(2)}, u32[]{:S(2)}) %collective-permute-start.43) | collective-permute-done | bytes 393248 | tf_op jit(solution)/shard_map/ppermute | solution.py:175
  87.9 8.1 %collective-permute-done.44.refs_3_ = bf16[384,512]{1,0:T(8,128)(2,1)S(1)} collective-permute-done((bf16[384,512]{1,0:T(8,128)(2,1)S(1)}, bf16[384,512]{1,0:T(8,128)(2,1)S(1)}, u32[]{:S(2)}, u32[]{:S(2)}) %collective-permute-start.44) | collective-permute-done | bytes 393248 | tf_op jit(solution)/shard_map/ppermute | solution.py:175
  99.4 19.7 %collective-permute-done.37.refs_2_ = bf16[384,768]{1,0:T(8,128)(2,1)S(1)} collective-permute-done((bf16[384,768]{1,0:T(8,128)(2,1)S(1)}, bf16[384,768]{1,0:T(8,128)(2,1)S(1)}, u32[]{:S(2)}, u32[]{:S(2)}) %collective-permute-start.37) | collective-permute-done | bytes 589856 | tf_op jit(solution)/shard_map/ppermute | solution.py:175
  125.7 13.4 %collective-permute-done.21.refs_2_ = bf16[384,384]{1,0:T(8,128)(2,1)S(1)} collective-permute-done((bf16[384,384]{1,0:T(8,128)(2,1)S(1)}, bf16[384,384]{1,0:T(8,128)(2,1)S(1)}, u32[]{:S(2)}, u32[]{:S(2)}) %collective-permute-start.21) | collective-permute-done | bytes 294944 | tf_op jit(solution)/shard_map/ppermute | solution.py:175
  139.1 6.0 %collective-permute-start.45 = (bf16[384,512]{1,0:T(8,128)(2,1)S(1)}, bf16[384,512]{1,0:T(8,128)(2,1)S(1)}, u32[]{:S(2)}, u32[]{:S(2)}) collective-permute-start(bf16[384,512]{1,0:T(8,128)(2,1)S(1)} %get-tuple-element.122), channel_id=1, source_target_pairs={{0,2},{2,6},{4,0},{6,4},{1,3},{3,7},{5,1},{7,5},{8,10},{10,14},{12... | collective-permute-start | bytes 1179656 | tf_op jit(solution)/shard_map/ppermute | solution.py:175
  145.1 3.5 pick_rows.10
  154.8 17.0 %collective-permute-done.45.refs_1_ = bf16[384,512]{1,0:T(8,128)(2,1)S(1)} collective-permute-done((bf16[384,512]{1,0:T(8,128)(2,1)S(1)}, bf16[384,512]{1,0:T(8,128)(2,1)S(1)}, u32[]{:S(2)}, u32[]{:S(2)}) %collective-permute-start.45) | collective-permute-done | bytes 393248 | tf_op jit(solution)/shard_map/ppermute | solution.py:175
  172.8 7.5 %collective-permute-start.39 = (bf16[384,768]{1,0:T(8,128)(2,1)S(1)}, bf16[384,768]{1,0:T(8,128)(2,1)S(1)}, u32[]{:S(2)}, u32[]{:S(2)}) collective-permute-start(bf16[384,768]{1,0:T(8,128)(2,1)S(1)} %get-tuple-element.114), channel_id=1, source_target_pairs={{0,2},{2,6},{4,0},{6,4},{1,3},{3,7},{5,1},{7,5},{8,10},{10,14},{12... | collective-permute-start | bytes 1769480 | tf_op jit(solution)/shard_map/ppermute | solution.py:175
  180.3 17.7 %collective-permute-done.47.refs_3_ = bf16[384,512]{1,0:T(8,128)(2,1)S(1)} collective-permute-done((bf16[384,512]{1,0:T(8,128)(2,1)S(1)}, bf16[384,512]{1,0:T(8,128)(2,1)S(1)}, u32[]{:S(2)}, u32[]{:S(2)}) %collective-permute-start.47) | collective-permute-done | bytes 393248 | tf_op jit(solution)/shard_map/ppermute | solution.py:175
  199.1 3.4 collective-permute-start.26
  209.0 3.8 %collective-permute-start.10 = (bf16[384,768]{1,0:T(8,128)(2,1)S(1)}, bf16[384,768]{1,0:T(8,128)(2,1)S(1)}, u32[]{:S(2)}, u32[]{:S(2)}) collective-permute-start(bf16[384,768]{1,0:T(8,128)(2,1)S(1)} %get-tuple-element.83), channel_id=1, source_target_pairs={{0,6},{2,4},{4,2},{6,0},{1,7},{3,5},{5,3},{7,1},{8,14},{10,12},{12... | collective-permute-start | bytes 1769480 | tf_op jit(solution)/shard_map/ppermute | solution.py:175
  213.9 7.5 %collective-permute-done.39.refs_1_ = bf16[384,768]{1,0:T(8,128)(2,1)S(1)} collective-permute-done((bf16[384,768]{1,0:T(8,128)(2,1)S(1)}, bf16[384,768]{1,0:T(8,128)(2,1)S(1)}, u32[]{:S(2)}, u32[]{:S(2)}) %collective-permute-start.39) | collective-permute-done | bytes 589856 | tf_op jit(solution)/shard_map/ppermute | solution.py:175
  221.5 6.9 %collective-permute-start.16 = (bf16[384,1024]{1,0:T(8,128)(2,1)S(1)}, bf16[384,1024]{1,0:T(8,128)(2,1)S(1)}, u32[]{:S(2)}, u32[]{:S(2)}) collective-permute-start(bf16[384,1024]{1,0:T(8,128)(2,1)S(1)} %get-tuple-element.91), channel_id=1, source_target_pairs={{0,6},{2,4},{4,2},{6,0},{1,7},{3,5},{5,3},{7,1},{8,14},{10,12},{12... | collective-permute-start | bytes 2359304 | tf_op jit(solution)/shard_map/ppermute | solution.py:175
  228.4 26.7 %collective-permute-start.17 = (bf16[384,1024]{1,0:T(8,128)(2,1)S(1)}, bf16[384,1024]{1,0:T(8,128)(2,1)S(1)}, u32[]{:S(2)}, u32[]{:S(2)}) collective-permute-start(bf16[384,1024]{1,0:T(8,128)(2,1)S(1)} %get-tuple-element.92), channel_id=1, source_target_pairs={{0,4},{2,0},{4,6},{6,2},{1,5},{3,1},{5,7},{7,3},{8,12},{10,8},{12,... | collective-permute-start | bytes 2359304 | tf_op jit(solution)/shard_map/ppermute | solution.py:175
  255.1 48.5 %collective-permute-start.9 = (bf16[384,768]{1,0:T(8,128)(2,1)S(1)}, bf16[384,768]{1,0:T(8,128)(2,1)S(1)}, u32[]{:S(2)}, u32[]{:S(2)}) collective-permute-start(bf16[384,768]{1,0:T(8,128)(2,1)S(1)} %get-tuple-element.82), channel_id=1, source_target_pairs={{0,2},{2,6},{4,0},{6,4},{1,3},{3,7},{5,1},{7,5},{8,10},{10,14},{12... | collective-permute-start | bytes 1769480 | tf_op jit(solution)/shard_map/ppermute | solution.py:175
  304.5 15.4 %collective-permute-done.15.refs_1_ = bf16[384,1024]{1,0:T(8,128)(2,1)S(1)} collective-permute-done((bf16[384,1024]{1,0:T(8,128)(2,1)S(1)}, bf16[384,1024]{1,0:T(8,128)(2,1)S(1)}, u32[]{:S(2)}, u32[]{:S(2)}) %collective-permute-start.15) | collective-permute-done | bytes 786464 | tf_op jit(solution)/shard_map/ppermute | solution.py:175
  325.4 20.2 %collective-permute-start.4 = (bf16[384,256]{1,0:T(8,128)(2,1)S(1)}, bf16[384,256]{1,0:T(8,128)(2,1)S(1)}, u32[]{:S(2)}, u32[]{:S(2)}) collective-permute-start(bf16[384,256]{1,0:T(8,128)(2,1)S(1)} %get-tuple-element.74), channel_id=1, source_target_pairs={{0,4},{2,0},{4,6},{6,2},{1,5},{3,1},{5,7},{7,3},{8,12},{10,8},{12,... | collective-permute-start | bytes 589832 | tf_op jit(solution)/shard_map/ppermute | solution.py:175
  354.2 3.6 %collective-permute-done.9.refs_1_ = bf16[384,768]{1,0:T(8,128)(2,1)S(1)} collective-permute-done((bf16[384,768]{1,0:T(8,128)(2,1)S(1)}, bf16[384,768]{1,0:T(8,128)(2,1)S(1)}, u32[]{:S(2)}, u32[]{:S(2)}) %collective-permute-start.9) | collective-permute-done | bytes 589856 | tf_op jit(solution)/shard_map/ppermute | solution.py:175
  (109 shorter events, 93.6 us)
Async XLA Ops:
  46.0 29.2 %collective-permute-start.42 = (bf16[384,512]{1,0:T(8,128)(2,1)S(1)}, bf16[384,512]{1,0:T(8,128)(2,1)S(1)}, u32[]{:S(2)}, u32[]{:S(2)}) collective-permute-start(bf16[384,512]{1,0:T(8,128)(2,1)S(1)} %get-tuple-element.118), channel_id=1, source_target_pairs={{0,8},{8,0},{16,24},{24,16},{1,9},{9,1},{17,25},{25,17},{2,10},{10... | collective-permute-start | bytes 1179656 | tf_op jit(solution)/shard_map/ppermute | solution.py:175
  73.4 45.8 %collective-permute-start.37 = (bf16[384,768]{1,0:T(8,128)(2,1)S(1)}, bf16[384,768]{1,0:T(8,128)(2,1)S(1)}, u32[]{:S(2)}, u32[]{:S(2)}) collective-permute-start(bf16[384,768]{1,0:T(8,128)(2,1)S(1)} %get-tuple-element.111), channel_id=1, source_target_pairs={{0,16},{8,24},{16,0},{24,8},{1,17},{9,25},{17,1},{25,9},{2,18},{10... | collective-permute-start | bytes 1769480 | tf_op jit(solution)/shard_map/ppermute | solution.py:175
  75.3 45.7 %collective-permute-start.38 = (bf16[384,768]{1,0:T(8,128)(2,1)S(1)}, bf16[384,768]{1,0:T(8,128)(2,1)S(1)}, u32[]{:S(2)}, u32[]{:S(2)}) collective-permute-start(bf16[384,768]{1,0:T(8,128)(2,1)S(1)} %get-tuple-element.112), channel_id=1, source_target_pairs={{0,24},{8,16},{16,8},{24,0},{1,25},{9,17},{17,9},{25,1},{2,26},{10... | collective-permute-start | bytes 1769480 | tf_op jit(solution)/shard_map/ppermute | solution.py:175
  87.2 62.7 %collective-permute-start.6 = (bf16[384,768]{1,0:T(8,128)(2,1)S(1)}, bf16[384,768]{1,0:T(8,128)(2,1)S(1)}, u32[]{:S(2)}, u32[]{:S(2)}) collective-permute-start(bf16[384,768]{1,0:T(8,128)(2,1)S(1)} %get-tuple-element.78), channel_id=1, source_target_pairs={{0,8},{8,0},{16,24},{24,16},{1,9},{9,1},{17,25},{25,17},{2,10},{10... | collective-permute-start | bytes 1769480 | tf_op jit(solution)/shard_map/ppermute | solution.py:175
  95.9 27.8 %collective-permute-start.19 = (bf16[384,384]{1,0:T(8,128)(2,1)S(1)}, bf16[384,384]{1,0:T(8,128)(2,1)S(1)}, u32[]{:S(2)}, u32[]{:S(2)}) collective-permute-start(bf16[384,384]{1,0:T(8,128)(2,1)S(1)} %collective-permute-done.18), channel_id=1, source_target_pairs={{0,8},{8,0},{16,24},{24,16},{1,9},{9,1},{17,25},{25,17},{2,10},{10... | collective-permute-start | bytes 884744 | tf_op jit(solution)/shard_map/ppermute | solution.py:175
  97.5 53.0 %collective-permute-start.7 = (bf16[384,768]{1,0:T(8,128)(2,1)S(1)}, bf16[384,768]{1,0:T(8,128)(2,1)S(1)}, u32[]{:S(2)}, u32[]{:S(2)}) collective-permute-start(bf16[384,768]{1,0:T(8,128)(2,1)S(1)} %get-tuple-element.79), channel_id=1, source_target_pairs={{0,16},{8,24},{16,0},{24,8},{1,17},{9,25},{17,1},{25,9},{2,18},{10... | collective-permute-start | bytes 1769480 | tf_op jit(solution)/shard_map/ppermute | solution.py:175
  121.0 27.6 %collective-permute-start.23 = (bf16[384,384]{1,0:T(8,128)(2,1)S(1)}, bf16[384,384]{1,0:T(8,128)(2,1)S(1)}, u32[]{:S(2)}, u32[]{:S(2)}) collective-permute-start(bf16[384,384]{1,0:T(8,128)(2,1)S(1)} %collective-permute-done.22), channel_id=1, source_target_pairs={{0,24},{8,16},{16,8},{24,0},{1,25},{9,17},{17,9},{25,1},{2,26},{10... | collective-permute-start | bytes 884744 | tf_op jit(solution)/shard_map/ppermute | solution.py:175
  123.7 28.4 %collective-permute-start.8 = (bf16[384,768]{1,0:T(8,128)(2,1)S(1)}, bf16[384,768]{1,0:T(8,128)(2,1)S(1)}, u32[]{:S(2)}, u32[]{:S(2)}) collective-permute-start(bf16[384,768]{1,0:T(8,128)(2,1)S(1)} %get-tuple-element.80), channel_id=1, source_target_pairs={{0,24},{8,16},{16,8},{24,0},{1,25},{9,17},{17,9},{25,1},{2,26},{10... | collective-permute-start | bytes 1769480 | tf_op jit(solution)/shard_map/ppermute | solution.py:175
  139.1 32.7 %collective-permute-start.45 = (bf16[384,512]{1,0:T(8,128)(2,1)S(1)}, bf16[384,512]{1,0:T(8,128)(2,1)S(1)}, u32[]{:S(2)}, u32[]{:S(2)}) collective-permute-start(bf16[384,512]{1,0:T(8,128)(2,1)S(1)} %get-tuple-element.122), channel_id=1, source_target_pairs={{0,2},{2,6},{4,0},{6,4},{1,3},{3,7},{5,1},{7,5},{8,10},{10,14},{12... | collective-permute-start | bytes 1179656 | tf_op jit(solution)/shard_map/ppermute | solution.py:175
  148.6 50.4 %collective-permute-start.12 = (bf16[384,1024]{1,0:T(8,128)(2,1)S(1)}, bf16[384,1024]{1,0:T(8,128)(2,1)S(1)}, u32[]{:S(2)}, u32[]{:S(2)}) collective-permute-start(bf16[384,1024]{1,0:T(8,128)(2,1)S(1)} %get-tuple-element.86), channel_id=1, source_target_pairs={{0,8},{8,0},{16,24},{24,16},{1,9},{9,1},{17,25},{25,17},{2,10},{10... | collective-permute-start | bytes 2359304 | tf_op jit(solution)/shard_map/ppermute | solution.py:175
  149.8 49.2 %collective-permute-start.13 = (bf16[384,1024]{1,0:T(8,128)(2,1)S(1)}, bf16[384,1024]{1,0:T(8,128)(2,1)S(1)}, u32[]{:S(2)}, u32[]{:S(2)}) collective-permute-start(bf16[384,1024]{1,0:T(8,128)(2,1)S(1)} %get-tuple-element.87), channel_id=1, source_target_pairs={{0,16},{8,24},{16,0},{24,8},{1,17},{9,25},{17,1},{25,9},{2,18},{10... | collective-permute-start | bytes 2359304 | tf_op jit(solution)/shard_map/ppermute | solution.py:175
  150.5 48.6 %collective-permute-start.14 = (bf16[384,1024]{1,0:T(8,128)(2,1)S(1)}, bf16[384,1024]{1,0:T(8,128)(2,1)S(1)}, u32[]{:S(2)}, u32[]{:S(2)}) collective-permute-start(bf16[384,1024]{1,0:T(8,128)(2,1)S(1)} %get-tuple-element.88), channel_id=1, source_target_pairs={{0,24},{8,16},{16,8},{24,0},{1,25},{9,17},{17,9},{25,1},{2,26},{10... | collective-permute-start | bytes 2359304 | tf_op jit(solution)/shard_map/ppermute | solution.py:175
  172.8 48.7 %collective-permute-start.39 = (bf16[384,768]{1,0:T(8,128)(2,1)S(1)}, bf16[384,768]{1,0:T(8,128)(2,1)S(1)}, u32[]{:S(2)}, u32[]{:S(2)}) collective-permute-start(bf16[384,768]{1,0:T(8,128)(2,1)S(1)} %get-tuple-element.114), channel_id=1, source_target_pairs={{0,2},{2,6},{4,0},{6,4},{1,3},{3,7},{5,1},{7,5},{8,10},{10,14},{12... | collective-permute-start | bytes 1769480 | tf_op jit(solution)/shard_map/ppermute | solution.py:175
  198.0 30.4 %collective-permute-start.40 = (bf16[384,768]{1,0:T(8,128)(2,1)S(1)}, bf16[384,768]{1,0:T(8,128)(2,1)S(1)}, u32[]{:S(2)}, u32[]{:S(2)}) collective-permute-start(bf16[384,768]{1,0:T(8,128)(2,1)S(1)} %get-tuple-element.115), channel_id=1, source_target_pairs={{0,6},{2,4},{4,2},{6,0},{1,7},{3,5},{5,3},{7,1},{8,14},{10,12},{12... | collective-permute-start | bytes 1769480 | tf_op jit(solution)/shard_map/ppermute | solution.py:175
  205.7 49.3 %collective-permute-start.41 = (bf16[384,768]{1,0:T(8,128)(2,1)S(1)}, bf16[384,768]{1,0:T(8,128)(2,1)S(1)}, u32[]{:S(2)}, u32[]{:S(2)}) collective-permute-start(bf16[384,768]{1,0:T(8,128)(2,1)S(1)} %get-tuple-element.116), channel_id=1, source_target_pairs={{0,4},{2,0},{4,6},{6,2},{1,5},{3,1},{5,7},{7,3},{8,12},{10,8},{12,... | collective-permute-start | bytes 1769480 | tf_op jit(solution)/shard_map/ppermute | solution.py:175
  209.0 46.1 %collective-permute-start.10 = (bf16[384,768]{1,0:T(8,128)(2,1)S(1)}, bf16[384,768]{1,0:T(8,128)(2,1)S(1)}, u32[]{:S(2)}, u32[]{:S(2)}) collective-permute-start(bf16[384,768]{1,0:T(8,128)(2,1)S(1)} %get-tuple-element.83), channel_id=1, source_target_pairs={{0,6},{2,4},{4,2},{6,0},{1,7},{3,5},{5,3},{7,1},{8,14},{10,12},{12... | collective-permute-start | bytes 1769480 | tf_op jit(solution)/shard_map/ppermute | solution.py:175
  213.9 106.0 %collective-permute-start.15 = (bf16[384,1024]{1,0:T(8,128)(2,1)S(1)}, bf16[384,1024]{1,0:T(8,128)(2,1)S(1)}, u32[]{:S(2)}, u32[]{:S(2)}) collective-permute-start(bf16[384,1024]{1,0:T(8,128)(2,1)S(1)} %get-tuple-element.90), channel_id=1, source_target_pairs={{0,2},{2,6},{4,0},{6,4},{1,3},{3,7},{5,1},{7,5},{8,10},{10,14},{12... | collective-permute-start | bytes 2359304 | tf_op jit(solution)/shard_map/ppermute | solution.py:175
  221.5 101.1 %collective-permute-start.16 = (bf16[384,1024]{1,0:T(8,128)(2,1)S(1)}, bf16[384,1024]{1,0:T(8,128)(2,1)S(1)}, u32[]{:S(2)}, u32[]{:S(2)}) collective-permute-start(bf16[384,1024]{1,0:T(8,128)(2,1)S(1)} %get-tuple-element.91), channel_id=1, source_target_pairs={{0,6},{2,4},{4,2},{6,0},{1,7},{3,5},{5,3},{7,1},{8,14},{10,12},{12... | collective-permute-start | bytes 2359304 | tf_op jit(solution)/shard_map/ppermute | solution.py:175
  228.4 97.1 %collective-permute-start.17 = (bf16[384,1024]{1,0:T(8,128)(2,1)S(1)}, bf16[384,1024]{1,0:T(8,128)(2,1)S(1)}, u32[]{:S(2)}, u32[]{:S(2)}) collective-permute-start(bf16[384,1024]{1,0:T(8,128)(2,1)S(1)} %get-tuple-element.92), channel_id=1, source_target_pairs={{0,4},{2,0},{4,6},{6,2},{1,5},{3,1},{5,7},{7,3},{8,12},{10,8},{12,... | collective-permute-start | bytes 2359304 | tf_op jit(solution)/shard_map/ppermute | solution.py:175
  255.1 99.1 %collective-permute-start.11 = (bf16[384,768]{1,0:T(8,128)(2,1)S(1)}, bf16[384,768]{1,0:T(8,128)(2,1)S(1)}, u32[]{:S(2)}, u32[]{:S(2)}) collective-permute-start(bf16[384,768]{1,0:T(8,128)(2,1)S(1)} %get-tuple-element.84), channel_id=1, source_target_pairs={{0,4},{2,0},{4,6},{6,2},{1,5},{3,1},{5,7},{7,3},{8,12},{10,8},{12,... | collective-permute-start | bytes 1769480 | tf_op jit(solution)/shard_map/ppermute | solution.py:175
  255.1 102.8 %collective-permute-start.9 = (bf16[384,768]{1,0:T(8,128)(2,1)S(1)}, bf16[384,768]{1,0:T(8,128)(2,1)S(1)}, u32[]{:S(2)}, u32[]{:S(2)}) collective-permute-start(bf16[384,768]{1,0:T(8,128)(2,1)S(1)} %get-tuple-element.82), channel_id=1, source_target_pairs={{0,2},{2,6},{4,0},{6,4},{1,3},{3,7},{5,1},{7,5},{8,10},{10,14},{12... | collective-permute-start | bytes 1769480 | tf_op jit(solution)/shard_map/ppermute | solution.py:175
  319.9 40.9 %collective-permute-start.5 = (bf16[384,256]{1,0:T(8,128)(2,1)S(1)}, bf16[384,256]{1,0:T(8,128)(2,1)S(1)}, u32[]{:S(2)}, u32[]{:S(2)}) collective-permute-start(bf16[384,256]{1,0:T(8,128)(2,1)S(1)} %get-tuple-element.76), channel_id=1, source_target_pairs={{0,2},{2,6},{4,0},{6,4},{1,3},{3,7},{5,1},{7,5},{8,10},{10,14},{12... | collective-permute-start | bytes 589832 | tf_op jit(solution)/shard_map/ppermute | solution.py:175
  322.6 38.9 %collective-permute-start.3 = (bf16[384,256]{1,0:T(8,128)(2,1)S(1)}, bf16[384,256]{1,0:T(8,128)(2,1)S(1)}, u32[]{:S(2)}, u32[]{:S(2)}) collective-permute-start(bf16[384,256]{1,0:T(8,128)(2,1)S(1)} %get-tuple-element.73), channel_id=1, source_target_pairs={{0,6},{2,4},{4,2},{6,0},{1,7},{3,5},{5,3},{7,1},{8,14},{10,12},{12... | collective-permute-start | bytes 589832 | tf_op jit(solution)/shard_map/ppermute | solution.py:175
  325.4 36.1 %collective-permute-start.4 = (bf16[384,256]{1,0:T(8,128)(2,1)S(1)}, bf16[384,256]{1,0:T(8,128)(2,1)S(1)}, u32[]{:S(2)}, u32[]{:S(2)}) collective-permute-start(bf16[384,256]{1,0:T(8,128)(2,1)S(1)} %get-tuple-element.74), channel_id=1, source_target_pairs={{0,4},{2,0},{4,6},{6,2},{1,5},{3,1},{5,7},{7,3},{8,12},{10,8},{12,... | collective-permute-start | bytes 589832 | tf_op jit(solution)/shard_map/ppermute | solution.py:175
  (30 other events, 465.8 us)

commit v9 on v8

--- a/solution.py
+++ b/solution.py
@@ -84,17 +84,22 @@
     tile = tile_of(offset, width)
     rows = weight.shape[1]
     block_rows = rows // count
+    lanes = block_rows % 128 == 0
 
     def kernel(owned_ref, weight_ref, *refs):
-        outs, turned = refs[:-1], refs[-1]
+        outs, turned = refs[:count], refs[count:]
         me, mine, replica = position()
-        turned[...] = weight_ref[...].T
+        if not lanes:
+            turned[0][...] = weight_ref[...].T
         columns = pl.ds(pl.multiple_of(pl.program_id(0) * tile, 128), tile)
         for step, out in enumerate(outs):
             row, column = me ^ step, partner_of("tp", mine, step, count)
             owners = [(line, column) if first else (row, line) for line in range(count)]
             span = sum(span_of(owned_ref, me, row, column, replica, sizes) for row, column in owners)
-            out[:, columns] = turned[pl.ds(pl.multiple_of(span * block_rows, 16), block_rows), :]
+            if lanes:
+                out[:, columns] = weight_ref[:, pl.ds(pl.multiple_of(span * block_rows, 128), block_rows)].T
+            else:
+                out[:, columns] = turned[0][pl.ds(pl.multiple_of(span * block_rows, 16), block_rows), :]
 
     return pl.pallas_call(
         kernel,
@@ -102,7 +107,7 @@
         in_specs=[SCALARS, pl.BlockSpec((tile, rows), lambda step: (offset // tile + step, 0))],
         out_specs=[WHOLE] * count,
         out_shape=[pltpu.VMEM((block_rows, width), weight.dtype)] * count,
-        scratch_shapes=[pltpu.VMEM((rows, tile), weight.dtype)],
+        scratch_shapes=[] if lanes else [pltpu.VMEM((rows, tile), weight.dtype)],
         compiler_params=PARAMS,
         name="pick_rows",
     )(owned, weight)

time: 363 us -> 364 us (level)
  transfers between devices with their start and end apart: 54 -> 54, of which waited for: 16 -> 16; matrix products, arithmetic and copies ran while one was open for 0% -> 0% of each run, Pallas kernels for 10% -> 9%
where the time goes in v9:
time: 364 us; the launch traced here: 362 us
  starting transfers between devices  199 us (55%)
  waiting for transfers between devices  127 us (35%)
  Pallas kernels  36.2 us (10%)
    ppermute x54, starting transfers between devices, exchange(): moved[step] = lax.ppermute(pieces[step], axis, pairs)  199 us
    ppermute x54, waiting for transfers between devices, exchange(): moved[step] = lax.ppermute(pieces[step], axis, pairs)  127 us
    pallas_call x8, Pallas kernels, pick_rows(): pl.pallas_call(kernel, grid=(width // tile,), in_specs=[SCALARS, pl.Block...  17.2 us
    pallas_call x9, Pallas kernels, place(): pl.pallas_call(kernel, in_specs=[SCALARS] * len(table) + [WHOLE] * count...  11.5 us
    pallas_call x8, Pallas kernels, choose(): pl.pallas_call(kernel, in_specs=[SCALARS] + [WHOLE] * count, out_specs=[W...  7.52 us
  transfers between devices with their start and end apart: 54, of which 16 were waited for; matrix products, arithmetic and copies ran while one was open for 0% of the time, Pallas kernels for 9%

profile of v9, /device:TPU:0, one launch (start us, length us, event | category | flops | bytes accessed | tf_op | source)
XLA Modules:
  0.0 362.3 jit_solution(8620871275581737359)
XLA Ops:
  1.2 3.1 collective-permute-start.27
  26.3 4.6 %collective-permute-done.30.refs_2_ = bf16[384,128]{1,0:T(8,128)(2,1)S(1)} collective-permute-done((bf16[384,128]{1,0:T(8,128)(2,1)S(1)}, bf16[384,128]{1,0:T(8,128)(2,1)S(1)}, u32[]{:S(2)}, u32[]{:S(2)}) %collective-permute-start.30) | collective-permute-done | bytes 98336 | tf_op jit(solution)/shard_map/ppermute | solution.py:180
  30.8 5.2 %collective-permute-start.18 = (bf16[384,384]{1,0:T(8,128)(2,1)S(1)}, bf16[384,384]{1,0:T(8,128)(2,1)S(1)}, u32[]{:S(2)}, u32[]{:S(2)}) collective-permute-start(bf16[384,384]{1,0:T(8,128)(2,1)S(1)} %get-tuple-element.94), channel_id=1, source_target_pairs={{0,2},{2,6},{4,0},{6,4},{1,3},{3,7},{5,1},{7,5},{8,10},{10,14},{12... | collective-permute-start | bytes 884744 | tf_op jit(solution)/shard_map/ppermute | solution.py:180
  50.3 8.8 %collective-permute-start.52 = (bf16[384,256]{1,0:T(8,128)(2,1)S(1)}, bf16[384,256]{1,0:T(8,128)(2,1)S(1)}, u32[]{:S(2)}, u32[]{:S(2)}) collective-permute-start(bf16[384,256]{1,0:T(8,128)(2,1)S(1)} %get-tuple-element.131), channel_id=1, source_target_pairs={{0,6},{2,4},{4,2},{6,0},{1,7},{3,5},{5,3},{7,1},{8,14},{10,12},{12... | collective-permute-start | bytes 589832 | tf_op jit(solution)/shard_map/ppermute | solution.py:180
  59.1 7.2 %collective-permute-start.53 = (bf16[384,256]{1,0:T(8,128)(2,1)S(1)}, bf16[384,256]{1,0:T(8,128)(2,1)S(1)}, u32[]{:S(2)}, u32[]{:S(2)}) collective-permute-start(bf16[384,256]{1,0:T(8,128)(2,1)S(1)} %get-tuple-element.132), channel_id=1, source_target_pairs={{0,4},{2,0},{4,6},{6,2},{1,5},{3,1},{5,7},{7,3},{8,12},{10,8},{12,... | collective-permute-start | bytes 589832 | tf_op jit(solution)/shard_map/ppermute | solution.py:180
  76.3 2.9 pick_rows.9
  79.1 7.9 %collective-permute-done.43.refs_2_ = bf16[384,512]{1,0:T(8,128)(2,1)S(1)} collective-permute-done((bf16[384,512]{1,0:T(8,128)(2,1)S(1)}, bf16[384,512]{1,0:T(8,128)(2,1)S(1)}, u32[]{:S(2)}, u32[]{:S(2)}) %collective-permute-start.43) | collective-permute-done | bytes 393248 | tf_op jit(solution)/shard_map/ppermute | solution.py:180
  87.8 8.0 %collective-permute-done.44.refs_3_ = bf16[384,512]{1,0:T(8,128)(2,1)S(1)} collective-permute-done((bf16[384,512]{1,0:T(8,128)(2,1)S(1)}, bf16[384,512]{1,0:T(8,128)(2,1)S(1)}, u32[]{:S(2)}, u32[]{:S(2)}) %collective-permute-start.44) | collective-permute-done | bytes 393248 | tf_op jit(solution)/shard_map/ppermute | solution.py:180
  99.3 19.7 %collective-permute-done.37.refs_2_ = bf16[384,768]{1,0:T(8,128)(2,1)S(1)} collective-permute-done((bf16[384,768]{1,0:T(8,128)(2,1)S(1)}, bf16[384,768]{1,0:T(8,128)(2,1)S(1)}, u32[]{:S(2)}, u32[]{:S(2)}) %collective-permute-start.37) | collective-permute-done | bytes 589856 | tf_op jit(solution)/shard_map/ppermute | solution.py:180
  125.6 13.4 %collective-permute-done.21.refs_2_ = bf16[384,384]{1,0:T(8,128)(2,1)S(1)} collective-permute-done((bf16[384,384]{1,0:T(8,128)(2,1)S(1)}, bf16[384,384]{1,0:T(8,128)(2,1)S(1)}, u32[]{:S(2)}, u32[]{:S(2)}) %collective-permute-start.21) | collective-permute-done | bytes 294944 | tf_op jit(solution)/shard_map/ppermute | solution.py:180
  139.0 6.0 %collective-permute-start.45 = (bf16[384,512]{1,0:T(8,128)(2,1)S(1)}, bf16[384,512]{1,0:T(8,128)(2,1)S(1)}, u32[]{:S(2)}, u32[]{:S(2)}) collective-permute-start(bf16[384,512]{1,0:T(8,128)(2,1)S(1)} %get-tuple-element.122), channel_id=1, source_target_pairs={{0,2},{2,6},{4,0},{6,4},{1,3},{3,7},{5,1},{7,5},{8,10},{10,14},{12... | collective-permute-start | bytes 1179656 | tf_op jit(solution)/shard_map/ppermute | solution.py:180
  145.0 3.3 pick_rows.10
  154.6 17.4 %collective-permute-done.45.refs_1_ = bf16[384,512]{1,0:T(8,128)(2,1)S(1)} collective-permute-done((bf16[384,512]{1,0:T(8,128)(2,1)S(1)}, bf16[384,512]{1,0:T(8,128)(2,1)S(1)}, u32[]{:S(2)}, u32[]{:S(2)}) %collective-permute-start.45) | collective-permute-done | bytes 393248 | tf_op jit(solution)/shard_map/ppermute | solution.py:180
  173.0 7.5 %collective-permute-start.39 = (bf16[384,768]{1,0:T(8,128)(2,1)S(1)}, bf16[384,768]{1,0:T(8,128)(2,1)S(1)}, u32[]{:S(2)}, u32[]{:S(2)}) collective-permute-start(bf16[384,768]{1,0:T(8,128)(2,1)S(1)} %get-tuple-element.114), channel_id=1, source_target_pairs={{0,2},{2,6},{4,0},{6,4},{1,3},{3,7},{5,1},{7,5},{8,10},{10,14},{12... | collective-permute-start | bytes 1769480 | tf_op jit(solution)/shard_map/ppermute | solution.py:180
  180.4 17.2 %collective-permute-done.47.refs_3_ = bf16[384,512]{1,0:T(8,128)(2,1)S(1)} collective-permute-done((bf16[384,512]{1,0:T(8,128)(2,1)S(1)}, bf16[384,512]{1,0:T(8,128)(2,1)S(1)}, u32[]{:S(2)}, u32[]{:S(2)}) %collective-permute-start.47) | collective-permute-done | bytes 393248 | tf_op jit(solution)/shard_map/ppermute | solution.py:180
  198.8 3.4 collective-permute-start.26
  208.7 3.8 %collective-permute-start.10 = (bf16[384,768]{1,0:T(8,128)(2,1)S(1)}, bf16[384,768]{1,0:T(8,128)(2,1)S(1)}, u32[]{:S(2)}, u32[]{:S(2)}) collective-permute-start(bf16[384,768]{1,0:T(8,128)(2,1)S(1)} %get-tuple-element.83), channel_id=1, source_target_pairs={{0,6},{2,4},{4,2},{6,0},{1,7},{3,5},{5,3},{7,1},{8,14},{10,12},{12... | collective-permute-start | bytes 1769480 | tf_op jit(solution)/shard_map/ppermute | solution.py:180
  213.6 8.5 %collective-permute-done.39.refs_1_ = bf16[384,768]{1,0:T(8,128)(2,1)S(1)} collective-permute-done((bf16[384,768]{1,0:T(8,128)(2,1)S(1)}, bf16[384,768]{1,0:T(8,128)(2,1)S(1)}, u32[]{:S(2)}, u32[]{:S(2)}) %collective-permute-start.39) | collective-permute-done | bytes 589856 | tf_op jit(solution)/shard_map/ppermute | solution.py:180
  222.1 6.8 %collective-permute-start.16 = (bf16[384,1024]{1,0:T(8,128)(2,1)S(1)}, bf16[384,1024]{1,0:T(8,128)(2,1)S(1)}, u32[]{:S(2)}, u32[]{:S(2)}) collective-permute-start(bf16[384,1024]{1,0:T(8,128)(2,1)S(1)} %get-tuple-element.91), channel_id=1, source_target_pairs={{0,6},{2,4},{4,2},{6,0},{1,7},{3,5},{5,3},{7,1},{8,14},{10,12},{12... | collective-permute-start | bytes 2359304 | tf_op jit(solution)/shard_map/ppermute | solution.py:180
  229.0 46.4 %collective-permute-start.17 = (bf16[384,1024]{1,0:T(8,128)(2,1)S(1)}, bf16[384,1024]{1,0:T(8,128)(2,1)S(1)}, u32[]{:S(2)}, u32[]{:S(2)}) collective-permute-start(bf16[384,1024]{1,0:T(8,128)(2,1)S(1)} %get-tuple-element.92), channel_id=1, source_target_pairs={{0,4},{2,0},{4,6},{6,2},{1,5},{3,1},{5,7},{7,3},{8,12},{10,8},{12,... | collective-permute-start | bytes 2359304 | tf_op jit(solution)/shard_map/ppermute | solution.py:180
  275.4 28.4 %collective-permute-start.9 = (bf16[384,768]{1,0:T(8,128)(2,1)S(1)}, bf16[384,768]{1,0:T(8,128)(2,1)S(1)}, u32[]{:S(2)}, u32[]{:S(2)}) collective-permute-start(bf16[384,768]{1,0:T(8,128)(2,1)S(1)} %get-tuple-element.82), channel_id=1, source_target_pairs={{0,2},{2,6},{4,0},{6,4},{1,3},{3,7},{5,1},{7,5},{8,10},{10,14},{12... | collective-permute-start | bytes 1769480 | tf_op jit(solution)/shard_map/ppermute | solution.py:180
  304.7 15.3 %collective-permute-done.15.refs_1_ = bf16[384,1024]{1,0:T(8,128)(2,1)S(1)} collective-permute-done((bf16[384,1024]{1,0:T(8,128)(2,1)S(1)}, bf16[384,1024]{1,0:T(8,128)(2,1)S(1)}, u32[]{:S(2)}, u32[]{:S(2)}) %collective-permute-start.15) | collective-permute-done | bytes 786464 | tf_op jit(solution)/shard_map/ppermute | solution.py:180
  325.6 20.2 %collective-permute-start.4 = (bf16[384,256]{1,0:T(8,128)(2,1)S(1)}, bf16[384,256]{1,0:T(8,128)(2,1)S(1)}, u32[]{:S(2)}, u32[]{:S(2)}) collective-permute-start(bf16[384,256]{1,0:T(8,128)(2,1)S(1)} %get-tuple-element.74), channel_id=1, source_target_pairs={{0,4},{2,0},{4,6},{6,2},{1,5},{3,1},{5,7},{7,3},{8,12},{10,8},{12,... | collective-permute-start | bytes 589832 | tf_op jit(solution)/shard_map/ppermute | solution.py:180
  354.4 3.6 %collective-permute-done.9.refs_1_ = bf16[384,768]{1,0:T(8,128)(2,1)S(1)} collective-permute-done((bf16[384,768]{1,0:T(8,128)(2,1)S(1)}, bf16[384,768]{1,0:T(8,128)(2,1)S(1)}, u32[]{:S(2)}, u32[]{:S(2)}) %collective-permute-start.9) | collective-permute-done | bytes 589856 | tf_op jit(solution)/shard_map/ppermute | solution.py:180
  (109 shorter events, 93.2 us)
Async XLA Ops:
  45.9 29.2 %collective-permute-start.42 = (bf16[384,512]{1,0:T(8,128)(2,1)S(1)}, bf16[384,512]{1,0:T(8,128)(2,1)S(1)}, u32[]{:S(2)}, u32[]{:S(2)}) collective-permute-start(bf16[384,512]{1,0:T(8,128)(2,1)S(1)} %get-tuple-element.118), channel_id=1, source_target_pairs={{0,8},{8,0},{16,24},{24,16},{1,9},{9,1},{17,25},{25,17},{2,10},{10... | collective-permute-start | bytes 1179656 | tf_op jit(solution)/shard_map/ppermute | solution.py:180
  73.3 45.8 %collective-permute-start.37 = (bf16[384,768]{1,0:T(8,128)(2,1)S(1)}, bf16[384,768]{1,0:T(8,128)(2,1)S(1)}, u32[]{:S(2)}, u32[]{:S(2)}) collective-permute-start(bf16[384,768]{1,0:T(8,128)(2,1)S(1)} %get-tuple-element.111), channel_id=1, source_target_pairs={{0,16},{8,24},{16,0},{24,8},{1,17},{9,25},{17,1},{25,9},{2,18},{10... | collective-permute-start | bytes 1769480 | tf_op jit(solution)/shard_map/ppermute | solution.py:180
  75.2 45.7 %collective-permute-start.38 = (bf16[384,768]{1,0:T(8,128)(2,1)S(1)}, bf16[384,768]{1,0:T(8,128)(2,1)S(1)}, u32[]{:S(2)}, u32[]{:S(2)}) collective-permute-start(bf16[384,768]{1,0:T(8,128)(2,1)S(1)} %get-tuple-element.112), channel_id=1, source_target_pairs={{0,24},{8,16},{16,8},{24,0},{1,25},{9,17},{17,9},{25,1},{2,26},{10... | collective-permute-start | bytes 1769480 | tf_op jit(solution)/shard_map/ppermute | solution.py:180
  87.1 62.4 %collective-permute-start.6 = (bf16[384,768]{1,0:T(8,128)(2,1)S(1)}, bf16[384,768]{1,0:T(8,128)(2,1)S(1)}, u32[]{:S(2)}, u32[]{:S(2)}) collective-permute-start(bf16[384,768]{1,0:T(8,128)(2,1)S(1)} %get-tuple-element.78), channel_id=1, source_target_pairs={{0,8},{8,0},{16,24},{24,16},{1,9},{9,1},{17,25},{25,17},{2,10},{10... | collective-permute-start | bytes 1769480 | tf_op jit(solution)/shard_map/ppermute | solution.py:180
  95.8 27.8 %collective-permute-start.19 = (bf16[384,384]{1,0:T(8,128)(2,1)S(1)}, bf16[384,384]{1,0:T(8,128)(2,1)S(1)}, u32[]{:S(2)}, u32[]{:S(2)}) collective-permute-start(bf16[384,384]{1,0:T(8,128)(2,1)S(1)} %collective-permute-done.18), channel_id=1, source_target_pairs={{0,8},{8,0},{16,24},{24,16},{1,9},{9,1},{17,25},{25,17},{2,10},{10... | collective-permute-start | bytes 884744 | tf_op jit(solution)/shard_map/ppermute | solution.py:180
  97.4 52.8 %collective-permute-start.7 = (bf16[384,768]{1,0:T(8,128)(2,1)S(1)}, bf16[384,768]{1,0:T(8,128)(2,1)S(1)}, u32[]{:S(2)}, u32[]{:S(2)}) collective-permute-start(bf16[384,768]{1,0:T(8,128)(2,1)S(1)} %get-tuple-element.79), channel_id=1, source_target_pairs={{0,16},{8,24},{16,0},{24,8},{1,17},{9,25},{17,1},{25,9},{2,18},{10... | collective-permute-start | bytes 1769480 | tf_op jit(solution)/shard_map/ppermute | solution.py:180
  120.9 27.4 %collective-permute-start.23 = (bf16[384,384]{1,0:T(8,128)(2,1)S(1)}, bf16[384,384]{1,0:T(8,128)(2,1)S(1)}, u32[]{:S(2)}, u32[]{:S(2)}) collective-permute-start(bf16[384,384]{1,0:T(8,128)(2,1)S(1)} %collective-permute-done.22), channel_id=1, source_target_pairs={{0,24},{8,16},{16,8},{24,0},{1,25},{9,17},{17,9},{25,1},{2,26},{10... | collective-permute-start | bytes 884744 | tf_op jit(solution)/shard_map/ppermute | solution.py:180
  123.6 28.2 %collective-permute-start.8 = (bf16[384,768]{1,0:T(8,128)(2,1)S(1)}, bf16[384,768]{1,0:T(8,128)(2,1)S(1)}, u32[]{:S(2)}, u32[]{:S(2)}) collective-permute-start(bf16[384,768]{1,0:T(8,128)(2,1)S(1)} %get-tuple-element.80), channel_id=1, source_target_pairs={{0,24},{8,16},{16,8},{24,0},{1,25},{9,17},{17,9},{25,1},{2,26},{10... | collective-permute-start | bytes 1769480 | tf_op jit(solution)/shard_map/ppermute | solution.py:180
  139.0 33.0 %collective-permute-start.45 = (bf16[384,512]{1,0:T(8,128)(2,1)S(1)}, bf16[384,512]{1,0:T(8,128)(2,1)S(1)}, u32[]{:S(2)}, u32[]{:S(2)}) collective-permute-start(bf16[384,512]{1,0:T(8,128)(2,1)S(1)} %get-tuple-element.122), channel_id=1, source_target_pairs={{0,2},{2,6},{4,0},{6,4},{1,3},{3,7},{5,1},{7,5},{8,10},{10,14},{12... | collective-permute-start | bytes 1179656 | tf_op jit(solution)/shard_map/ppermute | solution.py:180
  148.3 50.4 %collective-permute-start.12 = (bf16[384,1024]{1,0:T(8,128)(2,1)S(1)}, bf16[384,1024]{1,0:T(8,128)(2,1)S(1)}, u32[]{:S(2)}, u32[]{:S(2)}) collective-permute-start(bf16[384,1024]{1,0:T(8,128)(2,1)S(1)} %get-tuple-element.86), channel_id=1, source_target_pairs={{0,8},{8,0},{16,24},{24,16},{1,9},{9,1},{17,25},{25,17},{2,10},{10... | collective-permute-start | bytes 2359304 | tf_op jit(solution)/shard_map/ppermute | solution.py:180
  149.5 49.2 %collective-permute-start.13 = (bf16[384,1024]{1,0:T(8,128)(2,1)S(1)}, bf16[384,1024]{1,0:T(8,128)(2,1)S(1)}, u32[]{:S(2)}, u32[]{:S(2)}) collective-permute-start(bf16[384,1024]{1,0:T(8,128)(2,1)S(1)} %get-tuple-element.87), channel_id=1, source_target_pairs={{0,16},{8,24},{16,0},{24,8},{1,17},{9,25},{17,1},{25,9},{2,18},{10... | collective-permute-start | bytes 2359304 | tf_op jit(solution)/shard_map/ppermute | solution.py:180
  150.2 48.6 %collective-permute-start.14 = (bf16[384,1024]{1,0:T(8,128)(2,1)S(1)}, bf16[384,1024]{1,0:T(8,128)(2,1)S(1)}, u32[]{:S(2)}, u32[]{:S(2)}) collective-permute-start(bf16[384,1024]{1,0:T(8,128)(2,1)S(1)} %get-tuple-element.88), channel_id=1, source_target_pairs={{0,24},{8,16},{16,8},{24,0},{1,25},{9,17},{17,9},{25,1},{2,26},{10... | collective-permute-start | bytes 2359304 | tf_op jit(solution)/shard_map/ppermute | solution.py:180
  173.0 49.2 %collective-permute-start.39 = (bf16[384,768]{1,0:T(8,128)(2,1)S(1)}, bf16[384,768]{1,0:T(8,128)(2,1)S(1)}, u32[]{:S(2)}, u32[]{:S(2)}) collective-permute-start(bf16[384,768]{1,0:T(8,128)(2,1)S(1)} %get-tuple-element.114), channel_id=1, source_target_pairs={{0,2},{2,6},{4,0},{6,4},{1,3},{3,7},{5,1},{7,5},{8,10},{10,14},{12... | collective-permute-start | bytes 1769480 | tf_op jit(solution)/shard_map/ppermute | solution.py:180
  197.7 31.3 %collective-permute-start.40 = (bf16[384,768]{1,0:T(8,128)(2,1)S(1)}, bf16[384,768]{1,0:T(8,128)(2,1)S(1)}, u32[]{:S(2)}, u32[]{:S(2)}) collective-permute-start(bf16[384,768]{1,0:T(8,128)(2,1)S(1)} %get-tuple-element.115), channel_id=1, source_target_pairs={{0,6},{2,4},{4,2},{6,0},{1,7},{3,5},{5,3},{7,1},{8,14},{10,12},{12... | collective-permute-start | bytes 1769480 | tf_op jit(solution)/shard_map/ppermute | solution.py:180
  205.4 69.9 %collective-permute-start.41 = (bf16[384,768]{1,0:T(8,128)(2,1)S(1)}, bf16[384,768]{1,0:T(8,128)(2,1)S(1)}, u32[]{:S(2)}, u32[]{:S(2)}) collective-permute-start(bf16[384,768]{1,0:T(8,128)(2,1)S(1)} %get-tuple-element.116), channel_id=1, source_target_pairs={{0,4},{2,0},{4,6},{6,2},{1,5},{3,1},{5,7},{7,3},{8,12},{10,8},{12,... | collective-permute-start | bytes 1769480 | tf_op jit(solution)/shard_map/ppermute | solution.py:180
  208.7 66.7 %collective-permute-start.10 = (bf16[384,768]{1,0:T(8,128)(2,1)S(1)}, bf16[384,768]{1,0:T(8,128)(2,1)S(1)}, u32[]{:S(2)}, u32[]{:S(2)}) collective-permute-start(bf16[384,768]{1,0:T(8,128)(2,1)S(1)} %get-tuple-element.83), channel_id=1, source_target_pairs={{0,6},{2,4},{4,2},{6,0},{1,7},{3,5},{5,3},{7,1},{8,14},{10,12},{12... | collective-permute-start | bytes 1769480 | tf_op jit(solution)/shard_map/ppermute | solution.py:180
  213.6 106.5 %collective-permute-start.15 = (bf16[384,1024]{1,0:T(8,128)(2,1)S(1)}, bf16[384,1024]{1,0:T(8,128)(2,1)S(1)}, u32[]{:S(2)}, u32[]{:S(2)}) collective-permute-start(bf16[384,1024]{1,0:T(8,128)(2,1)S(1)} %get-tuple-element.90), channel_id=1, source_target_pairs={{0,2},{2,6},{4,0},{6,4},{1,3},{3,7},{5,1},{7,5},{8,10},{10,14},{12... | collective-permute-start | bytes 2359304 | tf_op jit(solution)/shard_map/ppermute | solution.py:180
  222.1 100.6 %collective-permute-start.16 = (bf16[384,1024]{1,0:T(8,128)(2,1)S(1)}, bf16[384,1024]{1,0:T(8,128)(2,1)S(1)}, u32[]{:S(2)}, u32[]{:S(2)}) collective-permute-start(bf16[384,1024]{1,0:T(8,128)(2,1)S(1)} %get-tuple-element.91), channel_id=1, source_target_pairs={{0,6},{2,4},{4,2},{6,0},{1,7},{3,5},{5,3},{7,1},{8,14},{10,12},{12... | collective-permute-start | bytes 2359304 | tf_op jit(solution)/shard_map/ppermute | solution.py:180
  229.0 96.6 %collective-permute-start.17 = (bf16[384,1024]{1,0:T(8,128)(2,1)S(1)}, bf16[384,1024]{1,0:T(8,128)(2,1)S(1)}, u32[]{:S(2)}, u32[]{:S(2)}) collective-permute-start(bf16[384,1024]{1,0:T(8,128)(2,1)S(1)} %get-tuple-element.92), channel_id=1, source_target_pairs={{0,4},{2,0},{4,6},{6,2},{1,5},{3,1},{5,7},{7,3},{8,12},{10,8},{12,... | collective-permute-start | bytes 2359304 | tf_op jit(solution)/shard_map/ppermute | solution.py:180
  275.3 79.0 %collective-permute-start.11 = (bf16[384,768]{1,0:T(8,128)(2,1)S(1)}, bf16[384,768]{1,0:T(8,128)(2,1)S(1)}, u32[]{:S(2)}, u32[]{:S(2)}) collective-permute-start(bf16[384,768]{1,0:T(8,128)(2,1)S(1)} %get-tuple-element.84), channel_id=1, source_target_pairs={{0,4},{2,0},{4,6},{6,2},{1,5},{3,1},{5,7},{7,3},{8,12},{10,8},{12,... | collective-permute-start | bytes 1769480 | tf_op jit(solution)/shard_map/ppermute | solution.py:180
  275.4 82.6 %collective-permute-start.9 = (bf16[384,768]{1,0:T(8,128)(2,1)S(1)}, bf16[384,768]{1,0:T(8,128)(2,1)S(1)}, u32[]{:S(2)}, u32[]{:S(2)}) collective-permute-start(bf16[384,768]{1,0:T(8,128)(2,1)S(1)} %get-tuple-element.82), channel_id=1, source_target_pairs={{0,2},{2,6},{4,0},{6,4},{1,3},{3,7},{5,1},{7,5},{8,10},{10,14},{12... | collective-permute-start | bytes 1769480 | tf_op jit(solution)/shard_map/ppermute | solution.py:180
  320.0 40.7 %collective-permute-start.5 = (bf16[384,256]{1,0:T(8,128)(2,1)S(1)}, bf16[384,256]{1,0:T(8,128)(2,1)S(1)}, u32[]{:S(2)}, u32[]{:S(2)}) collective-permute-start(bf16[384,256]{1,0:T(8,128)(2,1)S(1)} %get-tuple-element.76), channel_id=1, source_target_pairs={{0,2},{2,6},{4,0},{6,4},{1,3},{3,7},{5,1},{7,5},{8,10},{10,14},{12... | collective-permute-start | bytes 589832 | tf_op jit(solution)/shard_map/ppermute | solution.py:180
  322.8 38.7 %collective-permute-start.3 = (bf16[384,256]{1,0:T(8,128)(2,1)S(1)}, bf16[384,256]{1,0:T(8,128)(2,1)S(1)}, u32[]{:S(2)}, u32[]{:S(2)}) collective-permute-start(bf16[384,256]{1,0:T(8,128)(2,1)S(1)} %get-tuple-element.73), channel_id=1, source_target_pairs={{0,6},{2,4},{4,2},{6,0},{1,7},{3,5},{5,3},{7,1},{8,14},{10,12},{12... | collective-permute-start | bytes 589832 | tf_op jit(solution)/shard_map/ppermute | solution.py:180
  325.6 35.9 %collective-permute-start.4 = (bf16[384,256]{1,0:T(8,128)(2,1)S(1)}, bf16[384,256]{1,0:T(8,128)(2,1)S(1)}, u32[]{:S(2)}, u32[]{:S(2)}) collective-permute-start(bf16[384,256]{1,0:T(8,128)(2,1)S(1)} %get-tuple-element.74), channel_id=1, source_target_pairs={{0,4},{2,0},{4,6},{6,2},{1,5},{3,1},{5,7},{7,3},{8,12},{10,8},{12,... | collective-permute-start | bytes 589832 | tf_op jit(solution)/shard_map/ppermute | solution.py:180
  (30 other events, 465.5 us)
